TPU v7x, 32 devices: a whole 2x2x4 slice. The times are simulated.
32 devices in a mesh: seq: 4 (over y, x), wshard: 8 (over z, core).
Axes of the slice: x: 2, y: 2, z: 4, core: 2. Of those that a mesh axis runs over, the one named last changes fastest.
Arguments:
- layer_input: bfloat16 [8, 1024, 1536], P('wshard', 'seq'), may hold values from -6 to 6
- lengths: int32 [8], P('wshard'), may hold values from 256 to 1024, as said below
- norm_attn: float32 [1536], replicated, may hold values from 0.1 to 1.9
- w_query: bfloat16 [1536, 1536], P('wshard'), may hold values from -0.15625 to 0.15625
- w_key: bfloat16 [1536, 1536], P('wshard'), may hold values from -0.15625 to 0.15625
- w_value: bfloat16 [1536, 1536], P('wshard'), may hold values from -0.15625 to 0.15625
- w_ogate: bfloat16 [1536, 1536], P('wshard'), may hold values from -0.15625 to 0.15625
- w_forget: bfloat16 [1536, 24], P('wshard'), may hold values from -0.15625 to 0.15625
- forget_bias: float32 [24], replicated, may hold values from 3.5 to 8
- w_out: bfloat16 [1536, 1536], P('wshard'), may hold values from -1 to 1
- norm_ffn: float32 [1536], replicated, may hold values from 0.1 to 1.9
- w_gate: bfloat16 [1536, 4096], P('wshard'), may hold values from -0.15625 to 0.15625
- w_up: bfloat16 [1536, 4096], P('wshard'), may hold values from -0.15625 to 0.15625
- w_down: bfloat16 [4096, 1536], P('wshard'), may hold values from -0.09375 to 0.09375
- output_grad: bfloat16 [8, 1024, 1536], P('wshard', 'seq'), may hold values from -6 to 6
Outputs:
- layer_output: bfloat16 [8, 1024, 1536], P('wshard', 'seq')
- grad_input: float32 [8, 1024, 1536], P('wshard', 'seq')
- grad_norm_attn: float32 [1536], replicated
- grad_w_query: float32 [1536, 1536], P('wshard')
- grad_w_key: float32 [1536, 1536], P('wshard')
- grad_w_value: float32 [1536, 1536], P('wshard')
- grad_w_ogate: float32 [1536, 1536], P('wshard')
- grad_w_forget: float32 [1536, 24], P('wshard')
- grad_forget_bias: float32 [24], replicated
- grad_w_out: float32 [1536, 1536], P('wshard')
- grad_norm_ffn: float32 [1536], replicated
- grad_w_gate: float32 [1536, 4096], P('wshard')
- grad_w_up: float32 [1536, 4096], P('wshard')
- grad_w_down: float32 [4096, 1536], P('wshard')
Inputs may be any that keep to these rules, and one draw needn't show every extreme that they name: Each sequence has 1024 slots of which the first lengths[s] are valid; in every draw one sequence is full and one has exactly 256 valid slots.
All inputs are finite; a program needn't handle non-finite values.
Results may differ from a plain program's by a relative error of at most 0.014.
Values may be sent and summed in bfloat16 or wider, within the bound.
A program may use at most 320 MiB of HBM per device.

v0:
```python
import jax
import jax.numpy as jnp
from jax import lax
from jax.experimental import pallas as pl
from jax.experimental.pallas import tpu as pltpu
from jax.sharding import PartitionSpec as P

EPS = 1e-06
NEG_FILL = -1e30
PAIR = 128


def product(left, right):
    return jnp.dot(left, right, preferred_element_type=jnp.float32)


def product_tn(left, right):
    return lax.dot_general(
        left, right, (((0,), (0,)), ((), ())), preferred_element_type=jnp.float32
    )


def product_nt(left, right):
    return lax.dot_general(
        left, right, (((1,), (1,)), ((), ())), preferred_element_type=jnp.float32
    )


def rms_norm(values, gain):
    return values * lax.rsqrt(jnp.mean(values * values, axis=-1, keepdims=True) + EPS) * gain


def gate_product(attended, gate_pre):
    return attended * jax.nn.sigmoid(gate_pre)


def swiglu(gate, upward):
    return jax.nn.silu(gate) * upward


def low_triangle(size):
    rows = lax.broadcasted_iota(jnp.int32, (size, size), 0)
    return rows <= lax.broadcasted_iota(jnp.int32, (size, size), 1)


def exact(left, right):
    return jnp.dot(left, right, precision=lax.Precision.HIGHEST, preferred_element_type=jnp.float32)


class Forward:
    some = 8

    def __init__(self, joined, bias, length, attended, offset, col, logit, row, head_size, scale):
        self.joined, self.bias, self.length = joined, bias, length
        self.attended, self.offset, self.col, self.logit, self.row = attended, offset, col, logit, row
        self.head_size, self.scale = head_size, scale
        self.slots = joined.shape[0]
        self.pairs = (joined.shape[1] // PAIR - 1) // 3
        self.tile = min(256, self.slots)

    @staticmethod
    def results(slots, pairs):
        rows = jax.ShapeDtypeStruct((Forward.some, slots), jnp.float32)
        return [
            jax.ShapeDtypeStruct((slots, pairs * PAIR), jnp.bfloat16),
            rows,
            jax.ShapeDtypeStruct((slots, PAIR), jnp.float32),
            rows,
        ]

    def lanes(self, pair, part=0):
        return pl.ds(pl.multiple_of((part * self.pairs + pair) * PAIR, PAIR), PAIR)

    def start(self):
        slots, tile, some = self.slots, self.tile, self.some
        logits = self.joined[:, 3 * self.pairs * PAIR :].astype(jnp.float32) + self.bias[...]
        logit_rows = logits.T[:some]
        self.logit[...] = logit_rows
        logs = jnp.minimum(logit_rows, 0.0) - jnp.log1p(jnp.exp(-jnp.abs(logit_rows)))
        ones = low_triangle(tile).astype(jnp.float32)
        carry = jnp.zeros((some, 1), jnp.float32)
        for first in range(0, slots, tile):
            sums = exact(logs[:, first : first + tile], ones) + carry
            self.row[:, first : first + tile] = sums
            carry = sums[:, tile - 1 : tile]
        wide = jnp.concatenate([self.row[...], jnp.zeros((PAIR - some, slots), jnp.float32)], axis=0).T
        usable = lax.broadcasted_iota(jnp.int32, (slots, PAIR), 0) < self.length[...]
        self.col[...] = jnp.where(usable, wide, -NEG_FILL)

    def pair(self, pair):
        slots, tile, half = self.slots, self.tile, self.head_size
        key_all = self.joined[:, self.lanes(pair, 1)]
        value_t = self.joined[:, self.lanes(pair, 2)].T
        query_t = (self.joined[:, self.lanes(pair)].astype(jnp.float32) * self.scale).astype(jnp.bfloat16).T
        sub = lax.broadcasted_iota(jnp.int32, (PAIR, tile), 0)
        wide = lax.broadcasted_iota(jnp.int32, (slots, PAIR), 1)
        diag = low_triangle(tile)
        columns = [
            jnp.sum(jnp.where(wide == 2 * pair + a, self.col[...], 0.0), axis=1, keepdims=True) for a in range(2)
        ]
        for number in range(slots // tile):
            first, last = number * tile, (number + 1) * tile
            outs = []
            for a in range(2):
                mine = (sub >= a * half) & (sub < (a + 1) * half)
                at = pl.ds(2 * pair + a, 1)
                query = jnp.where(mine, query_t[:, first:last], jnp.zeros((), query_t.dtype))
                scores = product(key_all[:last], query)
                own_row = self.row[at, first:last]
                scores = scores + (own_row - columns[a][:last])
                tail = jnp.where(diag, scores[first:], NEG_FILL)
                scores = tail if number == 0 else jnp.concatenate([scores[:first], tail], axis=0)
                top = jnp.max(scores, axis=0, keepdims=True)
                weights = jnp.exp(scores - top)
                total = jnp.sum(weights, axis=0, keepdims=True)
                mixed = product(value_t[a * half : (a + 1) * half, :last], weights.astype(jnp.bfloat16))
                outs.append(mixed / total)
                self.offset[at, first:last] = own_row - (top + jnp.log(total))
            self.attended[first:last, self.lanes(pair)] = jnp.concatenate(outs, axis=0).T.astype(jnp.bfloat16)


def attention_fwd(joined, bias, length, head_size, scale):
    slots = joined.shape[0]
    pairs = (joined.shape[1] // PAIR - 1) // 3

    def body(joined_ref, bias_ref, length_ref, attended, offset, col, logit, row):
        work = Forward(joined_ref, bias_ref, length_ref, attended, offset, col, logit, row, head_size, scale)
        work.start()
        offset[...] = jnp.zeros_like(offset)

        def step(pair, carry):
            work.pair(pair)
            return carry

        lax.fori_loop(0, pairs, step, 0)

    vmem = pl.BlockSpec(memory_space=pltpu.VMEM)
    return pl.pallas_call(
        body,
        in_specs=[vmem] * 3,
        out_specs=[vmem] * 4,
        out_shape=Forward.results(slots, pairs),
        scratch_shapes=[pltpu.VMEM((Forward.some, slots), jnp.float32)],
        compiler_params=pltpu.CompilerParams(vmem_limit_bytes=56 << 20),
        cost_estimate=pl.CostEstimate(
            flops=4 * slots * slots * pairs * PAIR, bytes_accessed=8 * slots * pairs * PAIR, transcendentals=0
        ),
        name="attention_fwd",
    )(joined, bias, length)


def backward_scratch(slots):
    return [
        pltpu.VMEM((slots, PAIR), jnp.float32),
        pltpu.VMEM((slots, PAIR), jnp.float32),
        pltpu.VMEM((slots, PAIR), jnp.float32),
        pltpu.VMEM((8, slots), jnp.float32),
    ]


class Backward:
    def __init__(self, joined, d_out, offset, col, logit, grads, dk_acc, dv_acc, dcol, drow, head_size, scale):
        self.joined, self.d_out, self.offset, self.col = joined, d_out, offset, col
        self.logit, self.grads, self.dk_acc, self.dv_acc = logit, grads, dk_acc, dv_acc
        self.dcol, self.drow, self.head_size, self.scale = dcol, drow, head_size, scale
        self.slots = joined.shape[0]
        self.pairs = (joined.shape[1] // PAIR - 1) // 3
        self.tile = min(256, self.slots)

    def start(self):
        self.dcol[...] = jnp.zeros_like(self.dcol)
        self.drow[...] = jnp.zeros_like(self.drow)

    def lanes(self, pair, part=0):
        return pl.ds(pl.multiple_of((part * self.pairs + pair) * PAIR, PAIR), PAIR)

    def pair(self, pair):
        slots, tile, half = self.slots, self.tile, self.head_size
        dk_acc, dv_acc, dcol, drow = self.dk_acc, self.dv_acc, self.dcol, self.drow
        queries = (self.joined[:, self.lanes(pair)].astype(jnp.float32) * self.scale).astype(jnp.bfloat16)
        key_all = self.joined[:, self.lanes(pair, 1)]
        value_all = self.joined[:, self.lanes(pair, 2)]
        d_out = self.d_out[:, self.lanes(pair)]
        query_t, key_t, dout_t = queries.T, key_all.T, d_out.T
        sub = lax.broadcasted_iota(jnp.int32, (PAIR, tile), 0)
        lanes = lax.broadcasted_iota(jnp.int32, (tile, PAIR), 1)
        wide = lax.broadcasted_iota(jnp.int32, (slots, PAIR), 1)
        diag = low_triangle(tile)
        zero = jnp.zeros((), jnp.bfloat16)
        columns = [
            jnp.sum(jnp.where(wide == 2 * pair + a, self.col[...], 0.0), axis=1, keepdims=True) for a in range(2)
        ]
        dk_acc[...] = jnp.zeros_like(dk_acc)
        dv_acc[...] = jnp.zeros_like(dv_acc)
        for number in range(slots // tile):
            first, last = number * tile, (number + 1) * tile
            outs = []
            for a in range(2):
                mine = (sub >= a * half) & (sub < (a + 1) * half)
                own = (lanes >= a * half) & (lanes < (a + 1) * half)
                at = pl.ds(2 * pair + a, 1)
                scores = product(key_all[:last], jnp.where(mine, query_t[:, first:last], zero))
                scores = scores + (self.offset[at, first:last] - columns[a][:last])
                tail = jnp.where(diag, scores[first:], NEG_FILL)
                scores = tail if number == 0 else jnp.concatenate([scores[:first], tail], axis=0)
                probs = jnp.exp(scores)
                d_probs = product(value_all[:last], jnp.where(mine, dout_t[:, first:last], zero))
                dot = jnp.sum(d_probs * probs, axis=0, keepdims=True)
                d_full = probs * (d_probs - dot)
                d_scores = d_full.astype(jnp.bfloat16)
                drow[at, first:last] = jnp.sum(d_full, axis=0, keepdims=True)
                sums = jnp.sum(d_full, axis=1, keepdims=True)
                dcol[:last, :] += jnp.where(wide[:last] == 2 * pair + a, sums, 0.0)
                outs.append(product(key_t[a * half : (a + 1) * half, :last], d_scores) * self.scale)
                dk_acc[:last, :] += product(d_scores, jnp.where(own, queries[first:last, :], zero))
                dv_acc[:last, :] += product(
                    probs.astype(jnp.bfloat16), jnp.where(own, d_out[first:last, :], zero)
                )
            self.grads[first:last, self.lanes(pair)] = jnp.concatenate(outs, axis=0).T.astype(self.grads.dtype)
        self.grads[:, self.lanes(pair, 1)] = dk_acc[...].astype(self.grads.dtype)
        self.grads[:, self.lanes(pair, 2)] = dv_acc[...].astype(self.grads.dtype)

    def end(self, bias_grad):
        slots, tile, some = self.slots, self.tile, 8
        change = self.drow[...] - self.dcol[...].T[:some]
        rows = lax.broadcasted_iota(jnp.int32, (tile, tile), 0)
        ones = (rows >= lax.broadcasted_iota(jnp.int32, (tile, tile), 1)).astype(jnp.float32)
        carry = jnp.zeros((some, 1), jnp.float32)
        pieces = []
        for first in reversed(range(0, slots, tile)):
            sums = exact(change[:, first : first + tile], ones) + carry
            carry = sums[:, :1]
            pieces.insert(0, sums)
        grad = jnp.concatenate(pieces, axis=1) * jax.nn.sigmoid(-self.logit[...])
        heads = lax.broadcasted_iota(jnp.int32, (some, slots), 0)
        grad = jnp.where(heads < 2 * self.pairs, grad, 0.0)
        bias_grad[...] = jnp.broadcast_to(jnp.sum(grad, axis=1, keepdims=True), bias_grad.shape)
        wide = jnp.concatenate([grad, jnp.zeros((PAIR - some, slots), jnp.float32)], axis=0).T
        self.grads[:, 3 * self.pairs * PAIR : (3 * self.pairs + 1) * PAIR] = wide.astype(self.grads.dtype)


def attention_bwd(joined, d_out, offset, col, logit, head_size, scale):
    slots, width = joined.shape
    pairs = (width // PAIR - 1) // 3

    def body(joined_ref, d_out_ref, offset_ref, col_ref, logit_ref, grads, bias_grad, *scratch):
        work = Backward(
            joined_ref, d_out_ref, offset_ref, col_ref, logit_ref, grads, *scratch, head_size, scale
        )
        work.start()

        def step(pair, carry):
            work.pair(pair)
            return carry

        lax.fori_loop(0, pairs, step, 0)
        work.end(bias_grad)

    vmem = pl.BlockSpec(memory_space=pltpu.VMEM)
    return pl.pallas_call(
        body,
        in_specs=[vmem] * 5,
        out_specs=[vmem] * 2,
        out_shape=[
            jax.ShapeDtypeStruct((slots, width), jnp.bfloat16),
            jax.ShapeDtypeStruct((8, PAIR), jnp.float32),
        ],
        scratch_shapes=backward_scratch(slots),
        compiler_params=pltpu.CompilerParams(vmem_limit_bytes=56 << 20),
        cost_estimate=pl.CostEstimate(
            flops=10 * slots * slots * pairs * PAIR, bytes_accessed=14 * slots * pairs * PAIR, transcendentals=0
        ),
        name="attention_bwd",
    )(joined, d_out, offset, col, logit)


MESH = pl.DeviceIdType.MESH
VMEM_LIMIT = 62 << 20


def square(groups):
    return groups == 4


def sides():
    rank = lax.axis_index("seq")
    return rank, rank + 1 - 2 * lax.rem(rank, 2), lax.rem(rank + 2, 4), 3 - rank


def meet(*others):
    barrier = pltpu.get_barrier_semaphore()
    for other in others:
        pl.semaphore_signal(barrier, inc=1, device_id=other, device_id_type=MESH)
    pl.semaphore_wait(barrier, len(others))


def push(source, target, send, recv, device):
    copy = pltpu.make_async_remote_copy(
        src_ref=source,
        dst_ref=target,
        send_sem=send,
        recv_sem=recv,
        device_id=device,
        device_id_type=MESH,
    )
    copy.start()
    return copy


def by_rows(rows, work):
    def step(number, carry):
        work(pl.ds(pl.multiple_of(number * 16, 16), 16))
        return carry

    lax.fori_loop(0, rows // 16, step, 0)


class Streams:
    def __init__(self, sems):
        self.sems, self.made = sems, []

    def start(self, source, target):
        copy = pltpu.make_async_copy(source, target, self.sems.at[len(self.made)])
        self.made.append(copy)
        copy.start()
        return copy

    def end(self):
        for copy in self.made:
            copy.wait()


class SquareGather:
    def __init__(self, own, full, send, recv):
        self.own, self.full, self.send, self.recv = own, full, send, recv
        self.rows = own.shape[0]
        self.half = self.rows // 2

    def place(self, rank, part):
        return self.full.at[pl.ds(pl.multiple_of(rank * self.rows + part * self.half, self.half), self.half)]

    def copy(self, index):
        me, side, down, across = sides()
        mine = [self.own.at[pl.ds(part * self.half, self.half)] for part in (0, 1)]
        source, target, peer = (
            (mine[0], self.place(me, 0), side),
            (mine[1], self.place(me, 1), down),
            (mine[1], self.place(me, 1), side),
            (mine[0], self.place(me, 0), down),
            (self.place(side, 0), self.place(side, 0), down),
            (self.place(down, 1), self.place(down, 1), side),
        )[index]
        return pltpu.make_async_remote_copy(
            src_ref=source,
            dst_ref=target,
            send_sem=self.send.at[index],
            recv_sem=self.recv.at[index],
            device_id={"seq": peer},
            device_id_type=MESH,
        )

    def start(self):
        for index in range(4):
            self.copy(index).start()

    def relay(self):
        for index in (0, 1):
            self.copy(index).wait_recv()
            self.copy(4 + index).start()

    def near(self):
        self.copy(2).wait_recv()
        self.copy(3).wait_recv()

    def far(self):
        self.copy(4).wait_recv()
        self.copy(5).wait_recv()

    def finish(self):
        for index in range(6):
            self.copy(index).wait_send()


def block_product(left, right, transposed, tile, store):
    total = right.shape[0] if transposed else right.shape[1]

    def step(number, carry):
        columns = pl.ds(pl.multiple_of(number * tile, tile), tile)
        if transposed:
            store(columns, product_nt(left[...], right[columns, :]))
        else:
            store(columns, product(left[...], right[:, columns]))
        return carry

    lax.fori_loop(0, total // tile, step, 0)


def transposed_product(left, right, out):
    tall = 512 if out.shape[0] % 512 == 0 else 384
    wide = next(size for size in (512, 384, 640, 128) if out.shape[1] % size == 0)
    across = out.shape[1] // wide

    def step(number, carry):
        rows = pl.ds(pl.multiple_of((number // across) * tall, tall), tall)
        columns = pl.ds(pl.multiple_of(lax.rem(number, across) * wide, wide), wide)
        out[rows, columns] = product_tn(left[:, rows], right[:, columns]).astype(out.dtype)
        return carry

    lax.fori_loop(0, (out.shape[0] // tall) * across, step, 0)


def line():
    shards, place = lax.axis_size("wshard"), lax.axis_index("wshard")
    chips = shards // 2
    chip, core = place // 2, lax.rem(place, 2)
    forth = {"wshard": lax.rem(place + 2, shards)}
    back = {"wshard": lax.rem(place + shards - 2, shards)}
    twin = {"wshard": place + 1 - 2 * core}
    return chips, chip, core, forth, back, twin


class LineGather:
    @staticmethod
    def scratch(chips):
        dma = pltpu.SemaphoreType.DMA
        return [dma((3, chips)), dma((2 * chips,)), dma((1,))]

    def __init__(self, own, full, send, recv, local):
        self.own, self.full, self.local = own, full, local.at[0]
        self.sends = (send.at[0], send.at[1], send.at[2])
        self.recv = recv
        self.rows = own.shape[0]
        self.chips, self.chip, self.core, *self.devices = line()

    def place(self, chip, core):
        return self.full.at[pl.ds(pl.multiple_of((2 * chip + core) * self.rows, self.rows), self.rows)]

    def copy(self, way, chip, source=None):
        target = self.place(chip, self.core)
        return pltpu.make_async_remote_copy(
            src_ref=target if source is None else source,
            dst_ref=target,
            send_sem=self.sends[way].at[chip],
            recv_sem=self.recv.at[2 * chip + self.core],
            device_id=self.devices[way],
            device_id_type=MESH,
        )

    def wait_for(self, chip, core):
        target = self.place(chip, core)
        pltpu.make_async_remote_copy(
            src_ref=target,
            dst_ref=target,
            send_sem=self.sends[2].at[0],
            recv_sem=self.recv.at[2 * chip + core],
            device_id=self.devices[2],
            device_id_type=MESH,
        ).wait_recv()

    def start(self):
        @pl.when(self.chip < self.chips - 1)
        def _():
            self.copy(0, self.chip, self.own).start()

        @pl.when(self.chip > 0)
        def _():
            self.copy(1, self.chip, self.own).start()

        self.copy(2, self.chip, self.own).start()
        self.keep().start()

    def keep(self):
        return pltpu.make_async_copy(self.own, self.place(self.chip, self.core), self.local)

    def step(self, number):
        left, right = self.chip - number, self.chip + number

        @pl.when(left >= 0)
        def _():
            self.wait_for(left, self.core)

            @pl.when(self.chip < self.chips - 1)
            def _():
                self.copy(0, left).start()

            self.copy(2, left).start()

        @pl.when(right < self.chips)
        def _():
            self.wait_for(right, self.core)

            @pl.when(self.chip > 0)
            def _():
                self.copy(1, right).start()

            self.copy(2, right).start()

    def finish(self):
        for chip in range(self.chips):
            self.wait_for(chip, 1 - self.core)
            self.copy(2, chip).wait_send()

            @pl.when((chip <= self.chip) & (self.chip < self.chips - 1))
            def _():
                self.copy(0, chip).wait_send()

            @pl.when((chip >= self.chip) & (self.chip > 0))
            def _():
                self.copy(1, chip).wait_send()

        self.keep().wait()


class PartExchange:
    @staticmethod
    def scratch():
        dma = pltpu.SemaphoreType.DMA
        return [dma((4,)), dma((4,)), dma((1,))]

    def __init__(self, parts, out, send, recv, local):
        self.parts, self.out, self.send, self.recv, self.local = parts, out, send, recv, local
        self.rank = lax.axis_index("seq")
        self.core, self.twin = line()[2], line()[5]
        self.others = [{"seq": lax.rem(self.rank + k, 4)} for k in range(1, 4)]
        self.rows = out.shape[2]

    def part(self, rank):
        return self.parts.at[pl.ds(pl.multiple_of((2 * rank + self.core) * self.rows, self.rows), self.rows)]

    def copy(self, index):
        if index == 3:
            source = target = self.out.at[self.core]
        else:
            source = self.part(lax.rem(self.rank + index + 1, 4))
            target = self.out.at[self.core, self.rank]
        return pltpu.make_async_remote_copy(
            src_ref=source,
            dst_ref=target,
            send_sem=self.send.at[index],
            recv_sem=self.recv.at[index],
            device_id=self.twin if index == 3 else self.others[index],
            device_id_type=MESH,
        )

    def keep(self):
        return pltpu.make_async_copy(self.part(self.rank), self.out.at[self.core, self.rank], self.local.at[0])

    def start(self):
        for index in (1, 0, 2):
            self.copy(index).start()
        self.keep().start()

    def relay(self):
        for index in range(3):
            self.copy(index).wait()
        self.keep().wait()
        self.copy(3).start()

    def end(self):
        self.copy(3).wait()


class Regroup:
    @staticmethod
    def scratch(rows, width):
        dma = pltpu.SemaphoreType.DMA
        return [pltpu.VMEM((4, rows, width), jnp.bfloat16), dma((7,)), dma((7,))]

    def __init__(self, piece, out, fours, send, recv):
        self.piece, self.out, self.fours, self.send, self.recv = piece, out, fours, send, recv
        self.rank, self.place = lax.axis_index("seq"), lax.axis_index("wshard")
        self.number = lax.rem(self.place, 4)
        self.others = [{"seq": lax.rem(self.rank + k, 4)} for k in range(1, 4)]
        self.along = [{"wshard": lax.rem(self.place + k, 8)} for k in range(1, 8)]

    def near(self, index):
        return pltpu.make_async_remote_copy(
            src_ref=self.piece,
            dst_ref=self.fours.at[self.rank],
            send_sem=self.send.at[index],
            recv_sem=self.recv.at[index],
            device_id=self.others[index],
            device_id_type=MESH,
        )

    def owner(self, rank):
        return 2 * rank + self.place // 4

    def far(self, rank, number):
        return pltpu.make_async_remote_copy(
            src_ref=self.fours.at[rank],
            dst_ref=self.out.at[number],
            send_sem=self.send.at[3 + rank],
            recv_sem=self.recv.at[3 + number],
            device_id={"wshard": self.owner(rank)},
            device_id_type=MESH,
        )

    def start(self):
        for index in range(3):
            self.near(index).start()
        self.fours[self.rank] = self.piece[...]

    def relay(self):
        for index in range(3):
            self.near(index).wait()
        for rank in range(4):

            @pl.when(self.owner(rank) != self.place)
            def _():
                self.far(rank, self.number).start()

            @pl.when(self.owner(rank) == self.place)
            def _():
                self.out[self.number] = self.fours[rank]

    def end(self):
        for rank in range(4):

            @pl.when(self.owner(rank) != self.place)
            def _():
                self.far(rank, self.number).wait_send()

        for number in range(4):

            @pl.when(4 * lax.rem(self.place, 2) + number != self.place)
            def _():
                self.far(0, number).wait_recv()


class Everywhere:
    def __init__(self, values, out, ranks, total, places, send, recv):
        self.values, self.out, self.ranks, self.total, self.places = values, out, ranks, total, places
        self.send, self.recv = send, recv
        self.groups, self.shards = ranks.shape[0], places.shape[0]
        self.rank, self.place = lax.axis_index("seq"), lax.axis_index("wshard")

    def others(self):
        return [{"seq": lax.rem(self.rank + k, self.groups)} for k in range(1, self.groups)]

    def along(self):
        return [{"wshard": lax.rem(self.place + k, self.shards)} for k in range(1, self.shards)]

    def start(self):
        self.first = [
            push(self.values, self.ranks.at[self.rank], self.send.at[k], self.recv.at[k], other)
            for k, other in enumerate(self.others())
        ]
        self.ranks[self.rank] = self.values[...]

    def relay(self):
        for copy in self.first:
            copy.wait()
        ranks, groups = self.ranks, self.groups
        self.total[...] = (ranks[0] + ranks[1]) + (ranks[2] + ranks[3])
        self.second = [
            push(self.total, self.places.at[self.place], self.send.at[groups + k], self.recv.at[groups + k], other)
            for k, other in enumerate(self.along())
        ]
        self.places[self.place] = self.total[...]

    def end(self):
        for copy in self.second:
            copy.wait()
        sums = [self.places[k] + self.places[k + 1] for k in range(0, self.shards, 2)]
        self.out[...] = (sums[0] + sums[1]) + (sums[2] + sums[3])


def last_gather(values, small, collective_id):
    count = len(values)
    groups = lax.axis_size("seq")
    shards = 2 * groups

    def body(*refs):
        own, small_ref = refs[:count], refs[count]
        full, small_out = refs[count + 1 : 2 * count + 1], refs[2 * count + 1]
        send, recv, local = refs[2 * count + 2 : 2 * count + 5]
        me, side, down, across = sides()
        total = Everywhere(small_ref, small_out, *refs[2 * count + 5 :])
        meet(*total.others(), *total.along())
        jobs = [SquareGather(own[i], full[i], send.at[i], recv.at[i]) for i in range(count)]
        total.start()
        keeps = []
        for i, job in enumerate(jobs):
            job.start()
            rows = own[i].shape[0]
            keep = pltpu.make_async_copy(
                own[i], full[i].at[pl.ds(pl.multiple_of(me * rows, rows), rows)], local.at[i]
            )
            keep.start()
            keeps.append(keep)
        total.relay()
        for job in jobs:
            job.relay()
        total.end()
        for job, keep in zip(jobs, keeps):
            job.near()
            job.far()
            job.finish()
            keep.wait()

    vmem = pl.BlockSpec(memory_space=pltpu.VMEM)
    dma = pltpu.SemaphoreType.DMA
    return pl.pallas_call(
        body,
        in_specs=[vmem] * (count + 1),
        out_specs=[pl.BlockSpec(memory_space=pl.ANY)] * count + [vmem],
        out_shape=[jax.ShapeDtypeStruct((4 * v.shape[0],) + v.shape[1:], v.dtype) for v in values]
        + [jax.ShapeDtypeStruct(small.shape, jnp.float32)],
        scratch_shapes=[
            dma((count, 6)),
            dma((count, 6)),
            dma((count,)),
            pltpu.VMEM((groups,) + small.shape, jnp.float32),
            pltpu.VMEM(small.shape, jnp.float32),
            pltpu.VMEM((shards,) + small.shape, jnp.float32),
            dma((groups + shards,)),
            dma((groups + shards,)),
        ],
        compiler_params=pltpu.CompilerParams(
            collective_id=collective_id, has_side_effects=True, vmem_limit_bytes=VMEM_LIMIT
        ),
        name="last_gather",
    )(*values, small)


def join_units(every_gate, every_up, down, out, part):
    groups, rows, units = every_gate.shape
    steps = 4
    tall = rows // steps

    def body(gate_in, up_in, down_in, out_in, gate_ref, up_ref, down_ref, out_ref):
        for every, to_ref in ((gate_in, gate_ref), (up_in, up_ref)):
            for group in range(groups):
                for block in range(units // part):
                    to = (block * groups + group) * part
                    to_ref[:, to : to + part] = every[group, :, block * part : (block + 1) * part].astype(
                        jnp.float32
                    )
        down_ref[...] = down_in[...].astype(jnp.float32)
        out_ref[...] = out_in[...].astype(jnp.float32)

    def flat(value):
        return pl.BlockSpec((value.shape[0] // steps, value.shape[1]), lambda i: (i, 0))

    wide = jax.ShapeDtypeStruct((rows, groups * units), jnp.float32)
    results = [wide, wide, *(jax.ShapeDtypeStruct(v.shape, jnp.float32) for v in (down, out))]
    return pl.pallas_call(
        body,
        grid=(steps,),
        in_specs=[pl.BlockSpec((groups, tall, units), lambda i: (0, i, 0))] * 2 + [flat(down), flat(out)],
        out_specs=[flat(value) for value in results],
        out_shape=results,
        name="join_units",
    )(every_gate, every_up, down, out)


def join_columns(every, gate, columns, starts, forget_at, heads):
    groups, rows, lanes = every.shape
    own = heads // groups
    steps = 4
    tall = rows // steps

    def body(every_ref, gate_ref, *outs):
        for group in range(groups):
            to = slice(group * columns, (group + 1) * columns)
            for start, out in zip(starts, outs):
                out[:, to] = every_ref[group, :, start : start + columns].astype(jnp.float32)
            outs[-2][:, to] = gate_ref[group].astype(jnp.float32)
            outs[-1][:, group * own : (group + 1) * own] = every_ref[
                group, :, forget_at : forget_at + own
            ].astype(jnp.float32)

    def flat(value):
        return pl.BlockSpec((tall, value.shape[1]), lambda i: (i, 0))

    wide = jax.ShapeDtypeStruct((rows, groups * columns), jnp.float32)
    results = [wide] * (len(starts) + 1) + [jax.ShapeDtypeStruct((rows, heads), jnp.float32)]
    return pl.pallas_call(
        body,
        grid=(steps,),
        in_specs=[pl.BlockSpec((groups, tall, v.shape[2]), lambda i: (0, i, 0)) for v in (every, gate)],
        out_specs=[flat(value) for value in results],
        out_shape=results,
        name="join_columns",
    )(every, gate)


class SquareScatter:
    @staticmethod
    def scratch(rows, width):
        half = rows // 2
        low = jnp.bfloat16
        return [
            pltpu.VMEM((rows, width), low),
            pltpu.VMEM((2, half, width), low),
            pltpu.VMEM((2, half, width), jnp.float32),
            pltpu.VMEM((6, half, width), low),
            pltpu.VMEM((2, half, width), low),
            pltpu.SemaphoreType.DMA((6,)),
            pltpu.SemaphoreType.DMA((6,)),
        ]

    def __init__(self, lefts, rights, transposed, out, far, near, kept, land, carry, send, recv):
        self.lefts, self.rights, self.transposed, self.out = lefts, rights, transposed, out
        self.far, self.near, self.kept, self.land, self.carry = far, near, kept, land, carry
        self.send, self.recv = send, recv
        self.rows, self.width = out.shape
        self.half = self.rows // 2
        self.tile = self.width // 3 if self.width % 384 == 0 else self.width

    def copy(self, index):
        me, side, down, across = sides()
        source = (
            self.far.at[pl.ds(0, self.half)],
            self.far.at[pl.ds(self.half, self.half)],
            self.near.at[0],
            self.near.at[1],
            self.carry.at[0],
            self.carry.at[1],
        )[index]
        return pltpu.make_async_remote_copy(
            src_ref=source,
            dst_ref=self.land.at[index],
            send_sem=self.send.at[index],
            recv_sem=self.recv.at[index],
            device_id={"seq": down if index in (0, 3, 5) else side},
            device_id_type=MESH,
        )

    def partial(self, rank, store):
        at = pl.ds(pl.multiple_of(rank * self.rows, self.rows), self.rows)

        def step(number, carried):
            columns = pl.ds(pl.multiple_of(number * self.tile, self.tile), self.tile)
            value = None
            for a, b in zip(self.lefts, self.rights):
                if self.transposed:
                    term = product_nt(a[at, :], b[columns, :])
                else:
                    term = product(a[at, :], b[:, columns])
                value = term if value is None else value + term
            store(columns, value)
            return carried

        lax.fori_loop(0, self.width // self.tile, step, 0)

    def begin(self):
        me, side, down, across = sides()
        half, far, near, kept = self.half, self.far, self.near, self.kept

        def store_far(columns, value):
            far[:, columns] = value.astype(far.dtype)

        def store_side(columns, value):
            kept[0, :, columns] = value[:half]
            near[0, :, columns] = value[half:].astype(near.dtype)

        def store_down(columns, value):
            near[1, :, columns] = value[:half].astype(near.dtype)
            kept[1, :, columns] = value[half:]

        self.partial(across, store_far)
        self.copy(0).start()
        self.copy(1).start()
        self.partial(side, store_side)
        self.copy(2).start()
        self.partial(down, store_down)
        self.copy(3).start()

    def relay(self):
        for index in (0, 1):
            self.copy(index).wait_recv()

            def add(at, index=index):
                total = self.kept[index, at, :] + self.land[index, at, :].astype(jnp.float32)
                self.carry[index, at, :] = total.astype(self.carry.dtype)

            by_rows(self.half, add)
            self.copy(4 + index).start()

    def own(self):
        out = self.out

        def store_own(columns, value):
            out[:, columns] = value

        self.partial(lax.axis_index("seq"), store_own)

    def end(self):
        for index in (2, 3, 4, 5):
            self.copy(index).wait_recv()
        land, half, out = self.land, self.half, self.out

        def add(at):
            out[at, :] += land[3, at, :].astype(jnp.float32) + land[4, at, :].astype(jnp.float32)

        def add_second(at):
            to = pl.ds(at.start + half, at.size)
            out[to, :] += land[2, at, :].astype(jnp.float32) + land[5, at, :].astype(jnp.float32)

        by_rows(half, add)
        by_rows(half, add_second)
        for index in range(6):
            self.copy(index).wait_send()


class LineScatter:
    @staticmethod
    def scratch(chips, rows, width):
        low = jnp.bfloat16
        dma = pltpu.SemaphoreType.DMA
        return [pltpu.VMEM((chips, rows, width), low)] * 3 + [dma((2, chips)), dma((3, chips))]

    def __init__(self, terms, out, twin_in, forth_in, back_in, send, recv):
        self.terms, self.out, self.twin_in = terms, out, twin_in
        self.forth_in, self.back_in, self.send, self.recv = forth_in, back_in, send, recv
        self.chips, self.chip, self.core, *self.devices = line()
        self.rows = twin_in.shape[1]

    def term(self, chip, core):
        return self.terms.at[pl.ds(pl.multiple_of((2 * chip + core) * self.rows, self.rows), self.rows)]

    def swap(self, chip):
        return pltpu.make_async_remote_copy(
            src_ref=self.term(chip, 1 - self.core),
            dst_ref=self.twin_in.at[chip],
            send_sem=self.send.at[0, chip],
            recv_sem=self.recv.at[0, chip],
            device_id=self.devices[2],
            device_id_type=MESH,
        )

    def hop(self, way, chip):
        return pltpu.make_async_remote_copy(
            src_ref=self.twin_in.at[chip],
            dst_ref=(self.forth_in, self.back_in)[way].at[chip],
            send_sem=self.send.at[1, chip],
            recv_sem=self.recv.at[1 + way, chip],
            device_id=self.devices[way],
            device_id_type=MESH,
        )

    def start(self):
        for chip in (self.chips - 1, 0, *range(1, self.chips - 1)):
            self.swap(chip).start()

    def add(self, chip, ways, out):
        def step(at):
            start = pl.multiple_of((2 * chip + self.core) * self.rows + at.start, at.size)
            total = self.terms[pl.ds(start, at.size), :].astype(jnp.float32)
            total = total + self.twin_in[chip, at, :].astype(jnp.float32)
            for way in ways:
                total = total + (self.forth_in, self.back_in)[way][chip, at, :].astype(jnp.float32)
            out[at, :] = total.astype(out.dtype)

        by_rows(self.rows, step)

    def pass_on(self, way, chip, first):
        self.swap(chip).wait_recv()
        if not first:
            self.hop(way, chip).wait_recv()
        self.add(chip, () if first else (way,), self.twin_in.at[chip])
        self.hop(way, chip).start()

    def slot(self, number):
        last = self.chips - 1
        for chip in range(self.chips):
            forth, back = number - (last - chip), last - (number - chip)
            if 0 <= forth < chip:

                @pl.when(self.chip == forth)
                def _():
                    self.pass_on(0, chip, forth == 0)

            if chip < back <= last:

                @pl.when(self.chip == back)
                def _():
                    self.pass_on(1, chip, back == last)

    def end(self):
        for chip in range(self.chips):

            @pl.when(self.chip == chip)
            def _():
                self.swap(chip).wait_recv()
                ways = [way for way, there in enumerate((chip > 0, chip < self.chips - 1)) if there]
                for way in ways:
                    self.hop(way, chip).wait_recv()
                self.add(chip, ways, self.out)

            self.swap(chip).wait_send()

            @pl.when(self.chip != chip)
            def _():
                self.hop(0, chip).wait_send()


def middle_backward(joined, d_out, offset, col, logit, hidden, w_down, gated, grad_branch, terms_up, share_down,
                    normed, d_pre, head_size, scale, collective_id):
    slots, lanes = joined.shape
    width = w_down.shape[1]
    tokens = slots // 4
    columns = gated.shape[1]
    shards = 2 * lax.axis_size("seq")
    chips = shards // 2
    rows_up = terms_up.shape[0] // shards

    def body(joined_ref, d_out_ref, offset_ref, col_ref, logit_ref, hidden_ref, down_ref, gated_ref, branch_ref,
             up_ref, share_ref, normed_ref, pre_ref,
             grads, bias_grad, lowered, collected, share_up, share_pre, every_down, terms, terms_pre, send, recv, keep, *scratch):
        me, side, down, across = sides()
        line_chips, chip, core, forth, back, twin = line()
        meet({"seq": side}, {"seq": down}, forth, back, twin)
        work = Backward(
            joined_ref, d_out_ref, offset_ref, col_ref, logit_ref, grads, *scratch[:4], head_size, scale
        )
        job = SquareScatter([hidden_ref], [down_ref], False, lowered, *scratch[4:11])
        collect = LineScatter(terms, collected, *scratch[11:16])
        run = LineScatter(up_ref, share_up, *scratch[16:21])
        run_pre = LineScatter(terms_pre, share_pre, *scratch[21:])
        every = SquareGather(share_ref, every_down, send, recv)
        size = share_ref.shape[0]
        kept = pltpu.make_async_copy(
            share_ref, every_down.at[pl.ds(pl.multiple_of(me * size, size), size)], keep.at[0]
        )
        kept.start()
        run.start()
        transposed_product(gated_ref, branch_ref, terms)
        collect.start()
        transposed_product(normed_ref, pre_ref, terms_pre)
        run_pre.start()
        collect.slot(0)
        run.slot(0)
        job.begin()
        run_pre.slot(0)
        work.start()

        def step(pair, carry):
            work.pair(pair)

            @pl.when(pair == 0)
            def _():
                job.relay()
                collect.slot(1)
                run.slot(1)
                run_pre.slot(1)
                every.start()

            @pl.when(pair == 1)
            def _():
                collect.slot(2)
                run.slot(2)
                run_pre.slot(2)

            return carry

        lax.fori_loop(0, work.pairs, step, 0)
        every.relay()
        job.own()
        work.end(bias_grad)
        job.end()
        run.end()
        run_pre.end()
        every.near()
        every.far()
        every.finish()
        kept.wait()
        collect.end()

    vmem = pl.BlockSpec(memory_space=pltpu.VMEM)
    low = jnp.bfloat16
    dma = pltpu.SemaphoreType.DMA
    return pl.pallas_call(
        body,
        in_specs=[vmem] * 13,
        out_specs=[vmem] * 6 + [pl.BlockSpec(memory_space=pl.ANY)],
        out_shape=[
            jax.ShapeDtypeStruct((slots, lanes), low),
            jax.ShapeDtypeStruct((8, PAIR), jnp.float32),
            jax.ShapeDtypeStruct((tokens, width), jnp.float32),
            jax.ShapeDtypeStruct((columns // shards, width), low),
            jax.ShapeDtypeStruct((rows_up, terms_up.shape[1]), low),
            jax.ShapeDtypeStruct((rows_up, columns), low),
            jax.ShapeDtypeStruct((4 * share_down.shape[0], width), low),
        ],
        scratch_shapes=[
            pltpu.VMEM((columns, width), low),
            pltpu.VMEM((width, columns), low),
            dma((6,)),
            dma((6,)),
            dma((1,)),
        ]
        + backward_scratch(slots)
        + SquareScatter.scratch(tokens, width)
        + LineScatter.scratch(chips, columns // shards, width)
        + LineScatter.scratch(chips, rows_up, terms_up.shape[1])
        + LineScatter.scratch(chips, rows_up, columns),
        compiler_params=pltpu.CompilerParams(
            collective_id=collective_id, has_side_effects=True, vmem_limit_bytes=VMEM_LIMIT
        ),
        name="middle_backward",
    )(joined, d_out, offset, col, logit, hidden, w_down, gated, grad_branch, terms_up, share_down, normed, d_pre)


def last_backward(grads, grad_gate_pre, normed, weights, gate_weights, collected, shares, collective_id):
    slots, depth = normed.shape
    front = grads.shape[1]
    count = len(shares)
    tokens = slots // 4
    shards = 2 * lax.axis_size("seq")
    rows = depth // shards

    def body(grads_ref, gate_ref, normed_ref, weights_ref, gate_weights_ref, collected_ref,
             *refs):
        share_refs, refs = refs[:count], refs[count:]
        summed, share, regrouped, *every_refs = refs[: 3 + count]
        terms, send, recv, keep, *scratch = refs[3 + count :]
        me, side, down, across = sides()
        chips, chip, core, forth, back, twin = line()
        regroup = Regroup(collected_ref, regrouped, *scratch[12:])
        meet(*regroup.others, *regroup.along)
        job = SquareScatter(
            [grads_ref, gate_ref],
            [weights_ref, gate_weights_ref],
            True,
            summed,
            *scratch[:7],
        )
        run = LineScatter(terms, share, *scratch[7:12])
        regroup.start()
        every = [
            SquareGather(share_refs[i], every_refs[i], send.at[i], recv.at[i]) for i in range(count)
        ]
        kept = []
        for i in range(count):
            size = share_refs[i].shape[0]
            kept.append(
                pltpu.make_async_copy(
                    share_refs[i],
                    every_refs[i].at[pl.ds(pl.multiple_of(me * size, size), size)],
                    keep.at[i],
                )
            )
            kept[i].start()
            every[i].start()
        transposed_product(normed_ref, grads_ref, terms)
        run.start()
        regroup.relay()
        job.begin()
        run.slot(0)
        for gathering in every:
            gathering.relay()
        job.relay()
        job.own()
        run.slot(1)
        run.slot(2)
        for gathering, copy in zip(every, kept):
            gathering.near()
            gathering.far()
            gathering.finish()
            copy.wait()
        job.end()
        regroup.end()
        run.end()

    vmem = pl.BlockSpec(memory_space=pltpu.VMEM)
    low = jnp.bfloat16
    dma = pltpu.SemaphoreType.DMA
    return pl.pallas_call(
        body,
        in_specs=[vmem] * (6 + count),
        out_specs=[vmem] * 3 + [pl.BlockSpec(memory_space=pl.ANY)] * count,
        out_shape=[
            jax.ShapeDtypeStruct((tokens, depth), jnp.float32),
            jax.ShapeDtypeStruct((rows, front), low),
            jax.ShapeDtypeStruct((4,) + collected.shape, low),
            *(jax.ShapeDtypeStruct((4 * v.shape[0], v.shape[1]), low) for v in shares),
        ],
        scratch_shapes=[
            pltpu.VMEM((depth, front), low),
            dma((count, 6)),
            dma((count, 6)),
            dma((count,)),
        ]
        + SquareScatter.scratch(tokens, depth)
        + LineScatter.scratch(shards // 2, rows, front)
        + Regroup.scratch(*collected.shape),
        compiler_params=pltpu.CompilerParams(
            collective_id=collective_id, has_side_effects=True, vmem_limit_bytes=VMEM_LIMIT
        ),
        name="last_backward",
    )(grads, grad_gate_pre, normed, weights, gate_weights, collected, *shares)


def norm_rows(values, gain):
    scale = lax.rsqrt(jnp.mean(values * values, axis=-1, keepdims=True) + EPS)
    return scale, values * scale * gain


def whole_forward(inputs, gain, cotangent, weights, forget, bias, length, block, w_gate, w_up,
                  head_size, scale, collective_id):
    rows, depth = inputs.shape
    groups = 4
    slots = groups * rows
    chips = groups
    shards = 2 * chips
    mine = weights[0].shape[0]
    columns = depth // groups
    front = 3 * columns + PAIR
    pairs = columns // PAIR
    part = w_gate.shape[1] // (groups * shards)
    units = shards * part
    early = units + units // 2
    low = jnp.bfloat16

    def body(inputs_ref, gain_ref, cot_ref, q_ref, k_ref, v_ref, og_ref, forget_ref, bias_ref, length_ref, block_ref,
             gate_ref, up_ref,
             normed_hbm, cot_full, full_front_hbm, full_gate_hbm, full_out_hbm, full_ffn, joined_hbm, attended_hbm,
             offset, col, logit, gate_pre_hbm, gated_hbm, middle, own_up,
             own_normed, own_front, own_gate, own_ffn, own_out, parts_out, row, picks, cot_send, cot_recv, keep,
             x_send, x_recv, normed, full_front, full_gate, full_out, joined, attended, gate_pre, gated, store_sems,
             *scratch):
        store = Streams(store_sems)
        me, side, down, across = sides()
        line_chips, chip, core, forth, back, twin = line()
        front_line = LineGather(own_front, full_front, *scratch[0:3])
        gate_line = LineGather(own_gate, full_gate, *scratch[3:6])
        ffn_line = LineGather(own_ffn, full_ffn, *scratch[6:9])
        out_line = LineGather(own_out, parts_out, *scratch[9:12])
        exchange = PartExchange(parts_out, full_out, *scratch[12:15])
        job = SquareScatter([gated], [full_out_rows(full_out)], False, middle, *scratch[15:22])
        taken = []
        my_columns = pl.ds(pl.multiple_of(me * columns, columns), columns)
        for index, source in enumerate((q_ref, k_ref, v_ref)):
            taken.append((source.at[:, my_columns], own_front.at[:, pl.ds(index * columns, columns)]))
        taken.append((og_ref.at[:, my_columns], own_gate))
        tall = own_out.shape[0]
        taken.append((block_ref.at[pl.ds(pl.multiple_of(me * tall, tall), tall)], own_out))
        for index, source in enumerate((gate_ref, up_ref)):
            for number in range(shards):
                column = pl.ds(pl.multiple_of((number * groups + me) * part, part), part)
                to = index * units + number * part
                target = own_ffn.at[:, pl.ds(to, part)] if to < early else own_up.at[:, pl.ds(to - early, part)]
                taken.append((source.at[:, column], target))
        taken = [pltpu.make_async_copy(a, b, picks.at[i]) for i, (a, b) in enumerate(taken)]
        for copy in taken:
            copy.start()
        values = inputs_ref[...].astype(jnp.float32)
        own_normed[...] = norm_rows(values, gain_ref[...])[1].astype(low)
        own_front[:, 3 * columns :] = forget_ref[...]
        meet(*exchange.others, forth, back, twin)
        one = SquareGather(own_normed, normed, x_send, x_recv)
        two = SquareGather(cot_ref, cot_full, cot_send, cot_recv)
        one.start()
        for copy in taken:
            copy.wait()
        front_line.start()
        at_me = pl.ds(pl.multiple_of(me * rows, rows), rows)
        kept = pltpu.make_async_copy(cot_ref, cot_full.at[at_me], keep.at[0])
        kept.start()
        normed[at_me, :] = own_normed[...]
        one.relay()
        two.start()
        front_line.step(1)
        front_line.step(2)
        one.near()
        one.far()
        front_line.step(3)
        store.start(normed, normed_hbm)
        front_line.finish()
        store.start(full_front, full_front_hbm)
        one.finish()
        out_line.start()
        gate_line.start()
        two.relay()

        def store_joined(at_columns, value):
            joined[:, at_columns] = value.astype(low)

        block_product(normed, full_front, False, 256, store_joined)
        store.start(joined, joined_hbm)
        work = Forward(joined, bias_ref, length_ref, attended, offset, col, logit, row, head_size, scale)
        offset[...] = jnp.zeros_like(offset)
        out_line.step(1)
        gate_line.step(1)
        work.start()
        out_line.step(2)
        gate_line.step(2)

        def step(pair, carry):
            work.pair(pair)

            @pl.when(pair == 0)
            def _():
                out_line.step(3)
                gate_line.step(3)
                out_line.finish()
                exchange.start()
                ffn_line.start()

            return carry

        lax.fori_loop(0, pairs, step, 0)
        store.start(attended, attended_hbm)
        gate_line.finish()
        store.start(full_gate, full_gate_hbm)
        exchange.relay()

        def store_gate(at_columns, value):
            gate_pre[:, at_columns] = value

        block_product(normed, full_gate, False, PAIR, store_gate)
        gated[...] = (attended[...].astype(jnp.float32) * jax.nn.sigmoid(gate_pre[...])).astype(low)
        store.start(gate_pre, gate_pre_hbm)
        store.start(gated, gated_hbm)
        exchange.end()
        store.start(full_out, full_out_hbm)
        job.begin()
        job.relay()
        ffn_line.step(1)
        job.own()
        two.near()
        two.far()
        two.finish()
        kept.wait()
        ffn_line.step(2)
        job.end()
        middle[...] += inputs_ref[...].astype(jnp.float32)
        ffn_line.step(3)
        ffn_line.finish()
        store.end()

    def shape(size, kind=low):
        return jax.ShapeDtypeStruct(size, kind)

    vmem = pl.BlockSpec(memory_space=pltpu.VMEM)
    anywhere = pl.BlockSpec(memory_space=pl.ANY)
    dma = pltpu.SemaphoreType.DMA
    results = [
        shape((slots, depth)),
        shape((slots, depth)),
        shape((depth, front)),
        shape((depth, columns)),
        shape((2, 4, block.shape[0] // 4, depth)),
        shape((depth, early)),
        shape((slots, front)),
        *Forward.results(slots, pairs),
        shape((slots, columns), jnp.float32),
        shape((slots, columns)),
        shape((rows, depth), jnp.float32),
        shape((mine, 2 * units - early)),
    ]
    kept_here = [results[i] for i in (0, 2, 3, 4, 6, 7, 11, 12)]
    return pl.pallas_call(
        body,
        in_specs=[vmem] * 3 + [anywhere] * 4 + [vmem] * 3 + [anywhere] * 3,
        out_specs=[anywhere] * 8 + [vmem] * 3 + [anywhere] * 2 + [vmem] * 2,
        out_shape=results,
        scratch_shapes=[
            pltpu.VMEM((rows, depth), low),
            pltpu.VMEM((mine, front), low),
            pltpu.VMEM((mine, columns), low),
            pltpu.VMEM((mine, early), low),
            pltpu.VMEM((block.shape[0] // 4, depth), low),
            pltpu.VMEM((shards * block.shape[0] // 4, depth), low),
            pltpu.VMEM((Forward.some, slots), jnp.float32),
            dma((5 + 2 * shards,)),
            dma((6,)),
            dma((6,)),
            dma((1,)),
            dma((6,)),
            dma((6,)),
            *(pltpu.VMEM(value.shape, value.dtype) for value in kept_here),
            dma((len(kept_here),)),
        ]
        + 4 * LineGather.scratch(chips)
        + PartExchange.scratch()
        + SquareScatter.scratch(rows, depth),
        compiler_params=pltpu.CompilerParams(
            collective_id=collective_id, has_side_effects=True, vmem_limit_bytes=VMEM_LIMIT
        ),
        name="whole_forward",
    )(inputs, gain, cotangent, *weights, forget, bias, length, block, w_gate, w_up)


class full_out_rows:
    def __init__(self, ref):
        self.ref = ref
        self.shape = (ref.shape[0] * ref.shape[1] * ref.shape[2], ref.shape[3])

    def __getitem__(self, index):
        taken = self.ref[:, :, :, index[1]]
        return taken.reshape(self.shape[0], taken.shape[3])


def feed_forward(middle, gain, weights, own_up, own_down, cotangent, collective_id):
    rows, depth = middle.shape
    slots = 4 * rows
    units = 4 * own_down.shape[0] * 2
    early = weights.shape[1]
    chips = 4
    low = jnp.bfloat16

    def body(middle_ref, gain_ref, weights_hbm, up_ref, down_ref, cot_hbm,
             normed_hbm, hidden_hbm, full_up_hbm, full_down_hbm, grads_hbm, terms_hbm,
             own_normed, both, send, recv,
             weights_ref, cot_ref, normed, hidden, full_up, full_down, grads, terms, fetch_sems, store_sems, *scratch):
        fetch, store = Streams(fetch_sems), Streams(store_sems)
        weights_in = fetch.start(weights_hbm, weights_ref)
        cot_in = fetch.start(cot_hbm, cot_ref)
        me, side, down, across = sides()
        line_chips, chip, core, forth, back, twin = line()
        up_line = LineGather(up_ref, full_up, *scratch[:3])
        down_line = LineGather(down_ref, full_down, *scratch[3:])
        own_normed[...] = norm_rows(middle_ref[...], gain_ref[...])[1].astype(low)
        meet({"seq": side}, {"seq": down}, forth, back, twin)
        job = SquareGather(own_normed, normed, send, recv)
        job.start()
        up_line.start()

        def rows_of(rank):
            return pl.ds(pl.multiple_of(rank * rows, rows), rows)

        def multiply(rank):
            at = rows_of(rank)

            def store(columns, value):
                both[at, columns] = value

            block_product(normed.at[at], weights_ref, False, 512, store)

        normed[rows_of(me), :] = own_normed[...]
        weights_in.wait()
        multiply(me)
        up_line.step(1)
        job.relay()
        up_line.step(2)
        down_line.start()
        up_line.step(3)
        job.near()
        multiply(side)
        multiply(down)
        job.far()
        down_line.step(1)
        store.start(normed, normed_hbm)
        multiply(across)
        up_line.finish()
        store.start(full_up, full_up_hbm)

        def ahead(number, carry):
            at = rows_of(number)
            both[at, early:] = product(normed[at, :], full_up[...])
            gate, upward = both[at, :units], both[at, units:]
            hidden[at, :] = (gate * jax.nn.sigmoid(gate) * upward).astype(low)
            return carry

        lax.fori_loop(0, 4, ahead, 0)
        down_line.step(2)
        job.finish()
        store.start(hidden, hidden_hbm)
        cot_in.wait()
        transposed_product(hidden, cot_ref, terms)
        store.start(terms, terms_hbm)
        down_line.step(3)
        down_line.finish()
        store.start(full_down, full_down_hbm)

        def behind(number, carry):
            at = rows_of(number)
            grad_hidden = product_nt(cot_ref[at, :], full_down[...])
            gate, upward = both[at, :units], both[at, units:]
            sigma = jax.nn.sigmoid(gate)
            grads[at, :units] = (grad_hidden * upward * sigma * (1.0 + gate * (1.0 - sigma))).astype(low)
            grads[at, units:] = (grad_hidden * gate * sigma).astype(low)
            part(number).start()
            return carry

        def part(number):
            at = rows_of(number)
            return pltpu.make_async_copy(grads.at[at], grads_hbm.at[at], store_sems.at[5 + number])

        lax.fori_loop(0, 4, behind, 0)
        for number in range(4):
            part(number).wait()
        store.end()

    def shape(size, kind=low):
        return jax.ShapeDtypeStruct(size, kind)

    vmem = pl.BlockSpec(memory_space=pltpu.VMEM)
    anywhere = pl.BlockSpec(memory_space=pl.ANY)
    dma = pltpu.SemaphoreType.DMA
    results = [
        shape((slots, depth)),
        shape((slots, units)),
        shape((depth, own_up.shape[1])),
        shape((units, depth)),
        shape((slots, 2 * units)),
        shape((units, depth)),
    ]
    return pl.pallas_call(
        body,
        in_specs=[vmem, vmem, anywhere, vmem, vmem, anywhere],
        out_specs=[anywhere] * 6,
        out_shape=results,
        scratch_shapes=[
            pltpu.VMEM((rows, depth), low),
            pltpu.VMEM((slots, 2 * units), jnp.float32),
            dma((6,)),
            dma((6,)),
            *(pltpu.VMEM(value.shape, value.dtype) for value in (weights, cotangent, *results)),
            dma((2,)),
            dma((9,)),
        ]
        + 2 * LineGather.scratch(chips),
        compiler_params=pltpu.CompilerParams(
            collective_id=collective_id, has_side_effects=True, vmem_limit_bytes=VMEM_LIMIT
        ),
        name="feed_forward",
    )(middle, gain, weights, own_up, own_down, cotangent)


def feed_backward(grads, weights, up_weights, normed, terms_down, w_out, middle, gain, cotangent, attended, gate_pre,
                  collective_id):
    rows, depth = middle.shape
    slots = 4 * rows
    units = grads.shape[1] // 2
    early = weights.shape[1]
    columns = attended.shape[1]
    shards = 2 * lax.axis_size("seq")
    chips = shards // 2
    low = jnp.bfloat16

    def body(grads_hbm, weights_hbm, up_weights_hbm, normed_hbm, down_hbm, out_hbm, middle_hbm, gain_ref, cot_hbm,
             attended_hbm, pre_hbm,
             grad_middle_hbm, grad_gain, branch_hbm, d_attended, d_pre, terms_up_hbm, share_down, share_gate,
             own_branch, summed, terms_gate, send, recv,
             grads_ref, weights_ref, up_weights_ref, normed_ref, down_ref, out_ref, middle_ref, cot_ref,
             attended_ref, pre_ref, grad_middle, branch, terms_up, fetch_sems, store_sems, *scratch):
        fetch, store = Streams(fetch_sems), Streams(store_sems)
        first_in = [
            fetch.start(*both)
            for both in (
                (grads_hbm, grads_ref),
                (weights_hbm, weights_ref),
                (up_weights_hbm, up_weights_ref),
                (down_hbm, down_ref),
            )
        ]
        normed_in = fetch.start(normed_hbm, normed_ref)
        rest_in = [
            fetch.start(*both)
            for both in (
                (middle_hbm, middle_ref),
                (cot_hbm, cot_ref),
                (out_hbm, out_ref),
                (attended_hbm, attended_ref),
                (pre_hbm, pre_ref),
            )
        ]
        me, side, down, across = sides()
        line_chips, chip, core, forth, back, twin = line()
        meet({"seq": side}, {"seq": down}, forth, back, twin)
        first, second = grads_ref.at[:, pl.ds(0, units)], grads_ref.at[:, pl.ds(units, units)]
        job = SquareScatter(
            [grads_ref.at[:, pl.ds(0, early)], grads_ref.at[:, pl.ds(early, 2 * units - early)]],
            [weights_ref, up_weights_ref],
            True,
            summed,
            *scratch[:7],
        )
        run_down = LineScatter(down_ref, share_down, *scratch[7:12])
        run_gate = LineScatter(terms_gate, share_gate, *scratch[12:])
        every = SquareGather(own_branch, branch, send, recv)
        for copy in first_in:
            copy.wait()
        run_down.start()
        job.begin()
        run_down.slot(0)
        normed_in.wait()
        transposed_product(normed_ref, first, terms_gate)
        run_gate.start()
        job.relay()
        run_down.slot(1)
        job.own()
        transposed_product(normed_ref, second, terms_up)
        store.start(terms_up, terms_up_hbm)
        run_down.slot(2)
        run_gate.slot(0)
        for copy in rest_in:
            copy.wait()
        job.end()
        values, change = middle_ref[...], summed[...]
        scale = norm_rows(values, gain_ref[...])[0]
        grad_gain[...] = jnp.sum(change * values * scale, axis=0, keepdims=True)
        change = change * gain_ref[...]
        mean = jnp.mean(change * values, axis=-1, keepdims=True)
        total = cot_ref[...].astype(jnp.float32) + scale * change - values * (scale * scale * scale * mean)
        grad_middle[...] = total
        own_branch[...] = total.astype(low)
        every.start()
        store.start(grad_middle, grad_middle_hbm)

        def rows_of(rank):
            return pl.ds(pl.multiple_of(rank * rows, rows), rows)

        def multiply(rank):
            at = rows_of(rank)
            grad_gated = product_nt(branch[at, :], out_ref[...])
            sigma = jax.nn.sigmoid(pre_ref[at, :])
            d_attended[at, :] = (grad_gated * sigma).astype(low)
            d_pre[at, :] = (
                grad_gated * attended_ref[at, :].astype(jnp.float32) * sigma * (1.0 - sigma)
            ).astype(low)

        branch[rows_of(me), :] = own_branch[...]
        multiply(me)
        run_gate.slot(1)
        every.relay()
        run_gate.slot(2)
        every.near()
        multiply(side)
        multiply(down)
        run_down.end()
        every.far()
        store.start(branch, branch_hbm)
        multiply(across)
        every.finish()
        run_gate.end()
        store.end()

    def shape(size, kind=low):
        return jax.ShapeDtypeStruct(size, kind)

    vmem = pl.BlockSpec(memory_space=pltpu.VMEM)
    anywhere = pl.BlockSpec(memory_space=pl.ANY)
    dma = pltpu.SemaphoreType.DMA
    fetched = (grads, weights, up_weights, normed, terms_down, w_out, middle, cotangent, attended, gate_pre)
    return pl.pallas_call(
        body,
        in_specs=[anywhere] * 7 + [vmem] + [anywhere] * 3,
        out_specs=[anywhere, vmem, anywhere, vmem, vmem, anywhere, vmem, vmem],
        out_shape=[
            shape((rows, depth), jnp.float32),
            shape((1, depth), jnp.float32),
            shape((slots, depth)),
            shape((slots, columns)),
            shape((slots, columns)),
            shape((depth, units)),
            shape((terms_down.shape[0] // shards, depth)),
            shape((depth // shards, units)),
        ],
        scratch_shapes=[
            pltpu.VMEM((rows, depth), low),
            pltpu.VMEM((rows, depth), jnp.float32),
            pltpu.VMEM((depth, units), low),
            dma((6,)),
            dma((6,)),
            *(pltpu.VMEM(value.shape, value.dtype) for value in fetched),
            pltpu.VMEM((rows, depth), jnp.float32),
            pltpu.VMEM((slots, depth), low),
            pltpu.VMEM((depth, units), low),
            dma((len(fetched),)),
            dma((3,)),
        ]
        + SquareScatter.scratch(rows, depth)
        + LineScatter.scratch(chips, terms_down.shape[0] // shards, depth)
        + LineScatter.scratch(chips, depth // shards, units),
        compiler_params=pltpu.CompilerParams(
            collective_id=collective_id, has_side_effects=True, vmem_limit_bytes=VMEM_LIMIT
        ),
        name="feed_backward",
    )(grads, weights, up_weights, normed, terms_down, w_out, middle, gain, cotangent, attended, gate_pre)


def gather(value, axis_name):
    return lax.all_gather(value, axis_name, axis=0, tiled=True)


def scatter(value, axis_name):
    return lax.psum_scatter(value, axis_name, scatter_dimension=0, tiled=True)


def on_device(
    layer_input,
    lengths,
    norm_attn,
    w_query,
    w_key,
    w_value,
    w_ogate,
    w_forget,
    forget_bias,
    w_out,
    norm_ffn,
    w_gate,
    w_up,
    w_down,
    output_grad,
):
    low = jnp.bfloat16
    tokens, width = layer_input.shape[1:]
    heads = forget_bias.shape[0]
    groups = lax.axis_size("seq")
    shards = lax.axis_size("wshard")
    fast = square(groups) and shards == 2 * groups
    local_heads = heads // groups
    head_size = width // heads
    columns = width // groups
    lanes = columns + -columns % PAIR
    front = 3 * lanes + PAIR
    slots = tokens * groups
    hidden_size = w_gate.shape[1]
    part = hidden_size // (groups * shards)
    units = shards * part
    scale = head_size ** (-0.5)
    length = lengths[0]
    seq_rank = lax.axis_index("seq")
    shard_rank = lax.axis_index("wshard")
    per_block = shards // groups
    positions = seq_rank * tokens + jnp.arange(tokens, dtype=jnp.int32)
    valid_slots = (positions < length)[:, None]
    inputs = layer_input[0].astype(jnp.float32)
    cotangent_low = jnp.where(valid_slots, output_grad[0], jnp.zeros((), low))
    cotangent = cotangent_low.astype(jnp.float32)

    def own_columns(weight, size):
        taken = lax.dynamic_slice_in_dim(weight, seq_rank * columns, columns, 1)
        return jnp.pad(taken, ((0, 0), (0, size - columns))) if size > columns else taken

    def own_units(weight):
        split = weight.reshape(weight.shape[0], shards, groups, part)
        mine = lax.dynamic_index_in_dim(split, seq_rank, 2, keepdims=False)
        return mine.reshape(weight.shape[0], units)

    own_forget = lax.dynamic_slice_in_dim(w_forget, seq_rank * local_heads, local_heads, 1)
    own_forget = jnp.pad(own_forget, ((0, 0), (0, PAIR - local_heads)))
    own_bias = lax.dynamic_slice_in_dim(forget_bias, seq_rank * local_heads, local_heads)
    own_bias = jnp.pad(own_bias, (0, PAIR - local_heads))[None]
    length_row = jnp.broadcast_to(lengths[:, None], (1, PAIR))
    mine_down = lax.dynamic_slice_in_dim(w_down, seq_rank * part, part, 0)
    if fast:
        (
            normed_attn, cotangent_all, full_front, full_ogate, full_out, full_ffn,
            joined, attended_low, offset, col, logit, gate_pre, gated, middle, mine_up,
        ) = whole_forward(
            layer_input[0], norm_attn[None], cotangent_low, (w_query, w_key, w_value, w_ogate), own_forget,
            own_bias, length_row, w_out, w_gate, w_up, head_size, scale, 0,
        )
        full_out = full_out.reshape(columns, width)
        normed_ffn, hidden, full_up, full_down, grad_gate_up, terms_down = feed_forward(
            middle, norm_ffn[None], full_ffn, mine_up, mine_down, cotangent_all, 1
        )
        (
            grad_middle, grad_norm_ffn, grad_branch, grad_attended, grad_gate_pre, terms_up, share_down, share_gate,
        ) = feed_backward(
            grad_gate_up, full_ffn, full_up, normed_ffn, terms_down, full_out, middle, norm_ffn[None],
            cotangent_low, attended_low, gate_pre, 2,
        )
        grad_norm_ffn = grad_norm_ffn[0]
        grads, bias_rows, lowered, collected, share_up, share_ogate, grad_down = middle_backward(
            joined, grad_attended, offset, col, logit, hidden, full_down, gated, grad_branch, terms_up, share_down,
            normed_attn, grad_gate_pre, head_size, scale, 3,
        )
        grad_normed_attn, share_attn, grad_out, every_gate, every_ogate = last_backward(
            grads, grad_gate_pre, normed_attn, full_front, full_ogate, collected, (share_gate, share_ogate), 4
        )
        grad_out = grad_out.reshape(columns // per_block, width)
    else:
        mine_front = jnp.concatenate(
            [*(own_columns(w, lanes) for w in (w_query, w_key, w_value)), own_forget], axis=1
        )
        full_front = gather(mine_front, "wshard")
        full_ogate = gather(own_columns(w_ogate, columns), "wshard")
        normed_attn = gather(rms_norm(inputs, norm_attn).astype(low), "seq")
        cotangent_all = gather(cotangent_low, "seq")
        full_out = lax.dynamic_slice_in_dim(gather(w_out, "wshard"), seq_rank * columns, columns, 0)
        full_ffn = gather(jnp.concatenate([own_units(w_gate), own_units(w_up)], axis=1), "wshard")
        joined = product(normed_attn, full_front).astype(low)
        gate_pre = product(normed_attn, full_ogate)
        attended_low, offset, col, logit = attention_fwd(joined, own_bias, length_row, head_size, scale)
        attended = attended_low[:, :columns].astype(jnp.float32)
        gated_full, pull_gate = jax.vjp(gate_product, attended, gate_pre)
        gated = gated_full.astype(low)
        middle = inputs + scatter(product(gated, full_out).astype(low), "seq").astype(jnp.float32)
        normed_ffn_own, pull_ffn_norm = jax.vjp(rms_norm, middle, norm_ffn)
        full_down = gather(mine_down, "wshard")
        normed_ffn = gather(normed_ffn_own.astype(low), "seq")
        gate_up = product(normed_ffn, full_ffn)
        hidden_full, pull_swiglu = jax.vjp(swiglu, gate_up[:, :units], gate_up[:, units:])
        hidden = hidden_full.astype(low)
        grad_hidden = product_nt(cotangent_all, full_down)
        grad_gate_full, grad_up_full = pull_swiglu(grad_hidden)
        grad_gate_up = jnp.concatenate([grad_gate_full.astype(low), grad_up_full.astype(low)], axis=1)
        share_down = scatter(product_tn(hidden, cotangent_all).astype(low), "wshard")
        share_ffn = scatter(product_tn(normed_ffn, grad_gate_up).astype(low), "wshard")
        grad_normed_ffn = scatter(product_nt(grad_gate_up, full_ffn).astype(low), "seq").astype(jnp.float32)
        grad_middle_part, grad_norm_ffn = pull_ffn_norm(grad_normed_ffn)
        grad_middle = cotangent + grad_middle_part
        grad_branch = gather(grad_middle.astype(low), "seq")
        grad_attended_full, grad_gate_pre_full = pull_gate(product_nt(grad_branch, full_out))
        grad_attended = grad_attended_full.astype(low)
        grad_gate_pre = grad_gate_pre_full.astype(low)
        if lanes > columns:
            grad_attended = jnp.pad(grad_attended, ((0, 0), (0, lanes - columns)))
        grads, bias_rows = attention_bwd(joined, grad_attended, offset, col, logit, head_size, scale)
        grad_projected = jnp.concatenate([grads, grad_gate_pre], axis=1)
        share_attn = scatter(product_tn(normed_attn, grad_projected).astype(low), "wshard")
        full_attn = jnp.concatenate([full_front, full_ogate], axis=1)
        grad_normed_attn = scatter(product_nt(grad_projected, full_attn).astype(low), "seq").astype(jnp.float32)
        lowered = scatter(product(hidden, full_down).astype(low), "seq").astype(jnp.float32)
        share_out = scatter(product_tn(gated, grad_branch).astype(low), "wshard")
        rows_out = columns // shards
        pieces_out = lax.all_gather(share_out, "seq", axis=0, tiled=False)
        takes = shards // per_block
        slots_out = jnp.where(
            (jnp.arange(per_block) == shard_rank // takes)[None, :, None, None],
            pieces_out[:, None],
            jnp.zeros((), low),
        ).reshape(shards, rows_out, width)
        moved = lax.all_to_all(slots_out, "wshard", split_axis=0, concat_axis=0, tiled=True)
        moved = moved.reshape(per_block, takes, rows_out, width)
        mine_out = lax.dynamic_index_in_dim(moved, shard_rank % per_block, 0, keepdims=False)
        grad_out = mine_out.reshape(columns // per_block, width).astype(jnp.float32)
    layer_output = (middle + lowered).astype(low)[None]
    grad_bias = lax.dynamic_update_slice_in_dim(
        jnp.zeros((heads,), jnp.float32), bias_rows[:local_heads, 0], seq_rank * local_heads, 0
    )
    unused_normed, pull_attn_norm = jax.vjp(rms_norm, inputs, norm_attn)
    grad_input_part, grad_norm_attn = pull_attn_norm(grad_normed_attn)
    grad_input = (grad_middle + grad_input_part)[None]

    rows = share_attn.shape[0]
    if fast:
        vector = jnp.concatenate([grad_norm_attn, grad_norm_ffn, grad_bias])
        vector = jnp.pad(vector, (0, -vector.shape[0] % 1024)).reshape(-1, 128)
        every_attn, every_up, vector = last_gather([share_attn, share_up], vector, 5)
        vector = vector.reshape(-1)
        small = vector[:width], vector[width : 2 * width], vector[2 * width : 2 * width + heads]
    else:
        every_attn, every_ffn, grad_down = [gather(v, "seq") for v in (share_attn, share_ffn, share_down)]
        small = lax.psum((grad_norm_attn, grad_norm_ffn, grad_bias), ("seq", "wshard"))
    every_attn = every_attn.reshape((groups,) + share_attn.shape)
    if fast:
        grad_w_gate, grad_w_up, grad_down, grad_out = join_units(
            every_gate.reshape((groups,) + share_gate.shape), every_up.reshape((groups,) + share_up.shape),
            grad_down, grad_out, part,
        )
        every_ogate = every_ogate.reshape((groups,) + share_ogate.shape)
        *weight_grads, grad_forget_w = join_columns(
            every_attn, every_ogate, columns, (0, lanes, 2 * lanes), 3 * lanes, heads
        )
    else:

        def join(first):
            taken = every_attn[:, :, first : first + columns]
            return taken.transpose(1, 0, 2).reshape(rows, width).astype(jnp.float32)

        def join_own_units(first):
            taken = every_ffn.reshape((groups,) + share_ffn.shape)[:, :, first * units : (first + 1) * units]
            taken = taken.reshape(groups, rows, shards, part).transpose(1, 2, 0, 3)
            return taken.reshape(rows, hidden_size).astype(jnp.float32)

        weight_grads = [join(first) for first in (0, lanes, 2 * lanes, front)]
        grad_w_gate, grad_w_up = join_own_units(0), join_own_units(1)
        grad_down = grad_down.astype(jnp.float32)
        grad_forget_w = every_attn[:, :, 3 * lanes : 3 * lanes + local_heads]
        grad_forget_w = grad_forget_w.transpose(1, 0, 2).reshape(rows, heads).astype(jnp.float32)
    return (
        layer_output,
        grad_input,
        small[0],
        *weight_grads,
        grad_forget_w,
        small[2],
        grad_out,
        small[1],
        grad_w_gate,
        grad_w_up,
        grad_down,
    )


def solution(mesh):
    return jax.shard_map(
        on_device,
        mesh=mesh,
        in_specs=(
            P("wshard", "seq", None),
            P("wshard"),
            P(),
            P("wshard", None),
            P("wshard", None),
            P("wshard", None),
            P("wshard", None),
            P("wshard", None),
            P(),
            P("wshard", None),
            P(),
            P("wshard", None),
            P("wshard", None),
            P("wshard", None),
            P("wshard", "seq", None),
        ),
        out_specs=(
            P("wshard", "seq", None),
            P("wshard", "seq", None),
            P(),
            P("wshard", None),
            P("wshard", None),
            P("wshard", None),
            P("wshard", None),
            P("wshard", None),
            P(),
            P("wshard", None),
            P(),
            P("wshard", None),
            P("wshard", None),
            P("wshard", None),
        ),
        check_vma=False,
    )
```

profile of v0, /device:TPU:0, one launch (start us, length us, event | category | flops | bytes accessed | tf_op | source)
XLA Modules:
  0.0 434.4 jit_solution(9550965996254051635)
XLA Ops:
  0.6 0.0 copy-start
  0.7 0.0 copy-start.4
  0.7 0.8 constant_dynamic-slice_fusion.1
  1.5 0.1 copy.33
  1.7 0.6 pad.12.forget_ref
  2.3 0.7 dynamic_slice.10
  3.0 0.5 pad_bitcast_fusion.bias_ref
  4.2 2.1 bitcast_select_fusion.cot_ref.cot_hbm
  6.3 0.5 broadcast_in_dim.44.length_ref
  6.9 0.0 copy-done.4
  6.9 0.6 broadcast_in_dim.40.gain_ref
  7.5 0.0 copy-start.6
  7.5 116.3 %whole_forward.1 = (bf16[1024,1536]{1,0:T(8,128)(2,1)}, bf16[1024,1536]{1,0:T(8,128)(2,1)}, bf16[1536,1280]{1,0:T(8,128)(2,1)}, bf16[1536,384]{1,0:T(8,128)(2,1)...) custom-call(bf16[256,1536]{1,0:T(8,128)(2,1)} %bitcast.29, ...), custom_call_target="tpu_custom_call" | custom-call | tf_op jit(solution)/shard_map/whole_forward/pallas_call | solution.py:1356
  123.8 0.0 copy-done
  123.8 0.8 constant_dynamic-slice_fusion.down_ref
  124.5 0.0 copy-done.6
  124.5 0.6 broadcast_in_dim.45.gain_ref
  125.1 56.3 %feed_forward.1 = (bf16[1024,1536]{1,0:T(8,128)(2,1)}, bf16[1024,1024]{1,0:T(8,128)(2,1)}, bf16[1536,512]{1,0:T(8,128)(2,1)}, bf16[1024,1536]{1,0:T(8,128)(2,1)}...) custom-call(f32[256,1536]{1,0:T(8,128)} %get-tuple-element.67.middle_ref.middle_hbm, ...), custom_call_target="tpu_custom_call" | custom-call | tf_op jit(solution)/shard_map/feed_forward/pallas_call | solution.py:1503
  181.4 70.7 %feed_backward.1 = (f32[256,1536]{1,0:T(8,128)}, f32[1,1536]{1,0:T(1,128)}, bf16[1024,1536]{1,0:T(8,128)(2,1)}, bf16[1024,384]{1,0:T(8,128)(2,1)}, bf16[1024,384...) custom-call(bf16[1024,2048]{1,0:T(8,128)(2,1)} %get-tuple-element.72.grads_hbm, ...), custom_call_target="tpu_custom_call" | custom-call | tf_op jit(solution)/shard_map/feed_backward/pallas_call | solution.py:1641
  252.2 60.4 %middle_backward.1 = (bf16[1024,1280]{1,0:T(8,128)(2,1)}, f32[8,128]{1,0:T(8,128)}, f32[256,1536]{1,0:T(8,128)}, bf16[48,1536]{1,0:T(8,128)(2,1)}, bf16[192,1024...) custom-call(bf16[1024,1280]{1,0:T(8,128)(2,1)} %get-tuple-element.68.joined_ref, ...), custom_call_target="tpu_custom_call" | custom-call | tf_op jit(solution)/shard_map/middle_backward/pallas_call | solution.py:1075
  312.6 0.0 copy-start.3
  312.6 64.2 %last_backward.1 = (f32[256,1536]{1,0:T(8,128)}, bf16[192,1280]{1,0:T(8,128)(2,1)}, bf16[4,48,1536]{2,1,0:T(8,128)(2,1)}, bf16[768,1024]{1,0:T(8,128)(2,1)}, bf16[768,384]{1,0:T(8,128)(2,1)}) custom-call(bf16[1024,1280]{1,0:T(8,128)(2,1)} %get-tuple-element.93.grads_ref, bf16[1024,384]{1,0:T(8,128)(2,1)} %get-tuple-element.90.pre_ref.gate_ref, ...), custom_call_target="tpu_custom_call" | custom-call | tf_op jit(solution)/shard_map/last_backward/pallas_call | solution.py:1171
  376.8 0.0 copy-done.3
  376.8 0.0 copy-start.8
  376.9 0.0 copy-start.7
  376.9 0.2 fusion.2
  377.1 1.9 fusion.5
  379.0 0.0 copy-done.8
  379.0 0.1 slice_reduce_fusion
  379.1 0.2 dynamic_update_slice.3
  379.4 0.0 copy-done.7
  379.4 0.6 fusion.7.refs_2_
  380.0 35.5 %last_gather.1 = (bf16[768,1280]{1,0:T(8,128)(2,1)}, bf16[768,1024]{1,0:T(8,128)(2,1)}, f32[32,128]{1,0:T(8,128)}) custom-call(bf16[192,1280]{1,0:T(8,128)(2,1)} %get-tuple-element.100.refs_0_, bf16[192,1024]{1,0:T(8,128)(2,1)} %get-tuple-element.101.refs_1_, f32[32,128]{1,0:T(8,128)} %fusion.7.refs_2_), custom_call_target="tpu_custom_call" | custom-call | tf_op jit(solution)/shard_map/last_gather/pallas_call | solution.py:704
  415.5 7.0 %join_units.1 = (f32[192,4096]{1,0:T(8,128)}, f32[192,4096]{1,0:T(8,128)}, f32[512,1536]{1,0:T(8,128)}, f32[192,1536]{1,0:T(8,128)}) custom-call(bf16[4,192,1024]{2,1,0:T(8,128)(2,1)} %bitcast.31, bf16[4,192,1024]{2,1,0:T(8,128)(2,1)} %bitcast.32, bf16[512,1536]{1,0:T(8,128)(2,1)} %get-tuple-element.114.down_in, bf16[192,1536]{1,0:T(8,128)(2,1)} %bitcast.35), custom_call_target="tpu_custom_call" | custom-call | tf_op jit(solution)/shard_map/join_units/pallas_call | solution.py:748
  422.5 0.0 copy-start.5
  422.5 0.0 copy-start.2
  422.5 4.4 %join_columns.1 = (f32[192,1536]{1,0:T(8,128)}, f32[192,1536]{1,0:T(8,128)}, f32[192,1536]{1,0:T(8,128)}, f32[192,1536]{1,0:T(8,128)}, f32[192,24]{1,0:T(8,128)}) custom-call(bf16[4,192,1280]{2,1,0:T(8,128)(2,1)} %bitcast.30, bf16[4,192,384]{2,1,0:T(8,128)(2,1)} %bitcast.34), custom_call_target="tpu_custom_call" | custom-call | tf_op jit(solution)/shard_map/join_columns/pallas_call | solution.py:779
  426.9 1.6 copy.32
  428.5 0.0 copy-done.5
  428.5 0.6 slice_bitcast_fusion
  429.1 0.5 slice.24
  429.6 0.0 copy-done.2
  429.6 0.0 copy-start.1
  429.7 4.7 %fusion.1 = (f32[1,256,1536]{2,1,0:T(8,128)}, bf16[1,256,1536]{2,1,0:T(8,128)(2,1)}) fusion(f32[256,1536]{1,0:T(8,128)} %get-tuple-element.92, f32[256,1536]{1,0:T(8,128)} %get-tuple-element.99, f32[256]{0:T(256)S(1)} %multiply_multiply_fusion, f32[256]{0:T(256)S(1)} %fusion.8, f32[1536]{0:T(1024)S(1)} %copy-done.4, bf16[1,256,1536]{2,1,0:T(8,128)(2,1)} %param.15, ...), kind=kLoop, calls=%fused_computation.6 | loop fusion | flops 3538944 | bytes 9445376 | tf_op jit(solution)/shard_map/broadcast_in_dim | solution.py:1833
  434.4 0.0 copy-done.1
  (5 shorter events, 0.0 us)
Async XLA Ops:
  0.6 123.1 %copy-start = (bf16[512,1536]{1,0:T(8,128)(2,1)S(1)}, bf16[512,1536]{1,0:T(8,128)(2,1)}, u32[]{:S(2)}) copy-start(bf16[512,1536]{1,0:T(8,128)(2,1)} %param.28) | copy-start | bytes 4718596
  0.7 6.2 %copy-start.4 = (f32[1536]{0:T(1024)S(1)}, f32[1536]{0:T(1024)}, u32[]{:S(2)}) copy-start(f32[1536]{0:T(1024)} %param.17) | copy-start | bytes 18436
  7.5 117.1 %copy-start.6 = (f32[1536]{0:T(1024)S(1)}, f32[1536]{0:T(1024)}, u32[]{:S(2)}) copy-start(f32[1536]{0:T(1024)} %param.25) | copy-start | bytes 18436
  312.6 64.3 %copy-start.3 = (bf16[1,256,1536]{2,1,0:T(8,128)(2,1)S(1)}, bf16[1,256,1536]{2,1,0:T(8,128)(2,1)}, u32[]{:S(2)}) copy-start(bf16[1,256,1536]{2,1,0:T(8,128)(2,1)} %param.15) | copy-start | bytes 2359300
  376.8 2.2 copy-start.8
  376.9 2.5 copy-start.7
  422.5 6.0 %copy-start.5 = (f32[32,128]{1,0:T(8,128)S(1)}, f32[32,128]{1,0:T(8,128)}, u32[]{:S(2)}) copy-start(f32[32,128]{1,0:T(8,128)} %get-tuple-element.104) | copy-start | bytes 49156
  422.5 7.1 %copy-start.2 = (f32[256,1536]{1,0:T(8,128)S(1)}, f32[256,1536]{1,0:T(8,128)}, u32[]{:S(2)}) copy-start(f32[256,1536]{1,0:T(8,128)} %get-tuple-element.67.middle_ref.middle_hbm) | copy-start | bytes 4718596
  429.6 4.8 %copy-start.1 = (bf16[512,1536]{1,0:T(8,128)(2,1)S(1)}, bf16[512,1536]{1,0:T(8,128)(2,1)}, u32[]{:S(2)}) copy-start(bf16[512,1536]{1,0:T(8,128)(2,1)} %param.28) | copy-start | bytes 4718596
where the time goes:
time: 435 us; the launch traced here: 434 us
  Pallas kernels  415 us (95%)
  other arithmetic  9.67 us (2%)
  local copies, waits for them, and re-layouts  8.43 us (2%)
    pallas_call x1, Pallas kernels, whole_forward(): pl.pallas_call(body, in_specs=[vmem] * 3 + [anywhere] * 4 + [vmem] * 3 +...  116 us
    pallas_call x1, Pallas kernels, feed_backward(): pl.pallas_call(body, in_specs=[anywhere] * 7 + [vmem] + [anywhere] * 3, o...  70.7 us
    pallas_call x1, Pallas kernels, last_backward(): pl.pallas_call(body, in_specs=[vmem] * (6 + count), out_specs=[vmem] * 3...  64.2 us
    pallas_call x1, Pallas kernels, middle_backward(): pl.pallas_call(body, in_specs=[vmem] * 13, out_specs=[vmem] * 6 + [pl.Blo...  60.4 us
    pallas_call x1, Pallas kernels, feed_forward(): pl.pallas_call(body, in_specs=[vmem, vmem, anywhere, vmem, vmem, anywhere...  56.3 us
    pallas_call x1, Pallas kernels, last_gather(): pl.pallas_call(body, in_specs=[vmem] * (count + 1), out_specs=[pl.BlockSp...  35.5 us

commit v1 on v0

--- a/solution.py
+++ b/solution.py
@@ -784,414 +784,6 @@
         out_shape=results,
         name="join_columns",
     )(every, gate)
-
-
-class SquareScatter:
-    @staticmethod
-    def scratch(rows, width):
-        half = rows // 2
-        low = jnp.bfloat16
-        return [
-            pltpu.VMEM((rows, width), low),
-            pltpu.VMEM((2, half, width), low),
-            pltpu.VMEM((2, half, width), jnp.float32),
-            pltpu.VMEM((6, half, width), low),
-            pltpu.VMEM((2, half, width), low),
-            pltpu.SemaphoreType.DMA((6,)),
-            pltpu.SemaphoreType.DMA((6,)),
-        ]
-
-    def __init__(self, lefts, rights, transposed, out, far, near, kept, land, carry, send, recv):
-        self.lefts, self.rights, self.transposed, self.out = lefts, rights, transposed, out
-        self.far, self.near, self.kept, self.land, self.carry = far, near, kept, land, carry
-        self.send, self.recv = send, recv
-        self.rows, self.width = out.shape
-        self.half = self.rows // 2
-        self.tile = self.width // 3 if self.width % 384 == 0 else self.width
-
-    def copy(self, index):
-        me, side, down, across = sides()
-        source = (
-            self.far.at[pl.ds(0, self.half)],
-            self.far.at[pl.ds(self.half, self.half)],
-            self.near.at[0],
-            self.near.at[1],
-            self.carry.at[0],
-            self.carry.at[1],
-        )[index]
-        return pltpu.make_async_remote_copy(
-            src_ref=source,
-            dst_ref=self.land.at[index],
-            send_sem=self.send.at[index],
-            recv_sem=self.recv.at[index],
-            device_id={"seq": down if index in (0, 3, 5) else side},
-            device_id_type=MESH,
-        )
-
-    def partial(self, rank, store):
-        at = pl.ds(pl.multiple_of(rank * self.rows, self.rows), self.rows)
-
-        def step(number, carried):
-            columns = pl.ds(pl.multiple_of(number * self.tile, self.tile), self.tile)
-            value = None
-            for a, b in zip(self.lefts, self.rights):
-                if self.transposed:
-                    term = product_nt(a[at, :], b[columns, :])
-                else:
-                    term = product(a[at, :], b[:, columns])
-                value = term if value is None else value + term
-            store(columns, value)
-            return carried
-
-        lax.fori_loop(0, self.width // self.tile, step, 0)
-
-    def begin(self):
-        me, side, down, across = sides()
-        half, far, near, kept = self.half, self.far, self.near, self.kept
-
-        def store_far(columns, value):
-            far[:, columns] = value.astype(far.dtype)
-
-        def store_side(columns, value):
-            kept[0, :, columns] = value[:half]
-            near[0, :, columns] = value[half:].astype(near.dtype)
-
-        def store_down(columns, value):
-            near[1, :, columns] = value[:half].astype(near.dtype)
-            kept[1, :, columns] = value[half:]
-
-        self.partial(across, store_far)
-        self.copy(0).start()
-        self.copy(1).start()
-        self.partial(side, store_side)
-        self.copy(2).start()
-        self.partial(down, store_down)
-        self.copy(3).start()
-
-    def relay(self):
-        for index in (0, 1):
-            self.copy(index).wait_recv()
-
-            def add(at, index=index):
-                total = self.kept[index, at, :] + self.land[index, at, :].astype(jnp.float32)
-                self.carry[index, at, :] = total.astype(self.carry.dtype)
-
-            by_rows(self.half, add)
-            self.copy(4 + index).start()
-
-    def own(self):
-        out = self.out
-
-        def store_own(columns, value):
-            out[:, columns] = value
-
-        self.partial(lax.axis_index("seq"), store_own)
-
-    def end(self):
-        for index in (2, 3, 4, 5):
-            self.copy(index).wait_recv()
-        land, half, out = self.land, self.half, self.out
-
-        def add(at):
-            out[at, :] += land[3, at, :].astype(jnp.float32) + land[4, at, :].astype(jnp.float32)
-
-        def add_second(at):
-            to = pl.ds(at.start + half, at.size)
-            out[to, :] += land[2, at, :].astype(jnp.float32) + land[5, at, :].astype(jnp.float32)
-
-        by_rows(half, add)
-        by_rows(half, add_second)
-        for index in range(6):
-            self.copy(index).wait_send()
-
-
-class LineScatter:
-    @staticmethod
-    def scratch(chips, rows, width):
-        low = jnp.bfloat16
-        dma = pltpu.SemaphoreType.DMA
-        return [pltpu.VMEM((chips, rows, width), low)] * 3 + [dma((2, chips)), dma((3, chips))]
-
-    def __init__(self, terms, out, twin_in, forth_in, back_in, send, recv):
-        self.terms, self.out, self.twin_in = terms, out, twin_in
-        self.forth_in, self.back_in, self.send, self.recv = forth_in, back_in, send, recv
-        self.chips, self.chip, self.core, *self.devices = line()
-        self.rows = twin_in.shape[1]
-
-    def term(self, chip, core):
-        return self.terms.at[pl.ds(pl.multiple_of((2 * chip + core) * self.rows, self.rows), self.rows)]
-
-    def swap(self, chip):
-        return pltpu.make_async_remote_copy(
-            src_ref=self.term(chip, 1 - self.core),
-            dst_ref=self.twin_in.at[chip],
-            send_sem=self.send.at[0, chip],
-            recv_sem=self.recv.at[0, chip],
-            device_id=self.devices[2],
-            device_id_type=MESH,
-        )
-
-    def hop(self, way, chip):
-        return pltpu.make_async_remote_copy(
-            src_ref=self.twin_in.at[chip],
-            dst_ref=(self.forth_in, self.back_in)[way].at[chip],
-            send_sem=self.send.at[1, chip],
-            recv_sem=self.recv.at[1 + way, chip],
-            device_id=self.devices[way],
-            device_id_type=MESH,
-        )
-
-    def start(self):
-        for chip in (self.chips - 1, 0, *range(1, self.chips - 1)):
-            self.swap(chip).start()
-
-    def add(self, chip, ways, out):
-        def step(at):
-            start = pl.multiple_of((2 * chip + self.core) * self.rows + at.start, at.size)
-            total = self.terms[pl.ds(start, at.size), :].astype(jnp.float32)
-            total = total + self.twin_in[chip, at, :].astype(jnp.float32)
-            for way in ways:
-                total = total + (self.forth_in, self.back_in)[way][chip, at, :].astype(jnp.float32)
-            out[at, :] = total.astype(out.dtype)
-
-        by_rows(self.rows, step)
-
-    def pass_on(self, way, chip, first):
-        self.swap(chip).wait_recv()
-        if not first:
-            self.hop(way, chip).wait_recv()
-        self.add(chip, () if first else (way,), self.twin_in.at[chip])
-        self.hop(way, chip).start()
-
-    def slot(self, number):
-        last = self.chips - 1
-        for chip in range(self.chips):
-            forth, back = number - (last - chip), last - (number - chip)
-            if 0 <= forth < chip:
-
-                @pl.when(self.chip == forth)
-                def _():
-                    self.pass_on(0, chip, forth == 0)
-
-            if chip < back <= last:
-
-                @pl.when(self.chip == back)
-                def _():
-                    self.pass_on(1, chip, back == last)
-
-    def end(self):
-        for chip in range(self.chips):
-
-            @pl.when(self.chip == chip)
-            def _():
-                self.swap(chip).wait_recv()
-                ways = [way for way, there in enumerate((chip > 0, chip < self.chips - 1)) if there]
-                for way in ways:
-                    self.hop(way, chip).wait_recv()
-                self.add(chip, ways, self.out)
-
-            self.swap(chip).wait_send()
-
-            @pl.when(self.chip != chip)
-            def _():
-                self.hop(0, chip).wait_send()
-
-
-def middle_backward(joined, d_out, offset, col, logit, hidden, w_down, gated, grad_branch, terms_up, share_down,
-                    normed, d_pre, head_size, scale, collective_id):
-    slots, lanes = joined.shape
-    width = w_down.shape[1]
-    tokens = slots // 4
-    columns = gated.shape[1]
-    shards = 2 * lax.axis_size("seq")
-    chips = shards // 2
-    rows_up = terms_up.shape[0] // shards
-
-    def body(joined_ref, d_out_ref, offset_ref, col_ref, logit_ref, hidden_ref, down_ref, gated_ref, branch_ref,
-             up_ref, share_ref, normed_ref, pre_ref,
-             grads, bias_grad, lowered, collected, share_up, share_pre, every_down, terms, terms_pre, send, recv, keep, *scratch):
-        me, side, down, across = sides()
-        line_chips, chip, core, forth, back, twin = line()
-        meet({"seq": side}, {"seq": down}, forth, back, twin)
-        work = Backward(
-            joined_ref, d_out_ref, offset_ref, col_ref, logit_ref, grads, *scratch[:4], head_size, scale
-        )
-        job = SquareScatter([hidden_ref], [down_ref], False, lowered, *scratch[4:11])
-        collect = LineScatter(terms, collected, *scratch[11:16])
-        run = LineScatter(up_ref, share_up, *scratch[16:21])
-        run_pre = LineScatter(terms_pre, share_pre, *scratch[21:])
-        every = SquareGather(share_ref, every_down, send, recv)
-        size = share_ref.shape[0]
-        kept = pltpu.make_async_copy(
-            share_ref, every_down.at[pl.ds(pl.multiple_of(me * size, size), size)], keep.at[0]
-        )
-        kept.start()
-        run.start()
-        transposed_product(gated_ref, branch_ref, terms)
-        collect.start()
-        transposed_product(normed_ref, pre_ref, terms_pre)
-        run_pre.start()
-        collect.slot(0)
-        run.slot(0)
-        job.begin()
-        run_pre.slot(0)
-        work.start()
-
-        def step(pair, carry):
-            work.pair(pair)
-
-            @pl.when(pair == 0)
-            def _():
-                job.relay()
-                collect.slot(1)
-                run.slot(1)
-                run_pre.slot(1)
-                every.start()
-
-            @pl.when(pair == 1)
-            def _():
-                collect.slot(2)
-                run.slot(2)
-                run_pre.slot(2)
-
-            return carry
-
-        lax.fori_loop(0, work.pairs, step, 0)
-        every.relay()
-        job.own()
-        work.end(bias_grad)
-        job.end()
-        run.end()
-        run_pre.end()
-        every.near()
-        every.far()
-        every.finish()
-        kept.wait()
-        collect.end()
-
-    vmem = pl.BlockSpec(memory_space=pltpu.VMEM)
-    low = jnp.bfloat16
-    dma = pltpu.SemaphoreType.DMA
-    return pl.pallas_call(
-        body,
-        in_specs=[vmem] * 13,
-        out_specs=[vmem] * 6 + [pl.BlockSpec(memory_space=pl.ANY)],
-        out_shape=[
-            jax.ShapeDtypeStruct((slots, lanes), low),
-            jax.ShapeDtypeStruct((8, PAIR), jnp.float32),
-            jax.ShapeDtypeStruct((tokens, width), jnp.float32),
-            jax.ShapeDtypeStruct((columns // shards, width), low),
-            jax.ShapeDtypeStruct((rows_up, terms_up.shape[1]), low),
-            jax.ShapeDtypeStruct((rows_up, columns), low),
-            jax.ShapeDtypeStruct((4 * share_down.shape[0], width), low),
-        ],
-        scratch_shapes=[
-            pltpu.VMEM((columns, width), low),
-            pltpu.VMEM((width, columns), low),
-            dma((6,)),
-            dma((6,)),
-            dma((1,)),
-        ]
-        + backward_scratch(slots)
-        + SquareScatter.scratch(tokens, width)
-        + LineScatter.scratch(chips, columns // shards, width)
-        + LineScatter.scratch(chips, rows_up, terms_up.shape[1])
-        + LineScatter.scratch(chips, rows_up, columns),
-        compiler_params=pltpu.CompilerParams(
-            collective_id=collective_id, has_side_effects=True, vmem_limit_bytes=VMEM_LIMIT
-        ),
-        name="middle_backward",
-    )(joined, d_out, offset, col, logit, hidden, w_down, gated, grad_branch, terms_up, share_down, normed, d_pre)
-
-
-def last_backward(grads, grad_gate_pre, normed, weights, gate_weights, collected, shares, collective_id):
-    slots, depth = normed.shape
-    front = grads.shape[1]
-    count = len(shares)
-    tokens = slots // 4
-    shards = 2 * lax.axis_size("seq")
-    rows = depth // shards
-
-    def body(grads_ref, gate_ref, normed_ref, weights_ref, gate_weights_ref, collected_ref,
-             *refs):
-        share_refs, refs = refs[:count], refs[count:]
-        summed, share, regrouped, *every_refs = refs[: 3 + count]
-        terms, send, recv, keep, *scratch = refs[3 + count :]
-        me, side, down, across = sides()
-        chips, chip, core, forth, back, twin = line()
-        regroup = Regroup(collected_ref, regrouped, *scratch[12:])
-        meet(*regroup.others, *regroup.along)
-        job = SquareScatter(
-            [grads_ref, gate_ref],
-            [weights_ref, gate_weights_ref],
-            True,
-            summed,
-            *scratch[:7],
-        )
-        run = LineScatter(terms, share, *scratch[7:12])
-        regroup.start()
-        every = [
-            SquareGather(share_refs[i], every_refs[i], send.at[i], recv.at[i]) for i in range(count)
-        ]
-        kept = []
-        for i in range(count):
-            size = share_refs[i].shape[0]
-            kept.append(
-                pltpu.make_async_copy(
-                    share_refs[i],
-                    every_refs[i].at[pl.ds(pl.multiple_of(me * size, size), size)],
-                    keep.at[i],
-                )
-            )
-            kept[i].start()
-            every[i].start()
-        transposed_product(normed_ref, grads_ref, terms)
-        run.start()
-        regroup.relay()
-        job.begin()
-        run.slot(0)
-        for gathering in every:
-            gathering.relay()
-        job.relay()
-        job.own()
-        run.slot(1)
-        run.slot(2)
-        for gathering, copy in zip(every, kept):
-            gathering.near()
-            gathering.far()
-            gathering.finish()
-            copy.wait()
-        job.end()
-        regroup.end()
-        run.end()
-
-    vmem = pl.BlockSpec(memory_space=pltpu.VMEM)
-    low = jnp.bfloat16
-    dma = pltpu.SemaphoreType.DMA
-    return pl.pallas_call(
-        body,
-        in_specs=[vmem] * (6 + count),
-        out_specs=[vmem] * 3 + [pl.BlockSpec(memory_space=pl.ANY)] * count,
-        out_shape=[
-            jax.ShapeDtypeStruct((tokens, depth), jnp.float32),
-            jax.ShapeDtypeStruct((rows, front), low),
-            jax.ShapeDtypeStruct((4,) + collected.shape, low),
-            *(jax.ShapeDtypeStruct((4 * v.shape[0], v.shape[1]), low) for v in shares),
-        ],
-        scratch_shapes=[
-            pltpu.VMEM((depth, front), low),
-            dma((count, 6)),
-            dma((count, 6)),
-            dma((count,)),
-        ]
-        + SquareScatter.scratch(tokens, depth)
-        + LineScatter.scratch(shards // 2, rows, front)
-        + Regroup.scratch(*collected.shape),
-        compiler_params=pltpu.CompilerParams(
-            collective_id=collective_id, has_side_effects=True, vmem_limit_bytes=VMEM_LIMIT
-        ),
-        name="last_backward",
-    )(grads, grad_gate_pre, normed, weights, gate_weights, collected, *shares)
 
 
 def norm_rows(values, gain):
@@ -1675,6 +1267,454 @@
     )(grads, weights, up_weights, normed, terms_down, w_out, middle, gain, cotangent, attended, gate_pre)
 
 
+class SquareScatter:
+    @staticmethod
+    def scratch(rows, width):
+        half = rows // 2
+        low = jnp.bfloat16
+        return [
+            pltpu.VMEM((rows, width), low),
+            pltpu.VMEM((2, half, width), low),
+            pltpu.VMEM((2, half, width), jnp.float32),
+            pltpu.VMEM((6, half, width), low),
+            pltpu.VMEM((2, half, width), low),
+            pltpu.SemaphoreType.DMA((6,)),
+            pltpu.SemaphoreType.DMA((6,)),
+        ]
+
+    def __init__(self, lefts, rights, transposed, out, far, near, kept, land, carry, send, recv):
+        self.lefts, self.rights, self.transposed, self.out = lefts, rights, transposed, out
+        self.far, self.near, self.kept, self.land, self.carry = far, near, kept, land, carry
+        self.send, self.recv = send, recv
+        self.rows, self.width = out.shape
+        self.half = self.rows // 2
+        self.tile = self.width // 3 if self.width % 384 == 0 else self.width
+
+    def copy(self, index):
+        me, side, down, across = sides()
+        source = (
+            self.far.at[pl.ds(0, self.half)],
+            self.far.at[pl.ds(self.half, self.half)],
+            self.near.at[0],
+            self.near.at[1],
+            self.carry.at[0],
+            self.carry.at[1],
+        )[index]
+        return pltpu.make_async_remote_copy(
+            src_ref=source,
+            dst_ref=self.land.at[index],
+            send_sem=self.send.at[index],
+            recv_sem=self.recv.at[index],
+            device_id={"seq": down if index in (0, 3, 5) else side},
+            device_id_type=MESH,
+        )
+
+    def partial(self, rank, store):
+        at = pl.ds(pl.multiple_of(rank * self.rows, self.rows), self.rows)
+
+        def step(number, carried):
+            columns = pl.ds(pl.multiple_of(number * self.tile, self.tile), self.tile)
+            value = None
+            for a, b in zip(self.lefts, self.rights):
+                if self.transposed:
+                    term = product_nt(a[at, :], b[columns, :])
+                else:
+                    term = product(a[at, :], b[:, columns])
+                value = term if value is None else value + term
+            store(columns, value)
+            return carried
+
+        lax.fori_loop(0, self.width // self.tile, step, 0)
+
+    def begin(self):
+        me, side, down, across = sides()
+        half, far, near, kept = self.half, self.far, self.near, self.kept
+
+        def store_far(columns, value):
+            far[:, columns] = value.astype(far.dtype)
+
+        def store_side(columns, value):
+            kept[0, :, columns] = value[:half]
+            near[0, :, columns] = value[half:].astype(near.dtype)
+
+        def store_down(columns, value):
+            near[1, :, columns] = value[:half].astype(near.dtype)
+            kept[1, :, columns] = value[half:]
+
+        self.partial(across, store_far)
+        self.copy(0).start()
+        self.copy(1).start()
+        self.partial(side, store_side)
+        self.copy(2).start()
+        self.partial(down, store_down)
+        self.copy(3).start()
+
+    def relay(self):
+        for index in (0, 1):
+            self.copy(index).wait_recv()
+
+            def add(at, index=index):
+                total = self.kept[index, at, :] + self.land[index, at, :].astype(jnp.float32)
+                self.carry[index, at, :] = total.astype(self.carry.dtype)
+
+            by_rows(self.half, add)
+            self.copy(4 + index).start()
+
+    def own(self):
+        out = self.out
+
+        def store_own(columns, value):
+            out[:, columns] = value
+
+        self.partial(lax.axis_index("seq"), store_own)
+
+    def end(self):
+        for index in (2, 3, 4, 5):
+            self.copy(index).wait_recv()
+        land, half, out = self.land, self.half, self.out
+
+        def add(at):
+            out[at, :] += land[3, at, :].astype(jnp.float32) + land[4, at, :].astype(jnp.float32)
+
+        def add_second(at):
+            to = pl.ds(at.start + half, at.size)
+            out[to, :] += land[2, at, :].astype(jnp.float32) + land[5, at, :].astype(jnp.float32)
+
+        by_rows(half, add)
+        by_rows(half, add_second)
+        for index in range(6):
+            self.copy(index).wait_send()
+
+
+class LineScatter:
+    @staticmethod
+    def scratch(chips, rows, width):
+        low = jnp.bfloat16
+        dma = pltpu.SemaphoreType.DMA
+        return [pltpu.VMEM((chips, rows, width), low)] * 3 + [dma((2, chips)), dma((3, chips))]
+
+    def __init__(self, terms, out, twin_in, forth_in, back_in, send, recv):
+        self.terms, self.out, self.twin_in = terms, out, twin_in
+        self.forth_in, self.back_in, self.send, self.recv = forth_in, back_in, send, recv
+        self.chips, self.chip, self.core, *self.devices = line()
+        self.rows = twin_in.shape[1]
+
+    def term(self, chip, core):
+        return self.terms.at[pl.ds(pl.multiple_of((2 * chip + core) * self.rows, self.rows), self.rows)]
+
+    def swap(self, chip):
+        return pltpu.make_async_remote_copy(
+            src_ref=self.term(chip, 1 - self.core),
+            dst_ref=self.twin_in.at[chip],
+            send_sem=self.send.at[0, chip],
+            recv_sem=self.recv.at[0, chip],
+            device_id=self.devices[2],
+            device_id_type=MESH,
+        )
+
+    def hop(self, way, chip):
+        return pltpu.make_async_remote_copy(
+            src_ref=self.twin_in.at[chip],
+            dst_ref=(self.forth_in, self.back_in)[way].at[chip],
+            send_sem=self.send.at[1, chip],
+            recv_sem=self.recv.at[1 + way, chip],
+            device_id=self.devices[way],
+            device_id_type=MESH,
+        )
+
+    def start(self):
+        for chip in (self.chips - 1, 0, *range(1, self.chips - 1)):
+            self.swap(chip).start()
+
+    def add(self, chip, ways, out):
+        def step(at):
+            start = pl.multiple_of((2 * chip + self.core) * self.rows + at.start, at.size)
+            total = self.terms[pl.ds(start, at.size), :].astype(jnp.float32)
+            total = total + self.twin_in[chip, at, :].astype(jnp.float32)
+            for way in ways:
+                total = total + (self.forth_in, self.back_in)[way][chip, at, :].astype(jnp.float32)
+            out[at, :] = total.astype(out.dtype)
+
+        by_rows(self.rows, step)
+
+    def pass_on(self, way, chip, first):
+        self.swap(chip).wait_recv()
+        if not first:
+            self.hop(way, chip).wait_recv()
+        self.add(chip, () if first else (way,), self.twin_in.at[chip])
+        self.hop(way, chip).start()
+
+    def slot(self, number):
+        last = self.chips - 1
+        for chip in range(self.chips):
+            forth, back = number - (last - chip), last - (number - chip)
+            if 0 <= forth < chip:
+
+                @pl.when(self.chip == forth)
+                def _():
+                    self.pass_on(0, chip, forth == 0)
+
+            if chip < back <= last:
+
+                @pl.when(self.chip == back)
+                def _():
+                    self.pass_on(1, chip, back == last)
+
+    def end(self):
+        for chip in range(self.chips):
+
+            @pl.when(self.chip == chip)
+            def _():
+                self.swap(chip).wait_recv()
+                ways = [way for way, there in enumerate((chip > 0, chip < self.chips - 1)) if there]
+                for way in ways:
+                    self.hop(way, chip).wait_recv()
+                self.add(chip, ways, self.out)
+
+            self.swap(chip).wait_send()
+
+            @pl.when(self.chip != chip)
+            def _():
+                self.hop(0, chip).wait_send()
+
+
+def middle_backward(joined, d_out, offset, col, logit, hidden, w_down, gated, grad_branch, terms_up, shares,
+                    normed, d_pre, middle, head_size, scale, collective_id):
+    slots, lanes = joined.shape
+    width = w_down.shape[1]
+    tokens = slots // 4
+    columns = gated.shape[1]
+    shards = 2 * lax.axis_size("seq")
+    chips = shards // 2
+    rows_up = terms_up.shape[0] // shards
+    fetched = (terms_up, gated, grad_branch, normed, d_pre, hidden, w_down, joined, d_out, middle)
+
+    def body(*refs):
+        sources, refs = refs[:10], refs[10:]
+        (offset_ref, col_ref, logit_ref, *share_refs), refs = refs[:5], refs[5:]
+        (grads, bias_grad, layer_output, collected, share_up, share_pre, *every_refs), refs = refs[:8], refs[8:]
+        buffers, refs = refs[:10], refs[10:]
+        terms, terms_pre, lowered, send, recv, keep, fetch_sems, *scratch = refs
+        up_ref, gated_ref, branch_ref, normed_ref, pre_ref, hidden_ref, down_ref, joined_ref, d_out_ref = buffers[:9]
+        fetch = Streams(fetch_sems)
+        comes = [fetch.start(source, buffer) for source, buffer in zip(sources, buffers)]
+        me, side, down, across = sides()
+        line_chips, chip, core, forth, back, twin = line()
+        meet({"seq": side}, {"seq": down}, forth, back, twin)
+        work = Backward(
+            joined_ref, d_out_ref, offset_ref, col_ref, logit_ref, grads, *scratch[:4], head_size, scale
+        )
+        job = SquareScatter([hidden_ref], [down_ref], False, lowered, *scratch[4:11])
+        collect = LineScatter(terms, collected, *scratch[11:16])
+        run = LineScatter(up_ref, share_up, *scratch[16:21])
+        run_pre = LineScatter(terms_pre, share_pre, *scratch[21:])
+        every = [SquareGather(share_refs[i], every_refs[i], send.at[i], recv.at[i]) for i in range(2)]
+        every[0].start()
+        comes[0].wait()
+        run.start()
+        kept = []
+        for i in range(2):
+            size = share_refs[i].shape[0]
+            kept.append(
+                pltpu.make_async_copy(
+                    share_refs[i],
+                    every_refs[i].at[pl.ds(pl.multiple_of(me * size, size), size)],
+                    keep.at[i],
+                )
+            )
+            kept[i].start()
+        comes[1].wait()
+        comes[2].wait()
+        transposed_product(gated_ref, branch_ref, terms)
+        collect.start()
+        run.slot(0)
+        comes[3].wait()
+        comes[4].wait()
+        transposed_product(normed_ref, pre_ref, terms_pre)
+        run_pre.start()
+        collect.slot(0)
+        for copy in comes[5:]:
+            copy.wait()
+        job.begin()
+        run_pre.slot(0)
+        work.start()
+
+        def step(pair, carry):
+            work.pair(pair)
+
+            @pl.when(pair == 0)
+            def _():
+                run.slot(1)
+                job.relay()
+                every[0].relay()
+                every[1].start()
+                collect.slot(1)
+                run_pre.slot(1)
+
+            @pl.when(pair == 1)
+            def _():
+                run.slot(2)
+                collect.slot(2)
+                run_pre.slot(2)
+                every[1].relay()
+
+            return carry
+
+        lax.fori_loop(0, work.pairs, step, 0)
+        job.own()
+        work.end(bias_grad)
+        job.end()
+        layer_output[...] = (buffers[9][...] + lowered[...]).astype(layer_output.dtype)
+        run.end()
+        collect.end()
+        run_pre.end()
+        for gathering, copy in zip(every, kept):
+            gathering.near()
+            gathering.far()
+            gathering.finish()
+            copy.wait()
+
+    vmem = pl.BlockSpec(memory_space=pltpu.VMEM)
+    anywhere = pl.BlockSpec(memory_space=pl.ANY)
+    low = jnp.bfloat16
+    dma = pltpu.SemaphoreType.DMA
+    return pl.pallas_call(
+        body,
+        in_specs=[anywhere] * 10 + [vmem] * 5,
+        out_specs=[vmem] * 6 + [anywhere] * 2,
+        out_shape=[
+            jax.ShapeDtypeStruct((slots, lanes), low),
+            jax.ShapeDtypeStruct((8, PAIR), jnp.float32),
+            jax.ShapeDtypeStruct((tokens, width), low),
+            jax.ShapeDtypeStruct((columns // shards, width), low),
+            jax.ShapeDtypeStruct((rows_up, terms_up.shape[1]), low),
+            jax.ShapeDtypeStruct((rows_up, columns), low),
+            *(jax.ShapeDtypeStruct((4 * v.shape[0], v.shape[1]), low) for v in shares),
+        ],
+        scratch_shapes=[
+            *(pltpu.VMEM(value.shape, value.dtype) for value in fetched),
+            pltpu.VMEM((columns, width), low),
+            pltpu.VMEM((width, columns), low),
+            pltpu.VMEM((tokens, width), jnp.float32),
+            dma((2, 6)),
+            dma((2, 6)),
+            dma((2,)),
+            dma((10,)),
+        ]
+        + backward_scratch(slots)
+        + SquareScatter.scratch(tokens, width)
+        + LineScatter.scratch(chips, columns // shards, width)
+        + LineScatter.scratch(chips, rows_up, terms_up.shape[1])
+        + LineScatter.scratch(chips, rows_up, columns),
+        compiler_params=pltpu.CompilerParams(
+            collective_id=collective_id, has_side_effects=True, vmem_limit_bytes=VMEM_LIMIT
+        ),
+        name="middle_backward",
+    )(*fetched, offset, col, logit, *shares)
+
+
+def last_backward(grads, d_pre, normed, weights, gate_weights, collected, shares, inputs, gain, grad_middle,
+                  collective_id):
+    slots, depth = normed.shape
+    front = grads.shape[1]
+    tokens = slots // 4
+    shards = 2 * lax.axis_size("seq")
+    rows = depth // shards
+    fetched = (normed, grads, d_pre, weights, gate_weights, inputs, grad_middle)
+
+    def body(*refs):
+        sources, refs = refs[:7], refs[7:]
+        (collected_ref, gain_ref, *share_refs), refs = refs[:4], refs[4:]
+        (grad_input, grad_gain, share, regrouped, *every_refs), refs = refs[:6], refs[6:]
+        buffers, refs = refs[:7], refs[7:]
+        terms, summed, send, recv, keep, fetch_sems, *scratch = refs
+        normed_ref, grads_ref, pre_ref, weights_ref, gate_weights_ref, inputs_ref, middle_ref = buffers
+        fetch = Streams(fetch_sems)
+        comes = [fetch.start(source, buffer) for source, buffer in zip(sources, buffers)]
+        me, side, down, across = sides()
+        regroup = Regroup(collected_ref, regrouped, *scratch[12:])
+        meet(*regroup.others, *regroup.along)
+        job = SquareScatter([grads_ref, pre_ref], [weights_ref, gate_weights_ref], True, summed, *scratch[:7])
+        run = LineScatter(terms, share, *scratch[7:12])
+        regroup.start()
+        every = [SquareGather(share_refs[i], every_refs[i], send.at[i], recv.at[i]) for i in range(2)]
+        every[0].start()
+        kept = []
+        for i in range(2):
+            size = share_refs[i].shape[0]
+            kept.append(
+                pltpu.make_async_copy(
+                    share_refs[i],
+                    every_refs[i].at[pl.ds(pl.multiple_of(me * size, size), size)],
+                    keep.at[i],
+                )
+            )
+            kept[i].start()
+        comes[0].wait()
+        comes[1].wait()
+        transposed_product(normed_ref, grads_ref, terms)
+        run.start()
+        every[0].relay()
+        regroup.relay()
+        run.slot(0)
+        for copy in comes[2:]:
+            copy.wait()
+        job.begin()
+        every[1].start()
+        job.relay()
+        run.slot(1)
+        job.own()
+        every[1].relay()
+        run.slot(2)
+        job.end()
+        values, change = inputs_ref[...].astype(jnp.float32), summed[...]
+        scale = norm_rows(values, gain_ref[...])[0]
+        grad_gain[...] = jnp.sum(change * values * scale, axis=0, keepdims=True)
+        change = change * gain_ref[...]
+        mean = jnp.mean(change * values, axis=-1, keepdims=True)
+        grad_input[...] = middle_ref[...] + scale * change - values * (scale * scale * scale * mean)
+        for gathering, copy in zip(every, kept):
+            gathering.near()
+            gathering.far()
+            gathering.finish()
+            copy.wait()
+        regroup.end()
+        run.end()
+
+    vmem = pl.BlockSpec(memory_space=pltpu.VMEM)
+    anywhere = pl.BlockSpec(memory_space=pl.ANY)
+    low = jnp.bfloat16
+    dma = pltpu.SemaphoreType.DMA
+    return pl.pallas_call(
+        body,
+        in_specs=[anywhere] * 7 + [vmem] * 4,
+        out_specs=[vmem] * 4 + [anywhere] * 2,
+        out_shape=[
+            jax.ShapeDtypeStruct((tokens, depth), jnp.float32),
+            jax.ShapeDtypeStruct((1, depth), jnp.float32),
+            jax.ShapeDtypeStruct((rows, front), low),
+            jax.ShapeDtypeStruct((4,) + collected.shape, low),
+            *(jax.ShapeDtypeStruct((4 * v.shape[0], v.shape[1]), low) for v in shares),
+        ],
+        scratch_shapes=[
+            *(pltpu.VMEM(value.shape, value.dtype) for value in fetched),
+            pltpu.VMEM((depth, front), low),
+            pltpu.VMEM((tokens, depth), jnp.float32),
+            dma((2, 6)),
+            dma((2, 6)),
+            dma((2,)),
+            dma((7,)),
+        ]
+        + SquareScatter.scratch(tokens, depth)
+        + LineScatter.scratch(shards // 2, rows, front)
+        + Regroup.scratch(*collected.shape),
+        compiler_params=pltpu.CompilerParams(
+            collective_id=collective_id, has_side_effects=True, vmem_limit_bytes=VMEM_LIMIT
+        ),
+        name="last_backward",
+    )(*fetched, collected, gain, *shares)
+
+
 def gather(value, axis_name):
     return lax.all_gather(value, axis_name, axis=0, tiled=True)
 
@@ -1760,13 +1800,15 @@
             cotangent_low, attended_low, gate_pre, 2,
         )
         grad_norm_ffn = grad_norm_ffn[0]
-        grads, bias_rows, lowered, collected, share_up, share_ogate, grad_down = middle_backward(
-            joined, grad_attended, offset, col, logit, hidden, full_down, gated, grad_branch, terms_up, share_down,
-            normed_attn, grad_gate_pre, head_size, scale, 3,
+        grads, bias_rows, layer_output, collected, share_up, share_ogate, grad_down, every_gate = middle_backward(
+            joined, grad_attended, offset, col, logit, hidden, full_down, gated, grad_branch, terms_up,
+            (share_down, share_gate), normed_attn, grad_gate_pre, middle, head_size, scale, 3,
         )
-        grad_normed_attn, share_attn, grad_out, every_gate, every_ogate = last_backward(
-            grads, grad_gate_pre, normed_attn, full_front, full_ogate, collected, (share_gate, share_ogate), 4
+        grad_input, grad_norm_attn, share_attn, grad_out, every_ogate, every_up = last_backward(
+            grads, grad_gate_pre, normed_attn, full_front, full_ogate, collected, (share_ogate, share_up),
+            layer_input[0], norm_attn[None], grad_middle, 4,
         )
+        grad_norm_attn = grad_norm_attn[0]
         grad_out = grad_out.reshape(columns // per_block, width)
     else:
         mine_front = jnp.concatenate(
@@ -1824,19 +1866,19 @@
         moved = moved.reshape(per_block, takes, rows_out, width)
         mine_out = lax.dynamic_index_in_dim(moved, shard_rank % per_block, 0, keepdims=False)
         grad_out = mine_out.reshape(columns // per_block, width).astype(jnp.float32)
-    layer_output = (middle + lowered).astype(low)[None]
+        layer_output = (middle + lowered).astype(low)
+        unused_normed, pull_attn_norm = jax.vjp(rms_norm, inputs, norm_attn)
+        grad_input_part, grad_norm_attn = pull_attn_norm(grad_normed_attn)
+        grad_input = grad_middle + grad_input_part
     grad_bias = lax.dynamic_update_slice_in_dim(
         jnp.zeros((heads,), jnp.float32), bias_rows[:local_heads, 0], seq_rank * local_heads, 0
     )
-    unused_normed, pull_attn_norm = jax.vjp(rms_norm, inputs, norm_attn)
-    grad_input_part, grad_norm_attn = pull_attn_norm(grad_normed_attn)
-    grad_input = (grad_middle + grad_input_part)[None]
 
     rows = share_attn.shape[0]
     if fast:
         vector = jnp.concatenate([grad_norm_attn, grad_norm_ffn, grad_bias])
         vector = jnp.pad(vector, (0, -vector.shape[0] % 1024)).reshape(-1, 128)
-        every_attn, every_up, vector = last_gather([share_attn, share_up], vector, 5)
+        every_attn, vector = last_gather([share_attn], vector, 5)
         vector = vector.reshape(-1)
         small = vector[:width], vector[width : 2 * width], vector[2 * width : 2 * width + heads]
     else:
@@ -1869,8 +1911,8 @@
         grad_forget_w = every_attn[:, :, 3 * lanes : 3 * lanes + local_heads]
         grad_forget_w = grad_forget_w.transpose(1, 0, 2).reshape(rows, heads).astype(jnp.float32)
     return (
-        layer_output,
-        grad_input,
+        layer_output[None],
+        grad_input[None],
         small[0],
         *weight_grads,
         grad_forget_w,

time: 435 us -> 413 us (0.949)
  Pallas kernels: 415 us -> 396 us
  other arithmetic: 9.67 us -> 2.8 us
    pallas_call x1, Pallas kernels: 35.5 us -> 24.5 us  [last_gather(): pl.pallas_call(body, in_specs=[vmem] * (count + 1), out_specs=[pl.BlockSp...]
    pallas_call x2, Pallas kernels: 125 us -> 117 us  [the longest x1 59.3 us: middle_backward(): pl.pallas_call(body, in_specs=[anywhere] * 10 + [vmem] * 5, out_specs=[vm...]
    broadcast_in_dim x1 -> x0, other arithmetic: 4.74 us -> none  [on_device(): grad_input = (grad_middle + grad_input_part)[None]]
where the time goes in v1:
time: 413 us; the launch traced here: 412 us
  Pallas kernels  396 us (96%)
  local copies, waits for them, and re-layouts  11.8 us (3%)
    pallas_call x1, Pallas kernels, whole_forward(): pl.pallas_call(body, in_specs=[vmem] * 3 + [anywhere] * 4 + [vmem] * 3 +...  116 us
    pallas_call x1, Pallas kernels, feed_backward(): pl.pallas_call(body, in_specs=[anywhere] * 7 + [vmem] + [anywhere] * 3, o...  70.8 us
    pallas_call x1, Pallas kernels, middle_backward(): pl.pallas_call(body, in_specs=[anywhere] * 10 + [vmem] * 5, out_specs=[vm...  59.3 us
    pallas_call x1, Pallas kernels, last_backward(): pl.pallas_call(body, in_specs=[anywhere] * 7 + [vmem] * 4, out_specs=[vme...  57.5 us
    pallas_call x1, Pallas kernels, feed_forward(): pl.pallas_call(body, in_specs=[vmem, vmem, anywhere, vmem, vmem, anywhere...  56.3 us
    pallas_call x1, Pallas kernels, last_gather(): pl.pallas_call(body, in_specs=[vmem] * (count + 1), out_specs=[pl.BlockSp...  24.5 us

profile of v1, /device:TPU:0, one launch (start us, length us, event | category | flops | bytes accessed | tf_op | source)
XLA Modules:
  0.0 412.0 jit_solution(1828741877080465652)
XLA Ops:
  0.6 0.0 copy-start
  0.7 0.0 copy-start.4
  0.7 0.8 constant_dynamic-slice_fusion.1
  1.5 0.1 copy.33
  1.6 0.6 pad.12.forget_ref
  2.3 0.7 dynamic_slice.10
  3.0 0.5 pad_bitcast_fusion.bias_ref
  4.2 2.1 bitcast_select_fusion.cot_ref.cot_hbm
  6.3 0.0 copy-done.4
  6.3 0.6 broadcast_in_dim.36.gain_ref.refs_8_
  6.9 0.5 broadcast_in_dim.40.length_ref
  7.5 0.0 copy-start.5
  7.5 116.3 %whole_forward.1 = (bf16[1024,1536]{1,0:T(8,128)(2,1)}, bf16[1024,1536]{1,0:T(8,128)(2,1)}, bf16[1536,1280]{1,0:T(8,128)(2,1)}, bf16[1536,384]{1,0:T(8,128)(2,1)...) custom-call(bf16[256,1536]{1,0:T(8,128)(2,1)} %bitcast.23, ...), custom_call_target="tpu_custom_call" | custom-call | tf_op jit(solution)/shard_map/whole_forward/pallas_call | solution.py:948
  123.7 0.0 copy-done
  123.8 0.8 constant_dynamic-slice_fusion.down_ref
  124.5 0.0 copy-done.5
  124.5 0.6 broadcast_in_dim.41.gain_ref
  125.1 56.3 %feed_forward.1 = (bf16[1024,1536]{1,0:T(8,128)(2,1)}, bf16[1024,1024]{1,0:T(8,128)(2,1)}, bf16[1536,512]{1,0:T(8,128)(2,1)}, bf16[1024,1536]{1,0:T(8,128)(2,1)}...) custom-call(f32[256,1536]{1,0:T(8,128)} %get-tuple-element.68.middle_ref.middle_hbm.refs_9_, ...), custom_call_target="tpu_custom_call" | custom-call | tf_op jit(solution)/shard_map/feed_forward/pallas_call | solution.py:1095
  181.4 70.8 %feed_backward.1 = (f32[256,1536]{1,0:T(8,128)}, f32[1,1536]{1,0:T(1,128)}, bf16[1024,1536]{1,0:T(8,128)(2,1)}, bf16[1024,384]{1,0:T(8,128)(2,1)}, bf16[1024,384...) custom-call(bf16[1024,2048]{1,0:T(8,128)(2,1)} %get-tuple-element.72.grads_hbm, ...), custom_call_target="tpu_custom_call" | custom-call | tf_op jit(solution)/shard_map/feed_backward/pallas_call | solution.py:1233
  252.2 59.3 %middle_backward.1 = (bf16[1024,1280]{1,0:T(8,128)(2,1)}, f32[8,128]{1,0:T(8,128)}, bf16[256,1536]{1,0:T(8,128)(2,1)}, bf16[48,1536]{1,0:T(8,128)(2,1)}, bf16[19...) custom-call(bf16[1536,1024]{1,0:T(8,128)(2,1)} %get-tuple-element.79.refs_, ...), custom_call_target="tpu_custom_call" | custom-call | tf_op jit(solution)/shard_map/middle_backward/pallas_call | solution.py:1581
  311.5 57.5 %last_backward.1 = (f32[256,1536]{1,0:T(8,128)}, f32[1,1536]{1,0:T(1,128)}, bf16[192,1280]{1,0:T(8,128)(2,1)}, bf16[4,48,1536]{2,1,0:T(8,128)(2,1)}, bf16[768,38...) custom-call(bf16[1024,1536]{1,0:T(8,128)(2,1)} %get-tuple-element.82.refs_3_.refs_0_, ...), custom_call_target="tpu_custom_call" | custom-call | tf_op jit(solution)/shard_map/last_backward/pallas_call | solution.py:1688
  368.9 0.0 copy-start.7
  369.0 0.0 copy-start.8
  369.0 0.0 copy-start.6
  369.0 7.0 %join_units.1 = (f32[192,4096]{1,0:T(8,128)}, f32[192,4096]{1,0:T(8,128)}, f32[512,1536]{1,0:T(8,128)}, f32[192,1536]{1,0:T(8,128)}) custom-call(bf16[4,192,1024]{2,1,0:T(8,128)(2,1)} %bitcast.27, bf16[4,192,1024]{2,1,0:T(8,128)(2,1)} %bitcast.28, bf16[512,1536]{1,0:T(8,128)(2,1)} %get-tuple-element.116.down_in, bf16[192,1536]{1,0:T(8,128)(2,1)} %bitcast.32), custom_call_target="tpu_custom_call" | custom-call | tf_op jit(solution)/shard_map/join_units/pallas_call | solution.py:748
  375.9 0.0 copy-done.7
  376.0 0.0 copy-done.8
  376.0 0.1 slice_reduce_fusion
  376.1 0.2 dynamic_update_slice.3
  376.3 0.0 copy-done.6
  376.4 0.6 fusion.refs_1_
  377.0 24.5 %last_gather.1 = (bf16[768,1280]{1,0:T(8,128)(2,1)}, f32[32,128]{1,0:T(8,128)}) custom-call(bf16[192,1280]{1,0:T(8,128)(2,1)} %get-tuple-element.102.refs_0_, f32[32,128]{1,0:T(8,128)} %fusion.refs_1_), custom_call_target="tpu_custom_call" | custom-call | tf_op jit(solution)/shard_map/last_gather/pallas_call | solution.py:704
  401.5 0.0 copy-start.3
  401.5 0.0 copy-start.2
  401.5 4.4 %join_columns.1 = (f32[192,1536]{1,0:T(8,128)}, f32[192,1536]{1,0:T(8,128)}, f32[192,1536]{1,0:T(8,128)}, f32[192,1536]{1,0:T(8,128)}, f32[192,24]{1,0:T(8,128)}) custom-call(bf16[4,192,1280]{2,1,0:T(8,128)(2,1)} %bitcast.25, bf16[4,192,384]{2,1,0:T(8,128)(2,1)} %bitcast.31), custom_call_target="tpu_custom_call" | custom-call | tf_op jit(solution)/shard_map/join_columns/pallas_call | solution.py:779
  406.0 1.6 copy.32
  407.5 0.0 copy-done.3
  407.5 0.6 slice_bitcast_fusion
  408.1 0.5 slice.24
  408.6 0.0 copy-start.1
  408.6 2.2 copy.38
  410.8 0.0 copy-done.2
  410.8 1.1 copy.39
  412.0 0.0 copy-done.1
  (4 shorter events, 0.1 us)
Async XLA Ops:
  0.6 123.1 %copy-start = (bf16[512,1536]{1,0:T(8,128)(2,1)S(1)}, bf16[512,1536]{1,0:T(8,128)(2,1)}, u32[]{:S(2)}) copy-start(bf16[512,1536]{1,0:T(8,128)(2,1)} %param.28) | copy-start | bytes 4718596
  0.7 5.7 %copy-start.4 = (f32[1536]{0:T(1024)S(1)}, f32[1536]{0:T(1024)}, u32[]{:S(2)}) copy-start(f32[1536]{0:T(1024)} %param.17) | copy-start | bytes 18436
  7.5 117.1 %copy-start.5 = (f32[1536]{0:T(1024)S(1)}, f32[1536]{0:T(1024)}, u32[]{:S(2)}) copy-start(f32[1536]{0:T(1024)} %param.25) | copy-start | bytes 18436
  368.9 7.0 %copy-start.7 = (f32[1,1536]{1,0:T(1,128)S(1)}, f32[1,1536]{1,0:T(1,128)}, u32[]{:S(2)}) copy-start(f32[1,1536]{1,0:T(1,128)} %get-tuple-element.103) | copy-start | bytes 18436
  369.0 7.0 %copy-start.8 = (f32[8,128]{1,0:T(8,128)S(1)}, f32[8,128]{1,0:T(8,128)}, u32[]{:S(2)}) copy-start(f32[8,128]{1,0:T(8,128)} %get-tuple-element.105) | copy-start | bytes 12292
  369.0 7.4 %copy-start.6 = (f32[1,1536]{1,0:T(1,128)S(1)}, f32[1,1536]{1,0:T(1,128)}, u32[]{:S(2)}) copy-start(f32[1,1536]{1,0:T(1,128)} %get-tuple-element.104) | copy-start | bytes 18436
  401.5 6.0 %copy-start.3 = (f32[32,128]{1,0:T(8,128)S(1)}, f32[32,128]{1,0:T(8,128)}, u32[]{:S(2)}) copy-start(f32[32,128]{1,0:T(8,128)} %get-tuple-element.106) | copy-start | bytes 49156
  401.5 9.3 %copy-start.2 = (f32[256,1536]{1,0:T(8,128)S(1)}, f32[256,1536]{1,0:T(8,128)}, u32[]{:S(2)}) copy-start(f32[256,1536]{1,0:T(8,128)} %get-tuple-element.101) | copy-start | bytes 4718596
  408.6 3.3 copy-start.1

commit v2 on v1

--- a/solution.py
+++ b/solution.py
@@ -724,66 +724,57 @@
     )(*values, small)
 
 
-def join_units(every_gate, every_up, down, out, part):
-    groups, rows, units = every_gate.shape
+def join_shares(every, gate, every_gate, every_up, down, out, columns, starts, forget_at, heads, part):
+    groups, rows, lanes = every.shape
+    units = every_gate.shape[2]
+    own = heads // groups
     steps = 4
     tall = rows // steps
 
-    def body(gate_in, up_in, down_in, out_in, gate_ref, up_ref, down_ref, out_ref):
-        for every, to_ref in ((gate_in, gate_ref), (up_in, up_ref)):
-            for group in range(groups):
+    def body(every_ref, gate_ref, wide_gate, wide_up, down_in, out_in, *outs):
+        firsts = len(starts)
+        for group in range(groups):
+            to = slice(group * columns, (group + 1) * columns)
+            for start, result in zip(starts, outs):
+                result[:, to] = every_ref[group, :, start : start + columns].astype(jnp.float32)
+            outs[firsts][:, to] = gate_ref[group].astype(jnp.float32)
+            outs[firsts + 1][:, group * own : (group + 1) * own] = every_ref[
+                group, :, forget_at : forget_at + own
+            ].astype(jnp.float32)
+            for source, result in ((wide_gate, outs[firsts + 2]), (wide_up, outs[firsts + 3])):
                 for block in range(units // part):
-                    to = (block * groups + group) * part
-                    to_ref[:, to : to + part] = every[group, :, block * part : (block + 1) * part].astype(
+                    at = (block * groups + group) * part
+                    result[:, at : at + part] = source[group, :, block * part : (block + 1) * part].astype(
                         jnp.float32
                     )
-        down_ref[...] = down_in[...].astype(jnp.float32)
-        out_ref[...] = out_in[...].astype(jnp.float32)
+        outs[firsts + 4][...] = down_in[...].astype(jnp.float32)
+        outs[firsts + 5][...] = out_in[...].astype(jnp.float32)
 
     def flat(value):
         return pl.BlockSpec((value.shape[0] // steps, value.shape[1]), lambda i: (i, 0))
 
-    wide = jax.ShapeDtypeStruct((rows, groups * units), jnp.float32)
-    results = [wide, wide, *(jax.ShapeDtypeStruct(v.shape, jnp.float32) for v in (down, out))]
+    def ranks(value):
+        return pl.BlockSpec((groups, tall, value.shape[2]), lambda i: (0, i, 0))
+
+    def shape(size):
+        return jax.ShapeDtypeStruct(size, jnp.float32)
+
+    results = [shape((rows, groups * columns))] * (len(starts) + 1) + [
+        shape((rows, heads)),
+        shape((rows, groups * units)),
+        shape((rows, groups * units)),
+        shape(down.shape),
+        shape(out.shape),
+    ]
     return pl.pallas_call(
         body,
         grid=(steps,),
-        in_specs=[pl.BlockSpec((groups, tall, units), lambda i: (0, i, 0))] * 2 + [flat(down), flat(out)],
+        in_specs=[ranks(v) for v in (every, gate, every_gate, every_up)] + [flat(down), flat(out)],
         out_specs=[flat(value) for value in results],
         out_shape=results,
-        name="join_units",
-    )(every_gate, every_up, down, out)
-
-
-def join_columns(every, gate, columns, starts, forget_at, heads):
-    groups, rows, lanes = every.shape
-    own = heads // groups
-    steps = 4
-    tall = rows // steps
-
-    def body(every_ref, gate_ref, *outs):
-        for group in range(groups):
-            to = slice(group * columns, (group + 1) * columns)
-            for start, out in zip(starts, outs):
-                out[:, to] = every_ref[group, :, start : start + columns].astype(jnp.float32)
-            outs[-2][:, to] = gate_ref[group].astype(jnp.float32)
-            outs[-1][:, group * own : (group + 1) * own] = every_ref[
-                group, :, forget_at : forget_at + own
-            ].astype(jnp.float32)
-
-    def flat(value):
-        return pl.BlockSpec((tall, value.shape[1]), lambda i: (i, 0))
-
-    wide = jax.ShapeDtypeStruct((rows, groups * columns), jnp.float32)
-    results = [wide] * (len(starts) + 1) + [jax.ShapeDtypeStruct((rows, heads), jnp.float32)]
-    return pl.pallas_call(
-        body,
-        grid=(steps,),
-        in_specs=[pl.BlockSpec((groups, tall, v.shape[2]), lambda i: (0, i, 0)) for v in (every, gate)],
-        out_specs=[flat(value) for value in results],
-        out_shape=results,
-        name="join_columns",
-    )(every, gate)
+        compiler_params=pltpu.CompilerParams(vmem_limit_bytes=56 << 20),
+        name="join_shares",
+    )(every, gate, every_gate, every_up, down, out)
 
 
 def norm_rows(values, gain):
@@ -811,13 +802,15 @@
              gate_ref, up_ref,
              normed_hbm, cot_full, full_front_hbm, full_gate_hbm, full_out_hbm, full_ffn, joined_hbm, attended_hbm,
              offset, col, logit, gate_pre_hbm, gated_hbm, middle, own_up,
-             own_normed, own_front, own_gate, own_ffn, own_out, parts_out, row, picks, cot_send, cot_recv, keep,
+             own_normed, own_front, own_gate, own_ffn, own_out, parts_out, own_cot, row, picks, cot_send, cot_recv, keep,
              x_send, x_recv, normed, full_front, full_gate, full_out, joined, attended, gate_pre, gated, store_sems,
              *scratch):
         store = Streams(store_sems)
         me, side, down, across = sides()
         line_chips, chip, core, forth, back, twin = line()
-        front_line = LineGather(own_front, full_front, *scratch[0:3])
+        halves = (pl.ds(0, 2 * columns), pl.ds(2 * columns, front - 2 * columns))
+        first_line = LineGather(own_front.at[:, halves[0]], full_front.at[:, halves[0]], *scratch[0:3])
+        second_line = LineGather(own_front.at[:, halves[1]], full_front.at[:, halves[1]], *scratch[22:25])
         gate_line = LineGather(own_gate, full_gate, *scratch[3:6])
         ffn_line = LineGather(own_ffn, full_ffn, *scratch[6:9])
         out_line = LineGather(own_out, parts_out, *scratch[9:12])
@@ -842,54 +835,70 @@
         values = inputs_ref[...].astype(jnp.float32)
         own_normed[...] = norm_rows(values, gain_ref[...])[1].astype(low)
         own_front[:, 3 * columns :] = forget_ref[...]
+        positions = me * rows + lax.broadcasted_iota(jnp.int32, (rows, depth), 0)
+        own_cot[...] = jnp.where(positions < length_ref[:, :1], cot_ref[...], jnp.zeros((), low))
         meet(*exchange.others, forth, back, twin)
         one = SquareGather(own_normed, normed, x_send, x_recv)
-        two = SquareGather(cot_ref, cot_full, cot_send, cot_recv)
+        two = SquareGather(own_cot, cot_full, cot_send, cot_recv)
         one.start()
         for copy in taken:
             copy.wait()
-        front_line.start()
+        first_line.start()
+        second_line.start()
         at_me = pl.ds(pl.multiple_of(me * rows, rows), rows)
-        kept = pltpu.make_async_copy(cot_ref, cot_full.at[at_me], keep.at[0])
+        kept = pltpu.make_async_copy(own_cot, cot_full.at[at_me], keep.at[0])
         kept.start()
         normed[at_me, :] = own_normed[...]
         one.relay()
         two.start()
-        front_line.step(1)
-        front_line.step(2)
+        first_line.step(1)
+        second_line.step(1)
+        first_line.step(2)
+        second_line.step(2)
         one.near()
         one.far()
-        front_line.step(3)
+        first_line.step(3)
+        second_line.step(3)
         store.start(normed, normed_hbm)
-        front_line.finish()
-        store.start(full_front, full_front_hbm)
-        one.finish()
         out_line.start()
         gate_line.start()
         two.relay()
-
-        def store_joined(at_columns, value):
-            joined[:, at_columns] = value.astype(low)
-
-        block_product(normed, full_front, False, 256, store_joined)
+        first_line.finish()
+
+        def product_of(columns_of_front):
+            view = joined.at[:, columns_of_front]
+
+            def store_joined(at_columns, value):
+                view[:, at_columns] = value.astype(low)
+
+            block_product(normed, full_front.at[:, columns_of_front], False, 256, store_joined)
+
+        product_of(halves[0])
+        second_line.finish()
+        product_of(halves[1])
+        store.start(full_front, full_front_hbm)
+        one.finish()
         store.start(joined, joined_hbm)
         work = Forward(joined, bias_ref, length_ref, attended, offset, col, logit, row, head_size, scale)
         offset[...] = jnp.zeros_like(offset)
         out_line.step(1)
         gate_line.step(1)
         work.start()
-        out_line.step(2)
-        gate_line.step(2)
 
         def step(pair, carry):
             work.pair(pair)
 
             @pl.when(pair == 0)
             def _():
+                out_line.step(2)
+                gate_line.step(2)
+
+            @pl.when(pair == 1)
+            def _():
                 out_line.step(3)
-                gate_line.step(3)
                 out_line.finish()
                 exchange.start()
+                gate_line.step(3)
                 ffn_line.start()
 
             return carry
@@ -898,20 +907,20 @@
         store.start(attended, attended_hbm)
         gate_line.finish()
         store.start(full_gate, full_gate_hbm)
-        exchange.relay()
 
         def store_gate(at_columns, value):
             gate_pre[:, at_columns] = value
 
         block_product(normed, full_gate, False, PAIR, store_gate)
         gated[...] = (attended[...].astype(jnp.float32) * jax.nn.sigmoid(gate_pre[...])).astype(low)
+        exchange.relay()
         store.start(gate_pre, gate_pre_hbm)
         store.start(gated, gated_hbm)
         exchange.end()
         store.start(full_out, full_out_hbm)
         job.begin()
+        ffn_line.step(1)
         job.relay()
-        ffn_line.step(1)
         job.own()
         two.near()
         two.far()
@@ -957,6 +966,7 @@
             pltpu.VMEM((mine, early), low),
             pltpu.VMEM((block.shape[0] // 4, depth), low),
             pltpu.VMEM((shards * block.shape[0] // 4, depth), low),
+            pltpu.VMEM((rows, depth), low),
             pltpu.VMEM((Forward.some, slots), jnp.float32),
             dma((5 + 2 * shards,)),
             dma((6,)),
@@ -969,7 +979,8 @@
         ]
         + 4 * LineGather.scratch(chips)
         + PartExchange.scratch()
-        + SquareScatter.scratch(rows, depth),
+        + SquareScatter.scratch(rows, depth)
+        + LineGather.scratch(chips),
         compiler_params=pltpu.CompilerParams(
             collective_id=collective_id, has_side_effects=True, vmem_limit_bytes=VMEM_LIMIT
         ),
@@ -1132,6 +1143,7 @@
              grads_ref, weights_ref, up_weights_ref, normed_ref, down_ref, out_ref, middle_ref, cot_ref,
              attended_ref, pre_ref, grad_middle, branch, terms_up, fetch_sems, store_sems, *scratch):
         fetch, store = Streams(fetch_sems), Streams(store_sems)
+        own_rows = pl.ds(pl.multiple_of(lax.axis_index("seq") * rows, rows), rows)
         first_in = [
             fetch.start(*both)
             for both in (
@@ -1146,7 +1158,7 @@
             fetch.start(*both)
             for both in (
                 (middle_hbm, middle_ref),
-                (cot_hbm, cot_ref),
+                (cot_hbm.at[own_rows], cot_ref),
                 (out_hbm, out_ref),
                 (attended_hbm, attended_ref),
                 (pre_hbm, pre_ref),
@@ -1229,7 +1241,8 @@
     vmem = pl.BlockSpec(memory_space=pltpu.VMEM)
     anywhere = pl.BlockSpec(memory_space=pl.ANY)
     dma = pltpu.SemaphoreType.DMA
-    fetched = (grads, weights, up_weights, normed, terms_down, w_out, middle, cotangent, attended, gate_pre)
+    own_shape = jax.ShapeDtypeStruct((rows, depth), low)
+    fetched = (grads, weights, up_weights, normed, terms_down, w_out, middle, own_shape, attended, gate_pre)
     return pl.pallas_call(
         body,
         in_specs=[anywhere] * 7 + [vmem] + [anywhere] * 3,
@@ -1487,7 +1500,7 @@
     shards = 2 * lax.axis_size("seq")
     chips = shards // 2
     rows_up = terms_up.shape[0] // shards
-    fetched = (terms_up, gated, grad_branch, normed, d_pre, hidden, w_down, joined, d_out, middle)
+    fetched = (terms_up, hidden, w_down, gated, grad_branch, normed, d_pre, joined, d_out, middle)
 
     def body(*refs):
         sources, refs = refs[:10], refs[10:]
@@ -1495,7 +1508,7 @@
         (grads, bias_grad, layer_output, collected, share_up, share_pre, *every_refs), refs = refs[:8], refs[8:]
         buffers, refs = refs[:10], refs[10:]
         terms, terms_pre, lowered, send, recv, keep, fetch_sems, *scratch = refs
-        up_ref, gated_ref, branch_ref, normed_ref, pre_ref, hidden_ref, down_ref, joined_ref, d_out_ref = buffers[:9]
+        up_ref, hidden_ref, down_ref, gated_ref, branch_ref, normed_ref, pre_ref, joined_ref, d_out_ref = buffers[:9]
         fetch = Streams(fetch_sems)
         comes = [fetch.start(source, buffer) for source, buffer in zip(sources, buffers)]
         me, side, down, across = sides()
@@ -1525,17 +1538,19 @@
             kept[i].start()
         comes[1].wait()
         comes[2].wait()
-        transposed_product(gated_ref, branch_ref, terms)
-        collect.start()
+        job.begin()
         run.slot(0)
         comes[3].wait()
         comes[4].wait()
+        transposed_product(gated_ref, branch_ref, terms)
+        collect.start()
+        comes[5].wait()
+        comes[6].wait()
         transposed_product(normed_ref, pre_ref, terms_pre)
         run_pre.start()
         collect.slot(0)
-        for copy in comes[5:]:
+        for copy in comes[7:]:
             copy.wait()
-        job.begin()
         run_pre.slot(0)
         work.start()
 
@@ -1786,7 +1801,7 @@
             normed_attn, cotangent_all, full_front, full_ogate, full_out, full_ffn,
             joined, attended_low, offset, col, logit, gate_pre, gated, middle, mine_up,
         ) = whole_forward(
-            layer_input[0], norm_attn[None], cotangent_low, (w_query, w_key, w_value, w_ogate), own_forget,
+            layer_input[0], norm_attn[None], output_grad[0], (w_query, w_key, w_value, w_ogate), own_forget,
             own_bias, length_row, w_out, w_gate, w_up, head_size, scale, 0,
         )
         full_out = full_out.reshape(columns, width)
@@ -1797,7 +1812,7 @@
             grad_middle, grad_norm_ffn, grad_branch, grad_attended, grad_gate_pre, terms_up, share_down, share_gate,
         ) = feed_backward(
             grad_gate_up, full_ffn, full_up, normed_ffn, terms_down, full_out, middle, norm_ffn[None],
-            cotangent_low, attended_low, gate_pre, 2,
+            cotangent_all, attended_low, gate_pre, 2,
         )
         grad_norm_ffn = grad_norm_ffn[0]
         grads, bias_rows, layer_output, collected, share_up, share_ogate, grad_down, every_gate = middle_backward(
@@ -1886,13 +1901,18 @@
         small = lax.psum((grad_norm_attn, grad_norm_ffn, grad_bias), ("seq", "wshard"))
     every_attn = every_attn.reshape((groups,) + share_attn.shape)
     if fast:
-        grad_w_gate, grad_w_up, grad_down, grad_out = join_units(
-            every_gate.reshape((groups,) + share_gate.shape), every_up.reshape((groups,) + share_up.shape),
-            grad_down, grad_out, part,
-        )
-        every_ogate = every_ogate.reshape((groups,) + share_ogate.shape)
-        *weight_grads, grad_forget_w = join_columns(
-            every_attn, every_ogate, columns, (0, lanes, 2 * lanes), 3 * lanes, heads
+        *weight_grads, grad_forget_w, grad_w_gate, grad_w_up, grad_down, grad_out = join_shares(
+            every_attn,
+            every_ogate.reshape((groups,) + share_ogate.shape),
+            every_gate.reshape((groups,) + share_gate.shape),
+            every_up.reshape((groups,) + share_up.shape),
+            grad_down,
+            grad_out,
+            columns,
+            (0, lanes, 2 * lanes),
+            3 * lanes,
+            heads,
+            part,
         )
     else:
 

time: 413 us -> 400 us (0.969)
  Pallas kernels: 396 us -> 384 us
    pallas_call x1, Pallas kernels: 116 us -> 107 us  [whole_forward(): pl.pallas_call(body, in_specs=[vmem] * 3 + [anywhere] * 4 + [vmem] * 3 +...]
    pallas_call x2 -> x1, Pallas kernels: 11.4 us -> 8.78 us  [join_shares(): pl.pallas_call(body, grid=(steps,), in_specs=[ranks(v) for v in (every, g...]
where the time goes in v2:
time: 400 us; the launch traced here: 399 us
  Pallas kernels  384 us (96%)
  local copies, waits for them, and re-layouts  12.6 us (3%)
    pallas_call x1, Pallas kernels, whole_forward(): pl.pallas_call(body, in_specs=[vmem] * 3 + [anywhere] * 4 + [vmem] * 3 +...  107 us
    pallas_call x1, Pallas kernels, feed_backward(): pl.pallas_call(body, in_specs=[anywhere] * 7 + [vmem] + [anywhere] * 3, o...  71.2 us
    pallas_call x1, Pallas kernels, middle_backward(): pl.pallas_call(body, in_specs=[anywhere] * 10 + [vmem] * 5, out_specs=[vm...  58.9 us
    pallas_call x1, Pallas kernels, last_backward(): pl.pallas_call(body, in_specs=[anywhere] * 7 + [vmem] * 4, out_specs=[vme...  58.2 us
    pallas_call x1, Pallas kernels, feed_forward(): pl.pallas_call(body, in_specs=[vmem, vmem, anywhere, vmem, vmem, anywhere...  56.6 us
    pallas_call x1, Pallas kernels, last_gather(): pl.pallas_call(body, in_specs=[vmem] * (count + 1), out_specs=[pl.BlockSp...  23.5 us
    pallas_call x1, Pallas kernels, join_shares(): pl.pallas_call(body, grid=(steps,), in_specs=[ranks(v) for v in (every, g...  8.78 us

profile of v2, /device:TPU:0, one launch (start us, length us, event | category | flops | bytes accessed | tf_op | source)
XLA Modules:
  0.0 399.2 jit_solution(12489573345727163077)
XLA Ops:
  0.6 0.0 copy-start
  0.7 0.8 constant_dynamic-slice_fusion.1
  1.5 0.1 copy.33
  1.6 0.6 pad.12.forget_ref
  2.3 0.7 dynamic_slice.10
  3.0 0.5 pad_bitcast_fusion.bias_ref
  3.5 1.3 broadcast_in_dim.25.gain_ref.refs_8_
  5.5 0.5 broadcast_in_dim.28.length_ref
  6.0 0.0 copy-start.4
  6.0 106.7 %whole_forward.1 = (bf16[1024,1536]{1,0:T(8,128)(2,1)}, bf16[1024,1536]{1,0:T(8,128)(2,1)}, bf16[1536,1280]{1,0:T(8,128)(2,1)}, bf16[1536,384]{1,0:T(8,128)(2,1)...) custom-call(bf16[256,1536]{1,0:T(8,128)(2,1)} %bitcast.21, ...), custom_call_target="tpu_custom_call" | custom-call | tf_op jit(solution)/shard_map/whole_forward/pallas_call | solution.py:957
  112.7 0.0 copy-done
  112.8 0.8 constant_dynamic-slice_fusion.down_ref
  113.5 0.0 copy-done.4
  113.5 0.6 broadcast_in_dim.29.gain_ref
  114.1 56.6 %feed_forward.1 = (bf16[1024,1536]{1,0:T(8,128)(2,1)}, bf16[1024,1024]{1,0:T(8,128)(2,1)}, bf16[1536,512]{1,0:T(8,128)(2,1)}, bf16[1024,1536]{1,0:T(8,128)(2,1)}...) custom-call(f32[256,1536]{1,0:T(8,128)} %get-tuple-element.68.middle_ref.middle_hbm.refs_9_, ...), custom_call_target="tpu_custom_call" | custom-call | tf_op jit(solution)/shard_map/feed_forward/pallas_call | solution.py:1106
  170.7 71.2 %feed_backward.1 = (f32[256,1536]{1,0:T(8,128)}, f32[1,1536]{1,0:T(1,128)}, bf16[1024,1536]{1,0:T(8,128)(2,1)}, bf16[1024,384]{1,0:T(8,128)(2,1)}, bf16[1024,384...) custom-call(bf16[1024,2048]{1,0:T(8,128)(2,1)} %get-tuple-element.72.grads_hbm, ...), custom_call_target="tpu_custom_call" | custom-call | tf_op jit(solution)/shard_map/feed_backward/pallas_call | solution.py:1246
  241.9 58.9 %middle_backward.1 = (bf16[1024,1280]{1,0:T(8,128)(2,1)}, f32[8,128]{1,0:T(8,128)}, bf16[256,1536]{1,0:T(8,128)(2,1)}, bf16[48,1536]{1,0:T(8,128)(2,1)}, bf16[19...) custom-call(bf16[1536,1024]{1,0:T(8,128)(2,1)} %get-tuple-element.79.refs_, ...), custom_call_target="tpu_custom_call" | custom-call | tf_op jit(solution)/shard_map/middle_backward/pallas_call | solution.py:1596
  300.8 0.0 copy-start.6
  300.8 0.0 copy-start.5
  300.8 58.2 %last_backward.1 = (f32[256,1536]{1,0:T(8,128)}, f32[1,1536]{1,0:T(1,128)}, bf16[192,1280]{1,0:T(8,128)(2,1)}, bf16[4,48,1536]{2,1,0:T(8,128)(2,1)}, bf16[768,38...) custom-call(bf16[1024,1536]{1,0:T(8,128)(2,1)} %get-tuple-element.84.refs_5_.refs_0_, ...), custom_call_target="tpu_custom_call" | custom-call | tf_op jit(solution)/shard_map/last_backward/pallas_call | solution.py:1703
  359.1 0.7 reduce
  359.8 0.0 copy-done.6
  359.8 0.1 slice_reduce_fusion
  359.9 0.2 dynamic_update_slice.3
  360.2 0.0 copy-done.5
  360.2 0.6 fusion.refs_1_
  360.8 23.5 %last_gather.1 = (bf16[768,1280]{1,0:T(8,128)(2,1)}, f32[32,128]{1,0:T(8,128)}) custom-call(bf16[192,1280]{1,0:T(8,128)(2,1)} %get-tuple-element.102.refs_0_, f32[32,128]{1,0:T(8,128)} %fusion.refs_1_), custom_call_target="tpu_custom_call" | custom-call | tf_op jit(solution)/shard_map/last_gather/pallas_call | solution.py:704
  384.3 0.0 copy-start.3
  384.3 8.8 %join_shares.1 = (f32[192,1536]{1,0:T(8,128)}, f32[192,1536]{1,0:T(8,128)}, f32[192,1536]{1,0:T(8,128)}, f32[192,1536]{1,0:T(8,128)}, f32[192,24]{1,0:T(8,128)},...) custom-call(bf16[4,192,1280]{2,1,0:T(8,128)(2,1)} %bitcast.23, ...), custom_call_target="tpu_custom_call" | custom-call | tf_op jit(solution)/shard_map/join_shares/pallas_call | solution.py:769
  393.1 0.0 copy-start.2
  393.1 1.7 copy.32
  394.8 0.0 copy-done.3
  394.8 0.6 slice_bitcast_fusion
  395.4 0.5 slice.24
  395.9 0.0 copy-start.1
  395.9 2.2 copy.38
  398.1 0.0 copy-done.2
  398.1 1.1 copy.39
  399.2 0.0 copy-done.1
  (2 shorter events, 0.0 us)
Async XLA Ops:
  0.6 112.1 %copy-start = (bf16[512,1536]{1,0:T(8,128)(2,1)S(1)}, bf16[512,1536]{1,0:T(8,128)(2,1)}, u32[]{:S(2)}) copy-start(bf16[512,1536]{1,0:T(8,128)(2,1)} %param.28) | copy-start | bytes 4718596
  6.0 107.6 %copy-start.4 = (f32[1536]{0:T(1024)S(1)}, f32[1536]{0:T(1024)}, u32[]{:S(2)}) copy-start(f32[1536]{0:T(1024)} %param.25) | copy-start | bytes 18436
  300.8 59.0 %copy-start.6 = (f32[8,128]{1,0:T(8,128)S(1)}, f32[8,128]{1,0:T(8,128)}, u32[]{:S(2)}) copy-start(f32[8,128]{1,0:T(8,128)} %get-tuple-element.105) | copy-start | bytes 12292
  300.8 59.4 %copy-start.5 = (f32[1,1536]{1,0:T(1,128)S(1)}, f32[1,1536]{1,0:T(1,128)}, u32[]{:S(2)}) copy-start(f32[1,1536]{1,0:T(1,128)} %get-tuple-element.104) | copy-start | bytes 18436
  384.3 10.5 %copy-start.3 = (f32[32,128]{1,0:T(8,128)S(1)}, f32[32,128]{1,0:T(8,128)}, u32[]{:S(2)}) copy-start(f32[32,128]{1,0:T(8,128)} %get-tuple-element.106) | copy-start | bytes 49156
  393.1 5.0 %copy-start.2 = (f32[256,1536]{1,0:T(8,128)S(1)}, f32[256,1536]{1,0:T(8,128)}, u32[]{:S(2)}) copy-start(f32[256,1536]{1,0:T(8,128)} %get-tuple-element.101) | copy-start | bytes 4718596
  395.9 3.3 copy-start.1

commit v3 on v2

--- a/solution.py
+++ b/solution.py
@@ -1020,8 +1020,9 @@
         own_normed[...] = norm_rows(middle_ref[...], gain_ref[...])[1].astype(low)
         meet({"seq": side}, {"seq": down}, forth, back, twin)
         job = SquareGather(own_normed, normed, send, recv)
+        up_line.start()
+        down_line.start()
         job.start()
-        up_line.start()
 
         def rows_of(rank):
             return pl.ds(pl.multiple_of(rank * rows, rows), rows)
@@ -1039,16 +1040,17 @@
         multiply(me)
         up_line.step(1)
         job.relay()
+        down_line.step(1)
         up_line.step(2)
-        down_line.start()
-        up_line.step(3)
         job.near()
         multiply(side)
+        up_line.step(3)
         multiply(down)
         job.far()
-        down_line.step(1)
         store.start(normed, normed_hbm)
+        down_line.step(2)
         multiply(across)
+        job.finish()
         up_line.finish()
         store.start(full_up, full_up_hbm)
 
@@ -1060,13 +1062,11 @@
             return carry
 
         lax.fori_loop(0, 4, ahead, 0)
-        down_line.step(2)
-        job.finish()
         store.start(hidden, hidden_hbm)
+        down_line.step(3)
         cot_in.wait()
         transposed_product(hidden, cot_ref, terms)
         store.start(terms, terms_hbm)
-        down_line.step(3)
         down_line.finish()
         store.start(full_down, full_down_hbm)
 
@@ -1147,10 +1147,10 @@
         first_in = [
             fetch.start(*both)
             for both in (
+                (down_hbm, down_ref),
                 (grads_hbm, grads_ref),
                 (weights_hbm, weights_ref),
                 (up_weights_hbm, up_weights_ref),
-                (down_hbm, down_ref),
             )
         ]
         normed_in = fetch.start(normed_hbm, normed_ref)
@@ -1178,21 +1178,23 @@
         run_down = LineScatter(down_ref, share_down, *scratch[7:12])
         run_gate = LineScatter(terms_gate, share_gate, *scratch[12:])
         every = SquareGather(own_branch, branch, send, recv)
-        for copy in first_in:
+        first_in[0].wait()
+        run_down.start()
+        for copy in first_in[1:]:
             copy.wait()
-        run_down.start()
-        job.begin()
+        job.begin_far()
         run_down.slot(0)
+        job.begin_near()
         normed_in.wait()
         transposed_product(normed_ref, first, terms_gate)
         run_gate.start()
         job.relay()
         run_down.slot(1)
+        run_gate.slot(0)
         job.own()
         transposed_product(normed_ref, second, terms_up)
         store.start(terms_up, terms_up_hbm)
         run_down.slot(2)
-        run_gate.slot(0)
         for copy in rest_in:
             copy.wait()
         job.end()
@@ -1340,11 +1342,23 @@
         lax.fori_loop(0, self.width // self.tile, step, 0)
 
     def begin(self):
+        self.begin_far()
+        self.begin_near()
+
+    def begin_far(self):
         me, side, down, across = sides()
-        half, far, near, kept = self.half, self.far, self.near, self.kept
+        far = self.far
 
         def store_far(columns, value):
             far[:, columns] = value.astype(far.dtype)
+
+        self.partial(across, store_far)
+        self.copy(0).start()
+        self.copy(1).start()
+
+    def begin_near(self):
+        me, side, down, across = sides()
+        half, near, kept = self.half, self.near, self.kept
 
         def store_side(columns, value):
             kept[0, :, columns] = value[:half]
@@ -1354,9 +1368,6 @@
             near[1, :, columns] = value[:half].astype(near.dtype)
             kept[1, :, columns] = value[half:]
 
-        self.partial(across, store_far)
-        self.copy(0).start()
-        self.copy(1).start()
         self.partial(side, store_side)
         self.copy(2).start()
         self.partial(down, store_down)

time: 400 us -> 392 us (0.980)
  Pallas kernels: 384 us -> 377 us
    pallas_call x1, Pallas kernels: 71.2 us -> 65.5 us  [feed_backward(): pl.pallas_call(body, in_specs=[anywhere] * 7 + [vmem] + [anywhere] * 3, o...]
where the time goes in v3:
time: 392 us
  Pallas kernels  377 us (96%)
  local copies, waits for them, and re-layouts  12.6 us (3%)
    pallas_call x1, Pallas kernels, whole_forward(): pl.pallas_call(body, in_specs=[vmem] * 3 + [anywhere] * 4 + [vmem] * 3 +...  107 us
    pallas_call x1, Pallas kernels, feed_backward(): pl.pallas_call(body, in_specs=[anywhere] * 7 + [vmem] + [anywhere] * 3, o...  65.5 us
    pallas_call x1, Pallas kernels, middle_backward(): pl.pallas_call(body, in_specs=[anywhere] * 10 + [vmem] * 5, out_specs=[vm...  59.4 us
    pallas_call x1, Pallas kernels, last_backward(): pl.pallas_call(body, in_specs=[anywhere] * 7 + [vmem] * 4, out_specs=[vme...  58.6 us
    pallas_call x1, Pallas kernels, feed_forward(): pl.pallas_call(body, in_specs=[vmem, vmem, anywhere, vmem, vmem, anywhere...  53.6 us
    pallas_call x1, Pallas kernels, last_gather(): pl.pallas_call(body, in_specs=[vmem] * (count + 1), out_specs=[pl.BlockSp...  23.8 us
    pallas_call x1, Pallas kernels, join_shares(): pl.pallas_call(body, grid=(steps,), in_specs=[ranks(v) for v in (every, g...  8.78 us

profile of v3, /device:TPU:0, one launch (start us, length us, event | category | flops | bytes accessed | tf_op | source)
XLA Modules:
  0.0 391.9 jit_solution(17394327832606583945)
XLA Ops:
  0.6 0.0 copy-start
  0.7 0.8 constant_dynamic-slice_fusion.1
  1.5 0.1 copy.33
  1.6 0.6 pad.12.forget_ref
  2.3 0.7 dynamic_slice.10
  3.0 0.5 pad_bitcast_fusion.bias_ref
  3.5 1.3 broadcast_in_dim.25.gain_ref.refs_8_
  5.5 0.5 broadcast_in_dim.28.length_ref
  6.0 0.0 copy-start.4
  6.0 106.7 %whole_forward.1 = (bf16[1024,1536]{1,0:T(8,128)(2,1)}, bf16[1024,1536]{1,0:T(8,128)(2,1)}, bf16[1536,1280]{1,0:T(8,128)(2,1)}, bf16[1536,384]{1,0:T(8,128)(2,1)...) custom-call(bf16[256,1536]{1,0:T(8,128)(2,1)} %bitcast.21, ...), custom_call_target="tpu_custom_call" | custom-call | tf_op jit(solution)/shard_map/whole_forward/pallas_call | solution.py:957
  112.7 0.0 copy-done
  112.8 0.8 constant_dynamic-slice_fusion.down_ref
  113.5 0.0 copy-done.4
  113.5 0.6 broadcast_in_dim.29.gain_ref
  114.1 53.6 %feed_forward.1 = (bf16[1024,1536]{1,0:T(8,128)(2,1)}, bf16[1024,1024]{1,0:T(8,128)(2,1)}, bf16[1536,512]{1,0:T(8,128)(2,1)}, bf16[1024,1536]{1,0:T(8,128)(2,1)}...) custom-call(f32[256,1536]{1,0:T(8,128)} %get-tuple-element.68.middle_ref.middle_hbm.refs_9_, ...), custom_call_target="tpu_custom_call" | custom-call | tf_op jit(solution)/shard_map/feed_forward/pallas_call | solution.py:1106
  167.8 65.5 %feed_backward.1 = (f32[256,1536]{1,0:T(8,128)}, f32[1,1536]{1,0:T(1,128)}, bf16[1024,1536]{1,0:T(8,128)(2,1)}, bf16[1024,384]{1,0:T(8,128)(2,1)}, bf16[1024,384...) custom-call(bf16[1024,2048]{1,0:T(8,128)(2,1)} %get-tuple-element.72.grads_hbm, ...), custom_call_target="tpu_custom_call" | custom-call | tf_op jit(solution)/shard_map/feed_backward/pallas_call | solution.py:1248
  233.3 59.4 %middle_backward.1 = (bf16[1024,1280]{1,0:T(8,128)(2,1)}, f32[8,128]{1,0:T(8,128)}, bf16[256,1536]{1,0:T(8,128)(2,1)}, bf16[48,1536]{1,0:T(8,128)(2,1)}, bf16[19...) custom-call(bf16[1536,1024]{1,0:T(8,128)(2,1)} %get-tuple-element.79.refs_, ...), custom_call_target="tpu_custom_call" | custom-call | tf_op jit(solution)/shard_map/middle_backward/pallas_call | solution.py:1607
  292.7 0.0 copy-start.6
  292.7 0.0 copy-start.5
  292.8 58.6 %last_backward.1 = (f32[256,1536]{1,0:T(8,128)}, f32[1,1536]{1,0:T(1,128)}, bf16[192,1280]{1,0:T(8,128)(2,1)}, bf16[4,48,1536]{2,1,0:T(8,128)(2,1)}, bf16[768,38...) custom-call(bf16[1024,1536]{1,0:T(8,128)(2,1)} %get-tuple-element.84.refs_5_.refs_0_, ...), custom_call_target="tpu_custom_call" | custom-call | tf_op jit(solution)/shard_map/last_backward/pallas_call | solution.py:1714
  351.4 0.7 reduce
  352.1 0.0 copy-done.6
  352.1 0.1 slice_reduce_fusion
  352.2 0.2 dynamic_update_slice.3
  352.5 0.0 copy-done.5
  352.5 0.6 fusion.refs_1_
  353.1 23.8 %last_gather.1 = (bf16[768,1280]{1,0:T(8,128)(2,1)}, f32[32,128]{1,0:T(8,128)}) custom-call(bf16[192,1280]{1,0:T(8,128)(2,1)} %get-tuple-element.102.refs_0_, f32[32,128]{1,0:T(8,128)} %fusion.refs_1_), custom_call_target="tpu_custom_call" | custom-call | tf_op jit(solution)/shard_map/last_gather/pallas_call | solution.py:704
  376.9 0.0 copy-start.3
  376.9 8.8 %join_shares.1 = (f32[192,1536]{1,0:T(8,128)}, f32[192,1536]{1,0:T(8,128)}, f32[192,1536]{1,0:T(8,128)}, f32[192,1536]{1,0:T(8,128)}, f32[192,24]{1,0:T(8,128)},...) custom-call(bf16[4,192,1280]{2,1,0:T(8,128)(2,1)} %bitcast.23, ...), custom_call_target="tpu_custom_call" | custom-call | tf_op jit(solution)/shard_map/join_shares/pallas_call | solution.py:769
  385.7 0.0 copy-start.2
  385.7 1.7 copy.32
  387.4 0.0 copy-done.3
  387.4 0.6 slice_bitcast_fusion
  388.0 0.5 slice.24
  388.6 0.0 copy-start.1
  388.6 2.2 copy.38
  390.7 0.0 copy-done.2
  390.7 1.1 copy.39
  391.9 0.0 copy-done.1
  (2 shorter events, 0.0 us)
Async XLA Ops:
  0.6 112.1 %copy-start = (bf16[512,1536]{1,0:T(8,128)(2,1)S(1)}, bf16[512,1536]{1,0:T(8,128)(2,1)}, u32[]{:S(2)}) copy-start(bf16[512,1536]{1,0:T(8,128)(2,1)} %param.28) | copy-start | bytes 4718596
  6.0 107.6 %copy-start.4 = (f32[1536]{0:T(1024)S(1)}, f32[1536]{0:T(1024)}, u32[]{:S(2)}) copy-start(f32[1536]{0:T(1024)} %param.25) | copy-start | bytes 18436
  292.7 59.4 %copy-start.6 = (f32[8,128]{1,0:T(8,128)S(1)}, f32[8,128]{1,0:T(8,128)}, u32[]{:S(2)}) copy-start(f32[8,128]{1,0:T(8,128)} %get-tuple-element.105) | copy-start | bytes 12292
  292.7 59.7 %copy-start.5 = (f32[1,1536]{1,0:T(1,128)S(1)}, f32[1,1536]{1,0:T(1,128)}, u32[]{:S(2)}) copy-start(f32[1,1536]{1,0:T(1,128)} %get-tuple-element.104) | copy-start | bytes 18436
  376.9 10.5 %copy-start.3 = (f32[32,128]{1,0:T(8,128)S(1)}, f32[32,128]{1,0:T(8,128)}, u32[]{:S(2)}) copy-start(f32[32,128]{1,0:T(8,128)} %get-tuple-element.106) | copy-start | bytes 49156
  385.7 5.0 %copy-start.2 = (f32[256,1536]{1,0:T(8,128)S(1)}, f32[256,1536]{1,0:T(8,128)}, u32[]{:S(2)}) copy-start(f32[256,1536]{1,0:T(8,128)} %get-tuple-element.101) | copy-start | bytes 4718596
  388.6 3.3 copy-start.1

commit v4 on v3

--- a/solution.py
+++ b/solution.py
@@ -629,6 +629,17 @@
 
 
 class Everywhere:
+    @staticmethod
+    def scratch(shape):
+        dma = pltpu.SemaphoreType.DMA
+        return [
+            pltpu.VMEM((4,) + shape, jnp.float32),
+            pltpu.VMEM(shape, jnp.float32),
+            pltpu.VMEM((8,) + shape, jnp.float32),
+            dma((12,)),
+            dma((12,)),
+        ]
+
     def __init__(self, values, out, ranks, total, places, send, recv):
         self.values, self.out, self.ranks, self.total, self.places = values, out, ranks, total, places
         self.send, self.recv = send, recv
@@ -664,64 +675,6 @@
             copy.wait()
         sums = [self.places[k] + self.places[k + 1] for k in range(0, self.shards, 2)]
         self.out[...] = (sums[0] + sums[1]) + (sums[2] + sums[3])
-
-
-def last_gather(values, small, collective_id):
-    count = len(values)
-    groups = lax.axis_size("seq")
-    shards = 2 * groups
-
-    def body(*refs):
-        own, small_ref = refs[:count], refs[count]
-        full, small_out = refs[count + 1 : 2 * count + 1], refs[2 * count + 1]
-        send, recv, local = refs[2 * count + 2 : 2 * count + 5]
-        me, side, down, across = sides()
-        total = Everywhere(small_ref, small_out, *refs[2 * count + 5 :])
-        meet(*total.others(), *total.along())
-        jobs = [SquareGather(own[i], full[i], send.at[i], recv.at[i]) for i in range(count)]
-        total.start()
-        keeps = []
-        for i, job in enumerate(jobs):
-            job.start()
-            rows = own[i].shape[0]
-            keep = pltpu.make_async_copy(
-                own[i], full[i].at[pl.ds(pl.multiple_of(me * rows, rows), rows)], local.at[i]
-            )
-            keep.start()
-            keeps.append(keep)
-        total.relay()
-        for job in jobs:
-            job.relay()
-        total.end()
-        for job, keep in zip(jobs, keeps):
-            job.near()
-            job.far()
-            job.finish()
-            keep.wait()
-
-    vmem = pl.BlockSpec(memory_space=pltpu.VMEM)
-    dma = pltpu.SemaphoreType.DMA
-    return pl.pallas_call(
-        body,
-        in_specs=[vmem] * (count + 1),
-        out_specs=[pl.BlockSpec(memory_space=pl.ANY)] * count + [vmem],
-        out_shape=[jax.ShapeDtypeStruct((4 * v.shape[0],) + v.shape[1:], v.dtype) for v in values]
-        + [jax.ShapeDtypeStruct(small.shape, jnp.float32)],
-        scratch_shapes=[
-            dma((count, 6)),
-            dma((count, 6)),
-            dma((count,)),
-            pltpu.VMEM((groups,) + small.shape, jnp.float32),
-            pltpu.VMEM(small.shape, jnp.float32),
-            pltpu.VMEM((shards,) + small.shape, jnp.float32),
-            dma((groups + shards,)),
-            dma((groups + shards,)),
-        ],
-        compiler_params=pltpu.CompilerParams(
-            collective_id=collective_id, has_side_effects=True, vmem_limit_bytes=VMEM_LIMIT
-        ),
-        name="last_gather",
-    )(*values, small)
 
 
 def join_shares(every, gate, every_gate, every_up, down, out, columns, starts, forget_at, heads, part):
@@ -1549,8 +1502,9 @@
             kept[i].start()
         comes[1].wait()
         comes[2].wait()
-        job.begin()
+        job.begin_far()
         run.slot(0)
+        job.begin_near()
         comes[3].wait()
         comes[4].wait()
         transposed_product(gated_ref, branch_ref, terms)
@@ -1640,7 +1594,7 @@
 
 
 def last_backward(grads, d_pre, normed, weights, gate_weights, collected, shares, inputs, gain, grad_middle,
-                  collective_id):
+                  small, collective_id):
     slots, depth = normed.shape
     front = grads.shape[1]
     tokens = slots // 4
@@ -1650,21 +1604,27 @@
 
     def body(*refs):
         sources, refs = refs[:7], refs[7:]
-        (collected_ref, gain_ref, *share_refs), refs = refs[:4], refs[4:]
-        (grad_input, grad_gain, share, regrouped, *every_refs), refs = refs[:6], refs[6:]
+        (collected_ref, gain_ref, small_ref, *share_refs), refs = refs[:5], refs[5:]
+        (grad_input, small_out, regrouped, *every_refs), refs = refs[:6], refs[6:]
         buffers, refs = refs[:7], refs[7:]
-        terms, summed, send, recv, keep, fetch_sems, *scratch = refs
+        terms, summed, share, small_own, send, recv, keep, fetch_sems, *scratch = refs
         normed_ref, grads_ref, pre_ref, weights_ref, gate_weights_ref, inputs_ref, middle_ref = buffers
         fetch = Streams(fetch_sems)
         comes = [fetch.start(source, buffer) for source, buffer in zip(sources, buffers)]
         me, side, down, across = sides()
-        regroup = Regroup(collected_ref, regrouped, *scratch[12:])
+        regroup = Regroup(collected_ref, regrouped, *scratch[12:15])
+        total = Everywhere(small_own, small_out, *scratch[20:])
         meet(*regroup.others, *regroup.along)
         job = SquareScatter([grads_ref, pre_ref], [weights_ref, gate_weights_ref], True, summed, *scratch[:7])
-        run = LineScatter(terms, share, *scratch[7:12])
+        halves = (pl.ds(0, front // 2), pl.ds(front // 2, front // 2))
+        runs = [
+            LineScatter(terms.at[:, half], share.at[:, half], *scratch[at : at + 5])
+            for half, at in zip(halves, (7, 15))
+        ]
         regroup.start()
         every = [SquareGather(share_refs[i], every_refs[i], send.at[i], recv.at[i]) for i in range(2)]
         every[0].start()
+        every[1].start()
         kept = []
         for i in range(2):
             size = share_refs[i].shape[0]
@@ -1678,34 +1638,53 @@
             kept[i].start()
         comes[0].wait()
         comes[1].wait()
-        transposed_product(normed_ref, grads_ref, terms)
-        run.start()
-        every[0].relay()
-        regroup.relay()
-        run.slot(0)
+        for half, run in zip(halves, runs):
+            transposed_product(normed_ref, grads_ref.at[:, half], terms.at[:, half])
+            run.start()
+        runs[0].slot(0)
         for copy in comes[2:]:
             copy.wait()
-        job.begin()
-        every[1].start()
+        job.begin_far()
+        runs[1].slot(0)
+        regroup.relay()
+        runs[0].slot(1)
+        job.begin_near()
+        runs[1].slot(1)
+        every[0].relay()
         job.relay()
-        run.slot(1)
+        runs[0].slot(2)
+        every[1].relay()
+        runs[1].slot(2)
         job.own()
-        every[1].relay()
-        run.slot(2)
         job.end()
         values, change = inputs_ref[...].astype(jnp.float32), summed[...]
         scale = norm_rows(values, gain_ref[...])[0]
-        grad_gain[...] = jnp.sum(change * values * scale, axis=0, keepdims=True)
+        small_own[...] = small_ref[...]
+        small_own[:, :depth] = jnp.sum(change * values * scale, axis=0, keepdims=True)
+        total.start()
         change = change * gain_ref[...]
         mean = jnp.mean(change * values, axis=-1, keepdims=True)
         grad_input[...] = middle_ref[...] + scale * change - values * (scale * scale * scale * mean)
+        for run in runs:
+            run.end()
+        every.append(SquareGather(share, every_refs[2], send.at[2], recv.at[2]))
+        every[2].start()
+        size = share.shape[0]
+        kept.append(
+            pltpu.make_async_copy(
+                share, every_refs[2].at[pl.ds(pl.multiple_of(me * size, size), size)], keep.at[2]
+            )
+        )
+        kept[2].start()
+        total.relay()
+        every[2].relay()
+        regroup.end()
+        total.end()
         for gathering, copy in zip(every, kept):
             gathering.near()
             gathering.far()
             gathering.finish()
             copy.wait()
-        regroup.end()
-        run.end()
 
     vmem = pl.BlockSpec(memory_space=pltpu.VMEM)
     anywhere = pl.BlockSpec(memory_space=pl.ANY)
@@ -1713,32 +1692,36 @@
     dma = pltpu.SemaphoreType.DMA
     return pl.pallas_call(
         body,
-        in_specs=[anywhere] * 7 + [vmem] * 4,
-        out_specs=[vmem] * 4 + [anywhere] * 2,
+        in_specs=[anywhere] * 7 + [vmem] * 5,
+        out_specs=[vmem] * 3 + [anywhere] * 3,
         out_shape=[
             jax.ShapeDtypeStruct((tokens, depth), jnp.float32),
-            jax.ShapeDtypeStruct((1, depth), jnp.float32),
-            jax.ShapeDtypeStruct((rows, front), low),
+            jax.ShapeDtypeStruct(small.shape, jnp.float32),
             jax.ShapeDtypeStruct((4,) + collected.shape, low),
             *(jax.ShapeDtypeStruct((4 * v.shape[0], v.shape[1]), low) for v in shares),
+            jax.ShapeDtypeStruct((4 * rows, front), low),
         ],
         scratch_shapes=[
             *(pltpu.VMEM(value.shape, value.dtype) for value in fetched),
             pltpu.VMEM((depth, front), low),
             pltpu.VMEM((tokens, depth), jnp.float32),
-            dma((2, 6)),
-            dma((2, 6)),
-            dma((2,)),
+            pltpu.VMEM((rows, front), low),
+            pltpu.VMEM(small.shape, jnp.float32),
+            dma((3, 6)),
+            dma((3, 6)),
+            dma((3,)),
             dma((7,)),
         ]
         + SquareScatter.scratch(tokens, depth)
-        + LineScatter.scratch(shards // 2, rows, front)
-        + Regroup.scratch(*collected.shape),
+        + LineScatter.scratch(shards // 2, rows, front // 2)
+        + Regroup.scratch(*collected.shape)
+        + LineScatter.scratch(shards // 2, rows, front // 2)
+        + Everywhere.scratch(small.shape),
         compiler_params=pltpu.CompilerParams(
             collective_id=collective_id, has_side_effects=True, vmem_limit_bytes=VMEM_LIMIT
         ),
         name="last_backward",
-    )(*fetched, collected, gain, *shares)
+    )(*fetched, collected, gain, small, *shares)
 
 
 def gather(value, axis_name):
@@ -1801,6 +1784,11 @@
         mine = lax.dynamic_index_in_dim(split, seq_rank, 2, keepdims=False)
         return mine.reshape(weight.shape[0], units)
 
+    def own_bias_grad(bias_rows):
+        return lax.dynamic_update_slice_in_dim(
+            jnp.zeros((heads,), jnp.float32), bias_rows[:local_heads, 0], seq_rank * local_heads, 0
+        )
+
     own_forget = lax.dynamic_slice_in_dim(w_forget, seq_rank * local_heads, local_heads, 1)
     own_forget = jnp.pad(own_forget, ((0, 0), (0, PAIR - local_heads)))
     own_bias = lax.dynamic_slice_in_dim(forget_bias, seq_rank * local_heads, local_heads)
@@ -1830,11 +1818,13 @@
             joined, grad_attended, offset, col, logit, hidden, full_down, gated, grad_branch, terms_up,
             (share_down, share_gate), normed_attn, grad_gate_pre, middle, head_size, scale, 3,
         )
-        grad_input, grad_norm_attn, share_attn, grad_out, every_ogate, every_up = last_backward(
+        vector = jnp.concatenate([jnp.zeros((width,), jnp.float32), grad_norm_ffn, own_bias_grad(bias_rows)])
+        vector = jnp.pad(vector, (0, -vector.shape[0] % PAIR))[None]
+        grad_input, vector, grad_out, every_ogate, every_up, every_attn = last_backward(
             grads, grad_gate_pre, normed_attn, full_front, full_ogate, collected, (share_ogate, share_up),
-            layer_input[0], norm_attn[None], grad_middle, 4,
+            layer_input[0], norm_attn[None], grad_middle, vector, 4,
         )
-        grad_norm_attn = grad_norm_attn[0]
+        small = vector[0, :width], vector[0, width : 2 * width], vector[0, 2 * width : 2 * width + heads]
         grad_out = grad_out.reshape(columns // per_block, width)
     else:
         mine_front = jnp.concatenate(
@@ -1896,21 +1886,11 @@
         unused_normed, pull_attn_norm = jax.vjp(rms_norm, inputs, norm_attn)
         grad_input_part, grad_norm_attn = pull_attn_norm(grad_normed_attn)
         grad_input = grad_middle + grad_input_part
-    grad_bias = lax.dynamic_update_slice_in_dim(
-        jnp.zeros((heads,), jnp.float32), bias_rows[:local_heads, 0], seq_rank * local_heads, 0
-    )
-
-    rows = share_attn.shape[0]
-    if fast:
-        vector = jnp.concatenate([grad_norm_attn, grad_norm_ffn, grad_bias])
-        vector = jnp.pad(vector, (0, -vector.shape[0] % 1024)).reshape(-1, 128)
-        every_attn, vector = last_gather([share_attn], vector, 5)
-        vector = vector.reshape(-1)
-        small = vector[:width], vector[width : 2 * width], vector[2 * width : 2 * width + heads]
-    else:
+    if not fast:
         every_attn, every_ffn, grad_down = [gather(v, "seq") for v in (share_attn, share_ffn, share_down)]
-        small = lax.psum((grad_norm_attn, grad_norm_ffn, grad_bias), ("seq", "wshard"))
-    every_attn = every_attn.reshape((groups,) + share_attn.shape)
+        small = lax.psum((grad_norm_attn, grad_norm_ffn, own_bias_grad(bias_rows)), ("seq", "wshard"))
+    rows = width // shards
+    every_attn = every_attn.reshape(groups, rows, every_attn.shape[1])
     if fast:
         *weight_grads, grad_forget_w, grad_w_gate, grad_w_up, grad_down, grad_out = join_shares(
             every_attn,

time: 392 us -> 383 us (0.977)
  Pallas kernels: 377 us -> 368 us
    pallas_call x2 -> x1, Pallas kernels: 82.4 us -> 73.5 us  [last_backward(): pl.pallas_call(body, in_specs=[anywhere] * 7 + [vmem] * 5, out_specs=[vme...]
where the time goes in v4:
time: 383 us
  Pallas kernels  368 us (96%)
  local copies, waits for them, and re-layouts  13.9 us (4%)
    pallas_call x1, Pallas kernels, whole_forward(): pl.pallas_call(body, in_specs=[vmem] * 3 + [anywhere] * 4 + [vmem] * 3 +...  107 us
    pallas_call x1, Pallas kernels, last_backward(): pl.pallas_call(body, in_specs=[anywhere] * 7 + [vmem] * 5, out_specs=[vme...  73.5 us
    pallas_call x1, Pallas kernels, feed_backward(): pl.pallas_call(body, in_specs=[anywhere] * 7 + [vmem] + [anywhere] * 3, o...  65.5 us
    pallas_call x1, Pallas kernels, middle_backward(): pl.pallas_call(body, in_specs=[anywhere] * 10 + [vmem] * 5, out_specs=[vm...  59.5 us
    pallas_call x1, Pallas kernels, feed_forward(): pl.pallas_call(body, in_specs=[vmem, vmem, anywhere, vmem, vmem, anywhere...  53.6 us
    pallas_call x1, Pallas kernels, join_shares(): pl.pallas_call(body, grid=(steps,), in_specs=[ranks(v) for v in (every, g...  8.78 us

profile of v4, /device:TPU:0, one launch (start us, length us, event | category | flops | bytes accessed | tf_op | source)
XLA Modules:
  0.0 383.0 jit_solution(15354957546075631538)
XLA Ops:
  0.6 0.0 copy-start
  0.7 0.8 constant_dynamic-slice_fusion.1
  1.5 0.1 copy.33
  1.6 0.6 pad.12.forget_ref
  2.3 0.7 dynamic_slice.10
  3.0 0.5 pad_bitcast_fusion.bias_ref
  3.5 1.3 broadcast_in_dim.31.gain_ref.refs_8_
  5.5 0.5 broadcast_in_dim.34.length_ref
  6.0 0.0 copy-start.4
  6.0 106.7 %whole_forward.1 = (bf16[1024,1536]{1,0:T(8,128)(2,1)}, bf16[1024,1536]{1,0:T(8,128)(2,1)}, bf16[1536,1280]{1,0:T(8,128)(2,1)}, bf16[1536,384]{1,0:T(8,128)(2,1)...) custom-call(bf16[256,1536]{1,0:T(8,128)(2,1)} %bitcast.16, ...), custom_call_target="tpu_custom_call" | custom-call | tf_op jit(solution)/shard_map/whole_forward/pallas_call | solution.py:910
  112.7 0.0 copy-done
  112.7 0.8 constant_dynamic-slice_fusion.down_ref
  113.5 0.0 copy-done.4
  113.5 0.6 broadcast_in_dim.35.gain_ref
  114.1 53.6 %feed_forward.1 = (bf16[1024,1536]{1,0:T(8,128)(2,1)}, bf16[1024,1024]{1,0:T(8,128)(2,1)}, bf16[1536,512]{1,0:T(8,128)(2,1)}, bf16[1024,1536]{1,0:T(8,128)(2,1)}...) custom-call(f32[256,1536]{1,0:T(8,128)} %get-tuple-element.66.middle_ref.middle_hbm.refs_9_, ...), custom_call_target="tpu_custom_call" | custom-call | tf_op jit(solution)/shard_map/feed_forward/pallas_call | solution.py:1059
  167.8 65.5 %feed_backward.1 = (f32[256,1536]{1,0:T(8,128)}, f32[1,1536]{1,0:T(1,128)}, bf16[1024,1536]{1,0:T(8,128)(2,1)}, bf16[1024,384]{1,0:T(8,128)(2,1)}, bf16[1024,384...) custom-call(bf16[1024,2048]{1,0:T(8,128)(2,1)} %get-tuple-element.70.grads_hbm, ...), custom_call_target="tpu_custom_call" | custom-call | tf_op jit(solution)/shard_map/feed_backward/pallas_call | solution.py:1201
  233.3 0.0 copy-start.5
  233.3 59.5 %middle_backward.1 = (bf16[1024,1280]{1,0:T(8,128)(2,1)}, f32[8,128]{1,0:T(8,128)}, bf16[256,1536]{1,0:T(8,128)(2,1)}, bf16[48,1536]{1,0:T(8,128)(2,1)}, bf16[19...) custom-call(bf16[1536,1024]{1,0:T(8,128)(2,1)} %get-tuple-element.77.refs_, ...), custom_call_target="tpu_custom_call" | custom-call | tf_op jit(solution)/shard_map/middle_backward/pallas_call | solution.py:1561
  292.8 0.8 slice_reduce_fusion.2
  293.6 0.2 dynamic_update_slice.3
  293.8 0.0 copy-done.5
  293.9 0.6 broadcast_in_dim.38.refs_9_
  294.5 73.5 %last_backward.1 = (f32[256,1536]{1,0:T(8,128)}, f32[1,3200]{1,0:T(1,128)}, bf16[4,48,1536]{2,1,0:T(8,128)(2,1)}, bf16[768,384]{1,0:T(8,128)(2,1)}, bf16[768,102...) custom-call(bf16[1024,1536]{1,0:T(8,128)(2,1)} %get-tuple-element.82.refs_5_.refs_0_, ...), custom_call_target="tpu_custom_call" | custom-call | tf_op jit(solution)/shard_map/last_backward/pallas_call | solution.py:1693
  368.0 0.0 copy-start.3
  368.0 8.8 %join_shares.1 = (f32[192,1536]{1,0:T(8,128)}, f32[192,1536]{1,0:T(8,128)}, f32[192,1536]{1,0:T(8,128)}, f32[192,1536]{1,0:T(8,128)}, f32[192,24]{1,0:T(8,128)},...) custom-call(bf16[4,192,1280]{2,1,0:T(8,128)(2,1)} %bitcast.18, ...), custom_call_target="tpu_custom_call" | custom-call | tf_op jit(solution)/shard_map/join_shares/pallas_call | solution.py:722
  376.8 0.0 copy-start.2
  376.8 1.7 copy.32
  378.5 0.0 copy-done.3
  378.5 0.6 slice_reduce_fusion
  379.1 0.5 slice_bitcast_fusion
  379.6 0.0 copy-start.1
  379.6 2.2 copy.38
  381.8 0.0 copy-done.2
  381.8 1.1 copy.39
  383.0 0.0 copy-done.1
  (4 shorter events, 0.0 us)
Async XLA Ops:
  0.6 112.1 %copy-start = (bf16[512,1536]{1,0:T(8,128)(2,1)S(1)}, bf16[512,1536]{1,0:T(8,128)(2,1)}, u32[]{:S(2)}) copy-start(bf16[512,1536]{1,0:T(8,128)(2,1)} %param.28) | copy-start | bytes 4718596
  6.0 107.5 %copy-start.4 = (f32[1536]{0:T(1024)S(1)}, f32[1536]{0:T(1024)}, u32[]{:S(2)}) copy-start(f32[1536]{0:T(1024)} %param.25) | copy-start | bytes 18436
  233.3 60.6 %copy-start.5 = (f32[1,1536]{1,0:T(1,128)S(1)}, f32[1,1536]{1,0:T(1,128)}, u32[]{:S(2)}) copy-start(f32[1,1536]{1,0:T(1,128)} %get-tuple-element.97) | copy-start | bytes 18436
  368.0 10.5 %copy-start.3 = (f32[1,3200]{1,0:T(1,128)S(1)}, f32[1,3200]{1,0:T(1,128)}, u32[]{:S(2)}) copy-start(f32[1,3200]{1,0:T(1,128)} %get-tuple-element.102) | copy-start | bytes 38404
  376.8 5.0 %copy-start.2 = (f32[256,1536]{1,0:T(8,128)S(1)}, f32[256,1536]{1,0:T(8,128)}, u32[]{:S(2)}) copy-start(f32[256,1536]{1,0:T(8,128)} %get-tuple-element.101) | copy-start | bytes 4718596
  379.6 3.3 copy-start.1

commit v5 on v4

--- a/solution.py
+++ b/solution.py
@@ -1517,6 +1517,7 @@
         for copy in comes[7:]:
             copy.wait()
         run_pre.slot(0)
+        run.slot(1)
         work.start()
 
         def step(pair, carry):
@@ -1524,16 +1525,15 @@
 
             @pl.when(pair == 0)
             def _():
-                run.slot(1)
                 job.relay()
                 every[0].relay()
                 every[1].start()
                 collect.slot(1)
                 run_pre.slot(1)
+                run.slot(2)
 
             @pl.when(pair == 1)
             def _():
-                run.slot(2)
                 collect.slot(2)
                 run_pre.slot(2)
                 every[1].relay()

time: 383 us -> 383 us (level)
  no operation moved by 1% of the time
where the time goes in v5:
time: 383 us
  Pallas kernels  368 us (96%)
  local copies, waits for them, and re-layouts  13.9 us (4%)
    pallas_call x1, Pallas kernels, whole_forward(): pl.pallas_call(body, in_specs=[vmem] * 3 + [anywhere] * 4 + [vmem] * 3 +...  107 us
    pallas_call x1, Pallas kernels, last_backward(): pl.pallas_call(body, in_specs=[anywhere] * 7 + [vmem] * 5, out_specs=[vme...  73.5 us
    pallas_call x1, Pallas kernels, feed_backward(): pl.pallas_call(body, in_specs=[anywhere] * 7 + [vmem] + [anywhere] * 3, o...  65.5 us
    pallas_call x1, Pallas kernels, middle_backward(): pl.pallas_call(body, in_specs=[anywhere] * 10 + [vmem] * 5, out_specs=[vm...  59.5 us
    pallas_call x1, Pallas kernels, feed_forward(): pl.pallas_call(body, in_specs=[vmem, vmem, anywhere, vmem, vmem, anywhere...  53.6 us
    pallas_call x1, Pallas kernels, join_shares(): pl.pallas_call(body, grid=(steps,), in_specs=[ranks(v) for v in (every, g...  8.78 us

profile of v5, /device:TPU:0, one launch (start us, length us, event | category | flops | bytes accessed | tf_op | source)
XLA Modules:
  0.0 383.0 jit_solution(15615235604752649884)
XLA Ops:
  0.6 0.0 copy-start
  0.7 0.8 constant_dynamic-slice_fusion.1
  1.5 0.1 copy.33
  1.6 0.6 pad.12.forget_ref
  2.3 0.7 dynamic_slice.10
  3.0 0.5 pad_bitcast_fusion.bias_ref
  3.5 1.3 broadcast_in_dim.31.gain_ref.refs_8_
  5.5 0.5 broadcast_in_dim.34.length_ref
  6.0 0.0 copy-start.4
  6.0 106.7 %whole_forward.1 = (bf16[1024,1536]{1,0:T(8,128)(2,1)}, bf16[1024,1536]{1,0:T(8,128)(2,1)}, bf16[1536,1280]{1,0:T(8,128)(2,1)}, bf16[1536,384]{1,0:T(8,128)(2,1)...) custom-call(bf16[256,1536]{1,0:T(8,128)(2,1)} %bitcast.16, ...), custom_call_target="tpu_custom_call" | custom-call | tf_op jit(solution)/shard_map/whole_forward/pallas_call | solution.py:910
  112.7 0.0 copy-done
  112.7 0.8 constant_dynamic-slice_fusion.down_ref
  113.5 0.0 copy-done.4
  113.5 0.6 broadcast_in_dim.35.gain_ref
  114.1 53.6 %feed_forward.1 = (bf16[1024,1536]{1,0:T(8,128)(2,1)}, bf16[1024,1024]{1,0:T(8,128)(2,1)}, bf16[1536,512]{1,0:T(8,128)(2,1)}, bf16[1024,1536]{1,0:T(8,128)(2,1)}...) custom-call(f32[256,1536]{1,0:T(8,128)} %get-tuple-element.66.middle_ref.middle_hbm.refs_9_, ...), custom_call_target="tpu_custom_call" | custom-call | tf_op jit(solution)/shard_map/feed_forward/pallas_call | solution.py:1059
  167.8 65.5 %feed_backward.1 = (f32[256,1536]{1,0:T(8,128)}, f32[1,1536]{1,0:T(1,128)}, bf16[1024,1536]{1,0:T(8,128)(2,1)}, bf16[1024,384]{1,0:T(8,128)(2,1)}, bf16[1024,384...) custom-call(bf16[1024,2048]{1,0:T(8,128)(2,1)} %get-tuple-element.70.grads_hbm, ...), custom_call_target="tpu_custom_call" | custom-call | tf_op jit(solution)/shard_map/feed_backward/pallas_call | solution.py:1201
  233.3 0.0 copy-start.5
  233.3 59.5 %middle_backward.1 = (bf16[1024,1280]{1,0:T(8,128)(2,1)}, f32[8,128]{1,0:T(8,128)}, bf16[256,1536]{1,0:T(8,128)(2,1)}, bf16[48,1536]{1,0:T(8,128)(2,1)}, bf16[19...) custom-call(bf16[1536,1024]{1,0:T(8,128)(2,1)} %get-tuple-element.77.refs_, ...), custom_call_target="tpu_custom_call" | custom-call | tf_op jit(solution)/shard_map/middle_backward/pallas_call | solution.py:1561
  292.8 0.8 slice_reduce_fusion.2
  293.6 0.2 dynamic_update_slice.3
  293.8 0.0 copy-done.5
  293.9 0.6 broadcast_in_dim.38.refs_9_
  294.5 73.5 %last_backward.1 = (f32[256,1536]{1,0:T(8,128)}, f32[1,3200]{1,0:T(1,128)}, bf16[4,48,1536]{2,1,0:T(8,128)(2,1)}, bf16[768,384]{1,0:T(8,128)(2,1)}, bf16[768,102...) custom-call(bf16[1024,1536]{1,0:T(8,128)(2,1)} %get-tuple-element.82.refs_5_.refs_0_, ...), custom_call_target="tpu_custom_call" | custom-call | tf_op jit(solution)/shard_map/last_backward/pallas_call | solution.py:1693
  368.0 0.0 copy-start.3
  368.0 8.8 %join_shares.1 = (f32[192,1536]{1,0:T(8,128)}, f32[192,1536]{1,0:T(8,128)}, f32[192,1536]{1,0:T(8,128)}, f32[192,1536]{1,0:T(8,128)}, f32[192,24]{1,0:T(8,128)},...) custom-call(bf16[4,192,1280]{2,1,0:T(8,128)(2,1)} %bitcast.18, ...), custom_call_target="tpu_custom_call" | custom-call | tf_op jit(solution)/shard_map/join_shares/pallas_call | solution.py:722
  376.8 0.0 copy-start.2
  376.8 1.7 copy.32
  378.5 0.0 copy-done.3
  378.5 0.6 slice_reduce_fusion
  379.1 0.5 slice_bitcast_fusion
  379.6 0.0 copy-start.1
  379.6 2.2 copy.38
  381.8 0.0 copy-done.2
  381.8 1.1 copy.39
  383.0 0.0 copy-done.1
  (4 shorter events, 0.0 us)
Async XLA Ops:
  0.6 112.1 %copy-start = (bf16[512,1536]{1,0:T(8,128)(2,1)S(1)}, bf16[512,1536]{1,0:T(8,128)(2,1)}, u32[]{:S(2)}) copy-start(bf16[512,1536]{1,0:T(8,128)(2,1)} %param.28) | copy-start | bytes 4718596
  6.0 107.5 %copy-start.4 = (f32[1536]{0:T(1024)S(1)}, f32[1536]{0:T(1024)}, u32[]{:S(2)}) copy-start(f32[1536]{0:T(1024)} %param.25) | copy-start | bytes 18436
  233.3 60.6 %copy-start.5 = (f32[1,1536]{1,0:T(1,128)S(1)}, f32[1,1536]{1,0:T(1,128)}, u32[]{:S(2)}) copy-start(f32[1,1536]{1,0:T(1,128)} %get-tuple-element.97) | copy-start | bytes 18436
  368.0 10.5 %copy-start.3 = (f32[1,3200]{1,0:T(1,128)S(1)}, f32[1,3200]{1,0:T(1,128)}, u32[]{:S(2)}) copy-start(f32[1,3200]{1,0:T(1,128)} %get-tuple-element.102) | copy-start | bytes 38404
  376.8 5.0 %copy-start.2 = (f32[256,1536]{1,0:T(8,128)S(1)}, f32[256,1536]{1,0:T(8,128)}, u32[]{:S(2)}) copy-start(f32[256,1536]{1,0:T(8,128)} %get-tuple-element.101) | copy-start | bytes 4718596
  379.6 3.3 copy-start.1
